TPU v7x, 256 devices: a whole 4x4x8 slice. The times are simulated.
256 devices in a mesh: section: 2 (over y_hi), pen: 64 (over y_lo, z, x), slab: 2 (over core).
Axes of the slice: x: 4, y: 4 (y_hi: 2, y_lo: 2; y = y_hi * 2 + y_lo), z: 8, core: 2. Of those that a mesh axis runs over, the one named last changes fastest.
Arguments:
- velocity: float32 [3, 384, 384, 384], P(None, ('section', 'pen'), 'slab'), may hold values from -6 to 6
- vorticity: float32 [3, 384, 384, 384], P(None, ('section', 'pen'), 'slab'), may hold values from -6 to 6
- velocity_modes: float32 [3, 256, 256, 2, 256], P(None, None, ('section', 'pen'), None, 'slab'), may hold values from -6 to 6
Outputs:
- rhs_modes: float32 [3, 256, 256, 2, 256], P(None, None, ('section', 'pen'), None, 'slab')
All inputs are finite; a program needn't handle non-finite values.
Results may differ from a plain program's by a relative error of at most 0.000057.
Values sent between devices are 32-bit elements; how exact they have to be, the bound alone decides.
No kernel may reach another device: no remote copies, remote signals or barrier semaphores. Data moves between devices by JAX's collectives and lax.ppermute only.
A program may use at most 64 MiB of HBM per device.

v0:
```python
import functools
import math

import jax
import jax.numpy as jnp
import ml_dtypes
import numpy as np
from jax import lax
from jax.experimental import pallas as pl
from jax.experimental.pallas import tpu as pltpu
from jax.sharding import PartitionSpec as P

VMEM = pltpu.VMEM
GROUP = ("section", "pen")
NY, NZ, NX = 4, 8, 4
NXY = NX * NY


def signed(index, count):
    return np.where(index < count // 2, index, index - count)


def halves(table):
    high = table.astype(np.float32).astype(ml_dtypes.bfloat16)
    low = (table - high.astype(np.float64)).astype(np.float32).astype(ml_dtypes.bfloat16)
    return high, low


def angles(modes, positions, length):
    return 2.0 * math.pi / length * ((modes[:, None] * positions[None, :]) % length)


def rows_of(theta, cells):
    return np.stack(halves(np.concatenate([np.cos(theta), np.sin(theta)], axis=0) / math.sqrt(cells)))


def z_major_groups():
    return np.array([(y * NZ + z) * NX + x for z in range(NZ) for y in range(NY) for x in range(NX)])


def xy_major_groups():
    return np.array([(y * NZ + z) * NX + x for y in range(NY) for x in range(NX) for z in range(NZ)])


def x_table(cells, keep):
    theta = angles(signed(np.arange(keep), keep), np.arange(cells), cells).T
    block = keep // 2
    parts = []
    for h in range(2):
        cut = theta[:, h * block : (h + 1) * block]
        parts += [np.cos(cut), -np.sin(cut)]
    return np.concatenate(halves(np.concatenate(parts, axis=1) / math.sqrt(cells)), axis=0)


def y_table(cells, keep, order):
    modes = signed(np.arange(keep), keep)
    return np.stack(
        [rows_of(angles(modes[parity::2][order], np.arange(cells // 2), cells), cells) for parity in range(2)]
    )


def z_table(cells, keep, positions):
    return rows_of(angles(signed(np.arange(keep), keep), positions, cells), cells)


def split(x):
    high = x.astype(jnp.bfloat16)
    low = (x - high.astype(jnp.float32)).astype(jnp.bfloat16)
    return high, low


def product(a, b):
    return jnp.dot(a, b, preferred_element_type=jnp.float32)


def transformed(high_table, low_table, x):
    high, low = split(x)
    return product(
        jnp.concatenate([high_table, high_table, low_table], axis=1), jnp.concatenate([high, low, high], axis=0)
    )


def place():
    pen = lax.axis_index("pen")
    x = lax.rem(pen, NX)
    z = lax.rem(lax.div(pen, NX), NZ)
    y = lax.axis_index("section") * 2 + lax.div(pen, NX * NZ)
    return y, z, x


def x_kernel(planes, v_hbm, w_hbm, table_hbm, _, keep_ref, send_ref, v_ref, w_ref, table_ref, sems):
    rows = v_ref.shape[2]
    half = keep_ref.shape[-1]
    copies = []
    for i, plane in enumerate(planes):
        for c in range(3):
            copies.append(pltpu.make_async_copy(v_hbm.at[c, plane], v_ref.at[i, c], sems.at[i * 6 + c]))
            copies.append(pltpu.make_async_copy(w_hbm.at[c, plane], w_ref.at[i, c], sems.at[i * 6 + 3 + c]))
        if i == 0:
            copies.append(pltpu.make_async_copy(table_hbm, table_ref, sems.at[len(planes) * 6]))
    for copy in copies:
        copy.start()
    mine = lax.axis_index("slab") == 0
    deep = table_ref.shape[0] // 2
    for i in range(len(planes)):
        for copy in copies[:7] if i == 0 else copies[7 + (i - 1) * 6 : 7 + i * 6]:
            copy.wait()
        table = jnp.concatenate([table_ref[:deep], table_ref[:deep], table_ref[deep:]], axis=0)
        for c in range(3):
            a, b = (c + 1) % 3, (c + 2) % 3
            high, low = split(v_ref[i, a] * w_ref[i, b] - v_ref[i, b] * w_ref[i, a])
            out = product(jnp.concatenate([high, low, high], axis=1), table)
            first, second = out[:, :half], out[:, half:]
            here = slice((i * 3 + c) * rows, (i * 3 + c + 1) * rows)
            keep_ref[here] = jnp.where(mine, first, second)
            send_ref[here] = jnp.where(mine, second, first)


def y_blocks(keep_ref, got_ref, table_ref, rows):
    sign = jnp.where(lax.axis_index("slab") == 0, 1.0, -1.0).astype(jnp.float32)
    dests = table_ref.shape[2] // 2
    lanes = keep_ref.shape[1] // 2
    for block in range(keep_ref.shape[0] // rows):
        here = slice(block * rows, (block + 1) * rows)
        own, got = keep_ref[here], got_ref[here]
        for parity in range(2):
            folded = own + got if parity == 0 else (own - got) * sign
            out = transformed(table_ref[parity, 0], table_ref[parity, 1], folded)
            yield block, parity * 2, out[:dests, :lanes] + out[dests:, lanes:]
            yield block, parity * 2 + 1, out[:dests, lanes:] - out[dests:, :lanes]


def y_pack_kernel(rows, keep_ref, got_ref, table_ref, _, out_ref):
    dests = table_ref.shape[2] // 2
    per = out_ref.shape[0] // dests
    for block, q, value in y_blocks(keep_ref, got_ref, table_ref, rows):
        out_ref[pl.ds(block * 4 + q, dests, per), :] = value


def y_send_kernel(rows, keep_ref, got_ref, table_ref, *refs):
    outs, all_ref = refs[:-1], refs[-1]
    dests = table_ref.shape[2] // 2
    for block, q, value in y_blocks(keep_ref, got_ref, table_ref, rows):
        at = (block * 4 + q) * dests
        all_ref[at : at + dests] = value
    _, z, _ = place()
    for shift in range(NZ):
        to = lax.rem(z - shift + NZ, NZ)
        for k in range(all_ref.shape[0] // dests):
            outs[shift][k * NXY : (k + 1) * NXY] = all_ref[pl.ds(pl.multiple_of(k * dests + to * NXY, NXY), NXY), :]


def turn_kernel(*refs):
    gots, outs, all_ref = refs[:NZ], refs[NZ:-1], refs[-1]
    y, z, x = place()
    size = gots[0].shape[0]
    for shift in range(NZ):
        source = lax.rem(z + shift, NZ)
        all_ref[pl.ds(pl.multiple_of(source * size, size), size), :] = gots[shift][...]
    count = all_ref.shape[0] // NXY
    for dy in range(NY):
        for dx in range(NX):
            to = lax.rem(y - dy + NY, NY) * NX + lax.rem(x - dx + NX, NX)
            outs[dy * NX + dx][...] = all_ref[pl.ds(to, count, NXY), :]


def early_kernel(keep, *refs):
    gots, table_ref, out_ref, all_ref = refs[:NXY], refs[NXY], refs[NXY + 1], refs[NXY + 2]
    y, _, x = place()
    lanes = out_ref.shape[1]
    kinds = gots[0].shape[0] // NZ
    sources = NXY * NZ
    for dy in range(NY):
        for dx in range(NX):
            source = lax.rem(y + dy, NY) * NX + lax.rem(x + dx, NX)
            for k in range(kinds):
                at = pl.multiple_of(k * sources + source * NZ, NZ)
                all_ref[pl.ds(at, NZ), :] = gots[dy * NX + dx][pl.ds(k, NZ, kinds), :]
    for pair in range(kinds // 2):
        both = [all_ref[(pair * 2 + q) * sources : (pair * 2 + q + 1) * sources] for q in range(2)]
        out = transformed(table_ref[0], table_ref[1], jnp.concatenate(both, axis=1))
        out_ref[pair * 2 * keep : (pair * 2 + 1) * keep] = out[:keep, :lanes] + out[keep:, lanes:]
        out_ref[(pair * 2 + 1) * keep : (pair * 2 + 2) * keep] = out[:keep, lanes:] - out[keep:, :lanes]


def z_kernel(planes, keep, x_ref, early_ref, modes_ref, table_ref, out_ref):
    group = lax.axis_index("section") * lax.axis_size("pen") + lax.axis_index("pen")
    slab = lax.axis_index("slab")
    lanes = x_ref.shape[1]
    per = 3 * planes * 4
    sources = x_ref.shape[0] // per
    limit = -(keep // 2)
    visc = 0.5 / (keep // 2) ** 2
    row = lax.broadcasted_iota(jnp.int32, (keep, lanes), 0)
    col = lax.broadcasted_iota(jnp.int32, (keep, lanes), 1) + slab * lanes
    kz = jnp.where(row < keep // 2, row, row - keep)
    kx = jnp.where(col < keep // 2, col, col - keep)
    for parity in range(2):
        index = group * 2 + parity
        ky = jnp.where(index < keep // 2, index, index - keep)
        mask = ((kx != limit) & (kz != limit) & (ky != limit)).astype(jnp.float32)
        fx, fz = kx.astype(jnp.float32), kz.astype(jnp.float32)
        fy = ky.astype(jnp.float32)
        ksq = fx * fx + fy * fy + fz * fz
        inverse = 1.0 / jnp.maximum(ksq, 1.0)
        damp = visc * ksq
        real, imag = [], []
        for c in range(3):
            columns = []
            for q in range(2):
                base = parity * 2 + q
                columns.append(
                    jnp.concatenate(
                        [x_ref[pl.ds(base + (p * 3 + c) * 4, sources, per), :] for p in range(planes)], axis=0
                    )
                )
            out = transformed(table_ref[0], table_ref[1], jnp.concatenate(columns, axis=1))
            at = (c * 2 + parity) * 2 * keep
            real.append(early_ref[at : at + keep] + (out[:keep, :lanes] + out[keep:, lanes:]))
            imag.append(early_ref[at + keep : at + 2 * keep] + (out[:keep, lanes:] - out[keep:, :lanes]))
        for q, s in enumerate((real, imag)):
            inner = (fx * s[0] + fy * s[1] + fz * s[2]) * inverse
            for c, k in enumerate((fx, fy, fz)):
                where = pl.ds(c * keep * 4 + parity * 2 + q, keep, 4)
                out_ref[where, :] = mask * (s[c] - k * inner) - damp * modes_ref[where, :]


def call(kernel, outs, flops=0, scratch=(), spaces=None, limit=40 << 20):
    def run(*args):
        size = sum(a.size * a.dtype.itemsize for a in args) + sum(4 * math.prod(o) for o in outs)
        shapes = [jax.ShapeDtypeStruct(o, jnp.float32) for o in outs]
        specs = [pl.BlockSpec(memory_space=VMEM)] * len(outs)
        single = len(outs) == 1
        return pl.pallas_call(
            kernel,
            out_shape=shapes[0] if single else shapes,
            in_specs=[pl.BlockSpec(memory_space=s) for s in spaces or [VMEM] * len(args)],
            out_specs=specs[0] if single else specs,
            scratch_shapes=list(scratch),
            cost_estimate=pl.CostEstimate(flops=flops, bytes_accessed=size, transcendentals=0),
            compiler_params=pltpu.CompilerParams(vmem_limit_bytes=limit),
        )(*args)

    return run


def group_of(y, z, x):
    return ((y % NY) * NZ + z % NZ) * NX + x % NX


def from_shift(value, dy, dz, dx):
    pairs = [
        (group_of(y + dy, z + dz, x + dx), group_of(y, z, x))
        for y in range(NY)
        for z in range(NZ)
        for x in range(NX)
    ]
    return lax.ppermute(value, GROUP, pairs)


def per_device(velocity, vorticity, velocity_modes):
    _, planes, rows_y, cells = velocity.shape
    _, keep, rows_ky, _, lanes = velocity_modes.shape
    dests = lax.axis_size(GROUP)
    order = z_major_groups()
    table_y = jnp.asarray(y_table(cells, keep, order))
    table_x = jnp.asarray(x_table(cells, keep))
    keeps, gots = [], []
    for held in ([0], list(range(1, planes))):
        n = len(held)
        run = call(
            functools.partial(x_kernel, held),
            [(3 * n * rows_y, keep)] * 2,
            2 * 9 * n * rows_y * cells * 2 * keep,
            [
                VMEM((n, 3, rows_y, cells), jnp.float32),
                VMEM((n, 3, rows_y, cells), jnp.float32),
                VMEM(table_x.shape, jnp.bfloat16),
                pltpu.SemaphoreType.DMA((6 * n + 1,)),
            ],
            [pltpu.HBM] * 4,
            50 << 20,
        )
        mine, other = run(velocity, vorticity, table_x, keeps[0] if keeps else vorticity)
        keeps.append(mine)
        gots.append(lax.ppermute(other, "slab", [(0, 1), (1, 0)]))
    flops = 2 * 3 * 2 * keep * 3 * rows_y * keep
    kinds = 3 * 4
    sent = call(
        functools.partial(y_send_kernel, rows_y),
        [(kinds * NXY, lanes)] * NZ,
        flops,
        [VMEM((kinds * dests, lanes), jnp.float32)],
    )(keeps[0], gots[0], table_y)
    arrived = [sent[0]]
    for s in range(1, NZ):
        arrived.append(from_shift(sent[s], 0, s, 0))
    per = (planes - 1) * kinds
    packed = call(
        functools.partial(y_pack_kernel, rows_y),
        [(dests * per, lanes)],
        flops * (planes - 1),
        spaces=[VMEM] * 3 + [pl.ANY],
    )(keeps[1], gots[1], table_y, sent[0])
    late = lax.all_to_all(
        packed.reshape(dests, per, lanes), GROUP, 0, 0, axis_index_groups=[order.tolist()], tiled=True
    )
    turned = call(turn_kernel, [(NZ * kinds, lanes)] * NXY, 0, [VMEM((NZ * kinds * NXY, lanes), jnp.float32)])(*arrived)
    spread = [turned[0]] + [from_shift(turned[d], d // NX, 0, d % NX) for d in range(1, NXY)]
    early = call(
        functools.partial(early_kernel, keep),
        [(kinds * keep, lanes)],
        2 * 6 * 2 * keep * 3 * dests * keep,
        [VMEM((kinds * dests, lanes), jnp.float32)],
    )(*spread, jnp.asarray(z_table(cells, keep, planes * xy_major_groups())))
    rest = np.concatenate([planes * order + p for p in range(1, planes)])
    out = call(
        functools.partial(z_kernel, planes - 1, keep),
        [(3 * keep * 4, lanes)],
        2 * 6 * 2 * keep * 3 * (planes - 1) * dests * keep,
    )(
        late.reshape(dests * per, lanes),
        early,
        velocity_modes.reshape(3 * keep * 4, lanes),
        jnp.asarray(z_table(cells, keep, rest)),
    )
    return out.reshape(3, keep, rows_ky, 2, lanes)


def solution(mesh):
    return jax.shard_map(
        per_device,
        mesh=mesh,
        in_specs=(
            P(None, GROUP, "slab", None),
            P(None, GROUP, "slab", None),
            P(None, None, GROUP, None, "slab"),
        ),
        out_specs=P(None, None, GROUP, None, "slab"),
        check_vma=False,
    )
```

profile of v0, /device:TPU:32, one launch (start us, length us, event | category | flops | bytes accessed | tf_op | source)
XLA Modules:
  0.0 127.8 jit_solution(602741850737815481)
XLA Ops:
  1.1 2.4 %shard_map.73 = (f32[576,256]{1,0:T(8,128)S(1)}, f32[576,256]{1,0:T(8,128)S(1)}) custom-call(f32[3,3,192,384]{3,2,1,0:T(8,128)} %v_hbm.3, f32[3,3,192,384]{3,2,1,0:T(8,128)} %w_hbm.3, bf16[768,512]{1,0:T(8,128)(2,1)S(1)} %copy-done, f32[3,3,192,384]{3,2,1,0:T(8,128)} %w_hbm.3), custom_call_target="tpu_custom_call" | custom-call | flops 679477248 | bytes 9928704 | tf_op jit(solution)/shard_map/pallas_call | solution.py:234
  3.6 3.5 %shard_map.74 = (f32[1152,256]{1,0:T(8,128)S(1)}, f32[1152,256]{1,0:T(8,128)S(1)}) custom-call(f32[3,3,192,384]{3,2,1,0:T(8,128)} %v_hbm.3, f32[3,3,192,384]{3,2,1,0:T(8,128)} %w_hbm.3, bf16[768,512]{1,0:T(8,128)(2,1)S(1)} %copy-done, f32[576,256]{1,0:T(8,128)S(1)} %get-tuple-element.33._.keep_ref), custom_call_target="tpu_custom_call" | custom-call | flops 1358954496 | bytes 9043968 | tf_op jit(solution)/shard_map/pallas_call | solution.py:234
  7.6 3.2 %collective-permute-done.1.got_ref = f32[576,256]{1,0:T(8,128)S(1)} collective-permute-done((f32[576,256]{1,0:T(8,128)S(1)}, f32[576,256]{1,0:T(8,128)S(1)}, u32[]{:S(2)}, u32[]{:S(2)}) %collective-permute-start.1) | collective-permute-done | bytes 589856 | tf_op jit(solution)/shard_map/ppermute | solution.py:286
  11.7 2.7 %shard_map.76 = f32[3072,128]{1,0:T(8,128)} custom-call(f32[1152,256]{1,0:T(8,128)S(1)} %get-tuple-element.34.keep_ref, f32[1152,256]{1,0:T(8,128)S(1)} %collective-permute-done.got_ref, bf16[2,2,256,192]{3,2,1,0:T(8,128)(2,1)S(1)} %copy-done.1, f32[192,128]{1,0:T(8,128)S(1)} %get-tuple-element.37._.refs_0_), custom_call_target="tpu_custom_call" | custom-call | flops 905969664 | bytes 4423680 | tf_op jit(solution)/shard_map/pallas_call | solution.py:234
  14.4 15.1 %all-to-all-start = ((f32[128,24,128]{2,1,0:T(8,128)}), f32[128,24,128]{2,1,0:T(8,128)S(1)}, u32[]{:S(2)}, u32[]{:S(2)}) async-start(f32[128,24,128]{2,1,0:T(8,128)} %bitcast), calls=%async_computation | async-start | bytes 3145728 | tf_op jit(solution)/shard_map/all_to_all | solution.py:305
  30.5 3.8 %collective-permute-start.3 = (f32[192,128]{1,0:T(8,128)S(1)}, f32[192,128]{1,0:T(8,128)S(1)}, u32[]{:S(2)}, u32[]{:S(2)}) collective-permute-start(f32[192,128]{1,0:T(8,128)S(1)} %get-tuple-element.39), channel_id=1, source_target_pairs={{16,0},{18,2},{20,4},{22,6},{24,8},{26,10},{28,12},{30,14},{32,16}... | collective-permute-start | bytes 294920 | tf_op jit(solution)/shard_map/ppermute | solution.py:258
  34.3 2.0 %collective-permute-start.4 = (f32[192,128]{1,0:T(8,128)S(1)}, f32[192,128]{1,0:T(8,128)S(1)}, u32[]{:S(2)}, u32[]{:S(2)}) collective-permute-start(f32[192,128]{1,0:T(8,128)S(1)} %get-tuple-element.40), channel_id=1, source_target_pairs={{24,0},{26,2},{28,4},{30,6},{32,8},{34,10},{36,12},{38,14},{40,16}... | collective-permute-start | bytes 294920 | tf_op jit(solution)/shard_map/ppermute | solution.py:258
  36.3 3.1 %collective-permute-start.5 = (f32[192,128]{1,0:T(8,128)S(1)}, f32[192,128]{1,0:T(8,128)S(1)}, u32[]{:S(2)}, u32[]{:S(2)}) collective-permute-start(f32[192,128]{1,0:T(8,128)S(1)} %get-tuple-element.41), channel_id=1, source_target_pairs={{32,0},{34,2},{36,4},{38,6},{40,8},{42,10},{44,12},{46,14},{48,16}... | collective-permute-start | bytes 294920 | tf_op jit(solution)/shard_map/ppermute | solution.py:258
  41.2 28.5 %collective-permute-done.2.refs_1_ = f32[192,128]{1,0:T(8,128)S(1)} collective-permute-done((f32[192,128]{1,0:T(8,128)S(1)}, f32[192,128]{1,0:T(8,128)S(1)}, u32[]{:S(2)}, u32[]{:S(2)}) %collective-permute-start.2) | collective-permute-done | bytes 98336 | tf_op jit(solution)/shard_map/ppermute | solution.py:258
  69.8 1.8 %collective-permute-start.7 = (f32[192,128]{1,0:T(8,128)S(1)}, f32[192,128]{1,0:T(8,128)S(1)}, u32[]{:S(2)}, u32[]{:S(2)}) collective-permute-start(f32[192,128]{1,0:T(8,128)S(1)} %get-tuple-element.43), channel_id=1, source_target_pairs={{48,0},{50,2},{52,4},{54,6},{56,8},{58,10},{60,12},{62,14},{0,16},... | collective-permute-start | bytes 294920 | tf_op jit(solution)/shard_map/ppermute | solution.py:258
  71.9 5.1 %collective-permute-start.8 = (f32[192,128]{1,0:T(8,128)S(1)}, f32[192,128]{1,0:T(8,128)S(1)}, u32[]{:S(2)}, u32[]{:S(2)}) collective-permute-start(f32[192,128]{1,0:T(8,128)S(1)} %get-tuple-element.44), channel_id=1, source_target_pairs={{56,0},{58,2},{60,4},{62,6},{0,8},{2,10},{4,12},{6,14},{8,16},{10,... | collective-permute-start | bytes 294920 | tf_op jit(solution)/shard_map/ppermute | solution.py:258
  77.1 2.9 %collective-permute-done.4.refs_3_ = f32[192,128]{1,0:T(8,128)S(1)} collective-permute-done((f32[192,128]{1,0:T(8,128)S(1)}, f32[192,128]{1,0:T(8,128)S(1)}, u32[]{:S(2)}, u32[]{:S(2)}) %collective-permute-start.4) | collective-permute-done | bytes 98336 | tf_op jit(solution)/shard_map/ppermute | solution.py:258
  79.9 4.5 %collective-permute-done.5.refs_4_ = f32[192,128]{1,0:T(8,128)S(1)} collective-permute-done((f32[192,128]{1,0:T(8,128)S(1)}, f32[192,128]{1,0:T(8,128)S(1)}, u32[]{:S(2)}, u32[]{:S(2)}) %collective-permute-start.5) | collective-permute-done | bytes 98336 | tf_op jit(solution)/shard_map/ppermute | solution.py:258
  84.9 3.1 %collective-permute-start.9 = (f32[96,128]{1,0:T(8,128)S(1)}, f32[96,128]{1,0:T(8,128)S(1)}, u32[]{:S(2)}, u32[]{:S(2)}) collective-permute-start(f32[96,128]{1,0:T(8,128)S(1)} %get-tuple-element.46), channel_id=1, source_target_pairs={{2,0},{4,2},{6,4},{0,6},{10,8},{12,10},{14,12},{8,14},{18,16},{20,... | collective-permute-start | bytes 147464 | tf_op jit(solution)/shard_map/ppermute | solution.py:258
  89.7 2.8 %collective-permute-start.12 = (f32[96,128]{1,0:T(8,128)S(1)}, f32[96,128]{1,0:T(8,128)S(1)}, u32[]{:S(2)}, u32[]{:S(2)}) collective-permute-start(f32[96,128]{1,0:T(8,128)S(1)} %get-tuple-element.49), channel_id=1, source_target_pairs={{64,0},{66,2},{68,4},{70,6},{72,8},{74,10},{76,12},{78,14},{80,16}... | collective-permute-start | bytes 147464 | tf_op jit(solution)/shard_map/ppermute | solution.py:258
  92.5 2.6 %collective-permute-start.13 = (f32[96,128]{1,0:T(8,128)S(1)}, f32[96,128]{1,0:T(8,128)S(1)}, u32[]{:S(2)}, u32[]{:S(2)}) collective-permute-start(f32[96,128]{1,0:T(8,128)S(1)} %get-tuple-element.50), channel_id=1, source_target_pairs={{66,0},{68,2},{70,4},{64,6},{74,8},{76,10},{78,12},{72,14},{82,16}... | collective-permute-start | bytes 147464 | tf_op jit(solution)/shard_map/ppermute | solution.py:258
  96.6 2.8 %collective-permute-start.16 = (f32[96,128]{1,0:T(8,128)S(1)}, f32[96,128]{1,0:T(8,128)S(1)}, u32[]{:S(2)}, u32[]{:S(2)}) collective-permute-start(f32[96,128]{1,0:T(8,128)S(1)} %get-tuple-element.53), channel_id=1, source_target_pairs={{128,0},{130,2},{132,4},{134,6},{136,8},{138,10},{140,12},{142,14}... | collective-permute-start | bytes 147464 | tf_op jit(solution)/shard_map/ppermute | solution.py:258
  99.4 3.4 %collective-permute-start.17 = (f32[96,128]{1,0:T(8,128)S(1)}, f32[96,128]{1,0:T(8,128)S(1)}, u32[]{:S(2)}, u32[]{:S(2)}) collective-permute-start(f32[96,128]{1,0:T(8,128)S(1)} %get-tuple-element.54), channel_id=1, source_target_pairs={{130,0},{132,2},{134,4},{128,6},{138,8},{140,10},{142,12},{136,14}... | collective-permute-start | bytes 147464 | tf_op jit(solution)/shard_map/ppermute | solution.py:258
  102.8 3.3 %collective-permute-start.18 = (f32[96,128]{1,0:T(8,128)S(1)}, f32[96,128]{1,0:T(8,128)S(1)}, u32[]{:S(2)}, u32[]{:S(2)}) collective-permute-start(f32[96,128]{1,0:T(8,128)S(1)} %get-tuple-element.55), channel_id=1, source_target_pairs={{132,0},{134,2},{128,4},{130,6},{140,8},{142,10},{136,12},{138,14}... | collective-permute-start | bytes 147464 | tf_op jit(solution)/shard_map/ppermute | solution.py:258
  107.2 4.5 %collective-permute-start.21 = (f32[96,128]{1,0:T(8,128)S(1)}, f32[96,128]{1,0:T(8,128)S(1)}, u32[]{:S(2)}, u32[]{:S(2)}) collective-permute-start(f32[96,128]{1,0:T(8,128)S(1)} %get-tuple-element.58), channel_id=1, source_target_pairs={{194,0},{196,2},{198,4},{192,6},{202,8},{204,10},{206,12},{200,14}... | collective-permute-start | bytes 147464 | tf_op jit(solution)/shard_map/ppermute | solution.py:258
  111.7 2.1 %collective-permute-start.22 = (f32[96,128]{1,0:T(8,128)S(1)}, f32[96,128]{1,0:T(8,128)S(1)}, u32[]{:S(2)}, u32[]{:S(2)}) collective-permute-start(f32[96,128]{1,0:T(8,128)S(1)} %get-tuple-element.59), channel_id=1, source_target_pairs={{196,0},{198,2},{192,4},{194,6},{204,8},{206,10},{200,12},{202,14}... | collective-permute-start | bytes 147464 | tf_op jit(solution)/shard_map/ppermute | solution.py:258
  114.5 4.9 %collective-permute-done.22.refs_14_ = f32[96,128]{1,0:T(8,128)S(1)} collective-permute-done((f32[96,128]{1,0:T(8,128)S(1)}, f32[96,128]{1,0:T(8,128)S(1)}, u32[]{:S(2)}, u32[]{:S(2)}) %collective-permute-start.22) | collective-permute-done | bytes 49184 | tf_op jit(solution)/shard_map/ppermute | solution.py:258
  119.4 1.8 %collective-permute-done.23.refs_15_ = f32[96,128]{1,0:T(8,128)S(1)} collective-permute-done((f32[96,128]{1,0:T(8,128)S(1)}, f32[96,128]{1,0:T(8,128)S(1)}, u32[]{:S(2)}, u32[]{:S(2)}) %collective-permute-start.23) | collective-permute-done | bytes 49184 | tf_op jit(solution)/shard_map/ppermute | solution.py:258
  124.8 3.0 %shard_map.79 = f32[3072,128]{1,0:T(8,128)} custom-call(f32[3072,128]{1,0:T(8,128)S(1)} %bitcast.4, f32[3072,128]{1,0:T(8,128)S(1)} %shard_map.78.early_ref, f32[3072,128]{1,0:T(8,128)S(1)} %bitcast.5, bf16[2,512,256]{2,1,0:T(8,128)(2,1)S(1)} %copy-done.3), custom_call_target="tpu_custom_call" | custom-call | flops 1207959552 | bytes 6815744 | tf_op jit(solution)/shard_map/pallas_call | solution.py:234
  (43 shorter events, 14.8 us)
Async XLA Ops:
  7.0 4.7 %collective-permute-start = (f32[1152,256]{1,0:T(8,128)S(1)}, f32[1152,256]{1,0:T(8,128)S(1)}, u32[]{:S(2)}, u32[]{:S(2)}) collective-permute-start(f32[1152,256]{1,0:T(8,128)S(1)} %get-tuple-element.35), channel_id=1, source_target_pairs={{0,1},{1,0},{2,3},{3,2},{4,5},{5,4},{6,7},{7,6},{8,9},{9,8},{10,11... | collective-permute-start | bytes 3538952 | tf_op jit(solution)/shard_map/ppermute | solution.py:286
  14.4 107.9 %all-to-all-start = ((f32[128,24,128]{2,1,0:T(8,128)}), f32[128,24,128]{2,1,0:T(8,128)S(1)}, u32[]{:S(2)}, u32[]{:S(2)}) async-start(f32[128,24,128]{2,1,0:T(8,128)} %bitcast), calls=%async_computation | async-start | bytes 3145728 | tf_op jit(solution)/shard_map/all_to_all | solution.py:305
  29.5 40.2 %collective-permute-start.2 = (f32[192,128]{1,0:T(8,128)S(1)}, f32[192,128]{1,0:T(8,128)S(1)}, u32[]{:S(2)}, u32[]{:S(2)}) collective-permute-start(f32[192,128]{1,0:T(8,128)S(1)} %get-tuple-element.38), channel_id=1, source_target_pairs={{8,0},{10,2},{12,4},{14,6},{16,8},{18,10},{20,12},{22,14},{24,16},... | collective-permute-start | bytes 294920 | tf_op jit(solution)/shard_map/ppermute | solution.py:258
  30.5 41.4 %collective-permute-start.3 = (f32[192,128]{1,0:T(8,128)S(1)}, f32[192,128]{1,0:T(8,128)S(1)}, u32[]{:S(2)}, u32[]{:S(2)}) collective-permute-start(f32[192,128]{1,0:T(8,128)S(1)} %get-tuple-element.39), channel_id=1, source_target_pairs={{16,0},{18,2},{20,4},{22,6},{24,8},{26,10},{28,12},{30,14},{32,16}... | collective-permute-start | bytes 294920 | tf_op jit(solution)/shard_map/ppermute | solution.py:258
  34.3 45.7 %collective-permute-start.4 = (f32[192,128]{1,0:T(8,128)S(1)}, f32[192,128]{1,0:T(8,128)S(1)}, u32[]{:S(2)}, u32[]{:S(2)}) collective-permute-start(f32[192,128]{1,0:T(8,128)S(1)} %get-tuple-element.40), channel_id=1, source_target_pairs={{24,0},{26,2},{28,4},{30,6},{32,8},{34,10},{36,12},{38,14},{40,16}... | collective-permute-start | bytes 294920 | tf_op jit(solution)/shard_map/ppermute | solution.py:258
  36.3 48.1 %collective-permute-start.5 = (f32[192,128]{1,0:T(8,128)S(1)}, f32[192,128]{1,0:T(8,128)S(1)}, u32[]{:S(2)}, u32[]{:S(2)}) collective-permute-start(f32[192,128]{1,0:T(8,128)S(1)} %get-tuple-element.41), channel_id=1, source_target_pairs={{32,0},{34,2},{36,4},{38,6},{40,8},{42,10},{44,12},{46,14},{48,16}... | collective-permute-start | bytes 294920 | tf_op jit(solution)/shard_map/ppermute | solution.py:258
  39.4 45.0 %collective-permute-start.6 = (f32[192,128]{1,0:T(8,128)S(1)}, f32[192,128]{1,0:T(8,128)S(1)}, u32[]{:S(2)}, u32[]{:S(2)}) collective-permute-start(f32[192,128]{1,0:T(8,128)S(1)} %get-tuple-element.42), channel_id=1, source_target_pairs={{40,0},{42,2},{44,4},{46,6},{48,8},{50,10},{52,12},{54,14},{56,16}... | collective-permute-start | bytes 294920 | tf_op jit(solution)/shard_map/ppermute | solution.py:258
  69.8 14.6 %collective-permute-start.7 = (f32[192,128]{1,0:T(8,128)S(1)}, f32[192,128]{1,0:T(8,128)S(1)}, u32[]{:S(2)}, u32[]{:S(2)}) collective-permute-start(f32[192,128]{1,0:T(8,128)S(1)} %get-tuple-element.43), channel_id=1, source_target_pairs={{48,0},{50,2},{52,4},{54,6},{56,8},{58,10},{60,12},{62,14},{0,16},... | collective-permute-start | bytes 294920 | tf_op jit(solution)/shard_map/ppermute | solution.py:258
  71.9 12.5 %collective-permute-start.8 = (f32[192,128]{1,0:T(8,128)S(1)}, f32[192,128]{1,0:T(8,128)S(1)}, u32[]{:S(2)}, u32[]{:S(2)}) collective-permute-start(f32[192,128]{1,0:T(8,128)S(1)} %get-tuple-element.44), channel_id=1, source_target_pairs={{56,0},{58,2},{60,4},{62,6},{0,8},{2,10},{4,12},{6,14},{8,16},{10,... | collective-permute-start | bytes 294920 | tf_op jit(solution)/shard_map/ppermute | solution.py:258
  84.9 10.2 %collective-permute-start.9 = (f32[96,128]{1,0:T(8,128)S(1)}, f32[96,128]{1,0:T(8,128)S(1)}, u32[]{:S(2)}, u32[]{:S(2)}) collective-permute-start(f32[96,128]{1,0:T(8,128)S(1)} %get-tuple-element.46), channel_id=1, source_target_pairs={{2,0},{4,2},{6,4},{0,6},{10,8},{12,10},{14,12},{8,14},{18,16},{20,... | collective-permute-start | bytes 147464 | tf_op jit(solution)/shard_map/ppermute | solution.py:258
  88.0 8.6 %collective-permute-start.10 = (f32[96,128]{1,0:T(8,128)S(1)}, f32[96,128]{1,0:T(8,128)S(1)}, u32[]{:S(2)}, u32[]{:S(2)}) collective-permute-start(f32[96,128]{1,0:T(8,128)S(1)} %get-tuple-element.47), channel_id=1, source_target_pairs={{4,0},{6,2},{0,4},{2,6},{12,8},{14,10},{8,12},{10,14},{20,16},{22,... | collective-permute-start | bytes 147464 | tf_op jit(solution)/shard_map/ppermute | solution.py:258
  88.9 7.8 %collective-permute-start.11 = (f32[96,128]{1,0:T(8,128)S(1)}, f32[96,128]{1,0:T(8,128)S(1)}, u32[]{:S(2)}, u32[]{:S(2)}) collective-permute-start(f32[96,128]{1,0:T(8,128)S(1)} %get-tuple-element.48), channel_id=1, source_target_pairs={{6,0},{0,2},{2,4},{4,6},{14,8},{8,10},{10,12},{12,14},{22,16},{16,... | collective-permute-start | bytes 147464 | tf_op jit(solution)/shard_map/ppermute | solution.py:258
  89.7 9.7 %collective-permute-start.12 = (f32[96,128]{1,0:T(8,128)S(1)}, f32[96,128]{1,0:T(8,128)S(1)}, u32[]{:S(2)}, u32[]{:S(2)}) collective-permute-start(f32[96,128]{1,0:T(8,128)S(1)} %get-tuple-element.49), channel_id=1, source_target_pairs={{64,0},{66,2},{68,4},{70,6},{72,8},{74,10},{76,12},{78,14},{80,16}... | collective-permute-start | bytes 147464 | tf_op jit(solution)/shard_map/ppermute | solution.py:258
  92.5 10.3 %collective-permute-start.13 = (f32[96,128]{1,0:T(8,128)S(1)}, f32[96,128]{1,0:T(8,128)S(1)}, u32[]{:S(2)}, u32[]{:S(2)}) collective-permute-start(f32[96,128]{1,0:T(8,128)S(1)} %get-tuple-element.50), channel_id=1, source_target_pairs={{66,0},{68,2},{70,4},{64,6},{74,8},{76,10},{78,12},{72,14},{82,16}... | collective-permute-start | bytes 147464 | tf_op jit(solution)/shard_map/ppermute | solution.py:258
  95.1 10.9 %collective-permute-start.14 = (f32[96,128]{1,0:T(8,128)S(1)}, f32[96,128]{1,0:T(8,128)S(1)}, u32[]{:S(2)}, u32[]{:S(2)}) collective-permute-start(f32[96,128]{1,0:T(8,128)S(1)} %get-tuple-element.51), channel_id=1, source_target_pairs={{68,0},{70,2},{64,4},{66,6},{76,8},{78,10},{72,12},{74,14},{84,16}... | collective-permute-start | bytes 147464 | tf_op jit(solution)/shard_map/ppermute | solution.py:258
  96.6 9.6 %collective-permute-start.15 = (f32[96,128]{1,0:T(8,128)S(1)}, f32[96,128]{1,0:T(8,128)S(1)}, u32[]{:S(2)}, u32[]{:S(2)}) collective-permute-start(f32[96,128]{1,0:T(8,128)S(1)} %get-tuple-element.52), channel_id=1, source_target_pairs={{70,0},{64,2},{66,4},{68,6},{78,8},{72,10},{74,12},{76,14},{86,16}... | collective-permute-start | bytes 147464 | tf_op jit(solution)/shard_map/ppermute | solution.py:258
  96.6 10.5 %collective-permute-start.16 = (f32[96,128]{1,0:T(8,128)S(1)}, f32[96,128]{1,0:T(8,128)S(1)}, u32[]{:S(2)}, u32[]{:S(2)}) collective-permute-start(f32[96,128]{1,0:T(8,128)S(1)} %get-tuple-element.53), channel_id=1, source_target_pairs={{128,0},{130,2},{132,4},{134,6},{136,8},{138,10},{140,12},{142,14}... | collective-permute-start | bytes 147464 | tf_op jit(solution)/shard_map/ppermute | solution.py:258
  99.4 12.3 %collective-permute-start.17 = (f32[96,128]{1,0:T(8,128)S(1)}, f32[96,128]{1,0:T(8,128)S(1)}, u32[]{:S(2)}, u32[]{:S(2)}) collective-permute-start(f32[96,128]{1,0:T(8,128)S(1)} %get-tuple-element.54), channel_id=1, source_target_pairs={{130,0},{132,2},{134,4},{128,6},{138,8},{140,10},{142,12},{136,14}... | collective-permute-start | bytes 147464 | tf_op jit(solution)/shard_map/ppermute | solution.py:258
  102.8 11.0 %collective-permute-start.18 = (f32[96,128]{1,0:T(8,128)S(1)}, f32[96,128]{1,0:T(8,128)S(1)}, u32[]{:S(2)}, u32[]{:S(2)}) collective-permute-start(f32[96,128]{1,0:T(8,128)S(1)} %get-tuple-element.55), channel_id=1, source_target_pairs={{132,0},{134,2},{128,4},{130,6},{140,8},{142,10},{136,12},{138,14}... | collective-permute-start | bytes 147464 | tf_op jit(solution)/shard_map/ppermute | solution.py:258
  106.1 8.4 %collective-permute-start.19 = (f32[96,128]{1,0:T(8,128)S(1)}, f32[96,128]{1,0:T(8,128)S(1)}, u32[]{:S(2)}, u32[]{:S(2)}) collective-permute-start(f32[96,128]{1,0:T(8,128)S(1)} %get-tuple-element.56), channel_id=1, source_target_pairs={{134,0},{128,2},{130,4},{132,6},{142,8},{136,10},{138,12},{140,14}... | collective-permute-start | bytes 147464 | tf_op jit(solution)/shard_map/ppermute | solution.py:258
  106.2 8.3 %collective-permute-start.20 = (f32[96,128]{1,0:T(8,128)S(1)}, f32[96,128]{1,0:T(8,128)S(1)}, u32[]{:S(2)}, u32[]{:S(2)}) collective-permute-start(f32[96,128]{1,0:T(8,128)S(1)} %get-tuple-element.57), channel_id=1, source_target_pairs={{192,0},{194,2},{196,4},{198,6},{200,8},{202,10},{204,12},{206,14}... | collective-permute-start | bytes 147464 | tf_op jit(solution)/shard_map/ppermute | solution.py:258
  107.2 7.3 %collective-permute-start.21 = (f32[96,128]{1,0:T(8,128)S(1)}, f32[96,128]{1,0:T(8,128)S(1)}, u32[]{:S(2)}, u32[]{:S(2)}) collective-permute-start(f32[96,128]{1,0:T(8,128)S(1)} %get-tuple-element.58), channel_id=1, source_target_pairs={{194,0},{196,2},{198,4},{192,6},{202,8},{204,10},{206,12},{200,14}... | collective-permute-start | bytes 147464 | tf_op jit(solution)/shard_map/ppermute | solution.py:258
  111.7 7.7 %collective-permute-start.22 = (f32[96,128]{1,0:T(8,128)S(1)}, f32[96,128]{1,0:T(8,128)S(1)}, u32[]{:S(2)}, u32[]{:S(2)}) collective-permute-start(f32[96,128]{1,0:T(8,128)S(1)} %get-tuple-element.59), channel_id=1, source_target_pairs={{196,0},{198,2},{192,4},{194,6},{204,8},{206,10},{200,12},{202,14}... | collective-permute-start | bytes 147464 | tf_op jit(solution)/shard_map/ppermute | solution.py:258
  113.8 7.4 %collective-permute-start.23 = (f32[96,128]{1,0:T(8,128)S(1)}, f32[96,128]{1,0:T(8,128)S(1)}, u32[]{:S(2)}, u32[]{:S(2)}) collective-permute-start(f32[96,128]{1,0:T(8,128)S(1)} %get-tuple-element.60), channel_id=1, source_target_pairs={{198,0},{192,2},{194,4},{196,6},{206,8},{200,10},{202,12},{204,14}... | collective-permute-start | bytes 147464 | tf_op jit(solution)/shard_map/ppermute | solution.py:258
  (6 other events, 121.4 us)
where the time goes:
time: 128 us
  starting transfers between devices  63.2 us (49%)
  waiting for transfers between devices  46.9 us (37%)
  Pallas kernels  14 us (11%)
  local copies, waits for them, and re-layouts  3.59 us (3%)
    ppermute x22, starting transfers between devices, from_shift(): return lax.ppermute(value, GROUP, pairs)  47.5 us
    ppermute x22, waiting for transfers between devices, from_shift(): return lax.ppermute(value, GROUP, pairs)  43.7 us
    all_to_all x1, starting transfers between devices, per_device(): lax.all_to_all(packed.reshape(dests, per, lanes), GROUP, 0, 0, axis_index...  15.1 us
    pallas_call x7, Pallas kernels, run(): pl.pallas_call(kernel, out_shape=shapes[0] if single else shapes, in_spec...  14 us
    unnamed x10, local copies, waits for them, and re-layouts  3.59 us
    ppermute x2, waiting for transfers between devices, per_device(): gots.append(lax.ppermute(other, 'slab', [(0, 1), (1, 0)]))  3.18 us
  transfers between devices with their start and end apart: 25, of which 8 were waited for; matrix products, arithmetic and copies ran while one was open for 0% of the time, Pallas kernels for 2%

commit v1 on v0

--- a/solution.py
+++ b/solution.py
@@ -150,79 +150,100 @@
             outs[shift][k * NXY : (k + 1) * NXY] = all_ref[pl.ds(pl.multiple_of(k * dests + to * NXY, NXY), NXY), :]
 
 
-def turn_kernel(*refs):
+def turn_x_kernel(*refs):
     gots, outs, all_ref = refs[:NZ], refs[NZ:-1], refs[-1]
-    y, z, x = place()
+    _, z, x = place()
     size = gots[0].shape[0]
     for shift in range(NZ):
         source = lax.rem(z + shift, NZ)
         all_ref[pl.ds(pl.multiple_of(source * size, size), size), :] = gots[shift][...]
-    count = all_ref.shape[0] // NXY
-    for dy in range(NY):
-        for dx in range(NX):
-            to = lax.rem(y - dy + NY, NY) * NX + lax.rem(x - dx + NX, NX)
-            outs[dy * NX + dx][...] = all_ref[pl.ds(to, count, NXY), :]
-
-
-def early_kernel(keep, *refs):
-    gots, table_ref, out_ref, all_ref = refs[:NXY], refs[NXY], refs[NXY + 1], refs[NXY + 2]
+    for shift in range(NX):
+        to = lax.rem(x - shift + NX, NX)
+        outs[shift][...] = all_ref[pl.ds(to, all_ref.shape[0] // NX, NX), :]
+
+
+def turn_y_kernel(*refs):
+    gots, outs = refs[:NX], refs[NX:]
     y, _, x = place()
-    lanes = out_ref.shape[1]
-    kinds = gots[0].shape[0] // NZ
-    sources = NXY * NZ
-    for dy in range(NY):
-        for dx in range(NX):
-            source = lax.rem(y + dy, NY) * NX + lax.rem(x + dx, NX)
-            for k in range(kinds):
-                at = pl.multiple_of(k * sources + source * NZ, NZ)
-                all_ref[pl.ds(at, NZ), :] = gots[dy * NX + dx][pl.ds(k, NZ, kinds), :]
-    for pair in range(kinds // 2):
-        both = [all_ref[(pair * 2 + q) * sources : (pair * 2 + q + 1) * sources] for q in range(2)]
-        out = transformed(table_ref[0], table_ref[1], jnp.concatenate(both, axis=1))
-        out_ref[pair * 2 * keep : (pair * 2 + 1) * keep] = out[:keep, :lanes] + out[keep:, lanes:]
-        out_ref[(pair * 2 + 1) * keep : (pair * 2 + 2) * keep] = out[:keep, lanes:] - out[keep:, :lanes]
-
-
-def z_kernel(planes, keep, x_ref, early_ref, modes_ref, table_ref, out_ref):
+    size = gots[0].shape[0] // NY
+    for dx in range(NX):
+        at = pl.multiple_of(lax.rem(x + dx, NX) * size, size)
+        for dy in range(NY):
+            to = lax.rem(y - dy + NY, NY)
+            outs[dy][pl.ds(at, size), :] = gots[dx][pl.ds(to, size, NY), :]
+
+
+def wave_numbers(keep, lanes):
     group = lax.axis_index("section") * lax.axis_size("pen") + lax.axis_index("pen")
-    slab = lax.axis_index("slab")
-    lanes = x_ref.shape[1]
-    per = 3 * planes * 4
-    sources = x_ref.shape[0] // per
     limit = -(keep // 2)
     visc = 0.5 / (keep // 2) ** 2
     row = lax.broadcasted_iota(jnp.int32, (keep, lanes), 0)
-    col = lax.broadcasted_iota(jnp.int32, (keep, lanes), 1) + slab * lanes
+    col = lax.broadcasted_iota(jnp.int32, (keep, lanes), 1) + lax.axis_index("slab") * lanes
     kz = jnp.where(row < keep // 2, row, row - keep)
     kx = jnp.where(col < keep // 2, col, col - keep)
     for parity in range(2):
         index = group * 2 + parity
         ky = jnp.where(index < keep // 2, index, index - keep)
         mask = ((kx != limit) & (kz != limit) & (ky != limit)).astype(jnp.float32)
-        fx, fz = kx.astype(jnp.float32), kz.astype(jnp.float32)
-        fy = ky.astype(jnp.float32)
-        ksq = fx * fx + fy * fy + fz * fz
-        inverse = 1.0 / jnp.maximum(ksq, 1.0)
-        damp = visc * ksq
-        real, imag = [], []
+        waves = (kx.astype(jnp.float32), ky.astype(jnp.float32), kz.astype(jnp.float32))
+        ksq = waves[0] * waves[0] + waves[1] * waves[1] + waves[2] * waves[2]
+        yield parity, waves, mask, 1.0 / jnp.maximum(ksq, 1.0), visc * ksq
+
+
+def projected(s, waves, mask, inverse):
+    inner = (waves[0] * s[0] + waves[1] * s[1] + waves[2] * s[2]) * inverse
+    return [mask * (s[c] - waves[c] * inner) for c in range(3)]
+
+
+def z_sums(keep, lanes, table, columns):
+    out = transformed(table[0], table[1], columns)
+    return out[:keep, :lanes] + out[keep:, lanes:], out[:keep, lanes:] - out[keep:, :lanes]
+
+
+def early_kernel(keep, *refs):
+    gots, (modes_ref, table_ref, out_ref, all_ref) = refs[:NY], refs[NY:]
+    y, _, _ = place()
+    lanes = out_ref.shape[1]
+    kinds = gots[0].shape[0] // (NX * NZ)
+    sources = NY * NX * NZ
+    for dy in range(NY):
+        source = lax.rem(y + dy, NY) * (NX * NZ)
+        for k in range(kinds):
+            at = pl.multiple_of(k * sources + source, NX * NZ)
+            all_ref[pl.ds(at, NX * NZ), :] = gots[dy][pl.ds(k, NX * NZ, kinds), :]
+    for parity, waves, mask, inverse, damp in wave_numbers(keep, lanes):
+        sums = []
         for c in range(3):
-            columns = []
-            for q in range(2):
-                base = parity * 2 + q
-                columns.append(
-                    jnp.concatenate(
-                        [x_ref[pl.ds(base + (p * 3 + c) * 4, sources, per), :] for p in range(planes)], axis=0
-                    )
+            base = c * 4 + parity * 2
+            both = [all_ref[(base + q) * sources : (base + q + 1) * sources] for q in range(2)]
+            sums.append(z_sums(keep, lanes, table_ref, jnp.concatenate(both, axis=1)))
+        for q in range(2):
+            for c, value in enumerate(projected([s[q] for s in sums], waves, mask, inverse)):
+                where = pl.ds(c * keep * 4 + parity * 2 + q, keep, 4)
+                out_ref[where, :] = value - damp * modes_ref[where, :]
+
+
+def z_kernel(planes, keep, x_ref, early_ref, table_hbm, out_ref, table_ref, sem):
+    copy = pltpu.make_async_copy(table_hbm, table_ref, sem)
+    copy.start()
+    lanes = x_ref.shape[1]
+    per = 3 * planes * 4
+    sources = x_ref.shape[0] // per
+    copy.wait()
+    for parity, waves, mask, inverse, _ in wave_numbers(keep, lanes):
+        sums = []
+        for c in range(3):
+            columns = [
+                jnp.concatenate(
+                    [x_ref[pl.ds((p * 3 + c) * 4 + parity * 2 + q, sources, per), :] for p in range(planes)], axis=0
                 )
-            out = transformed(table_ref[0], table_ref[1], jnp.concatenate(columns, axis=1))
-            at = (c * 2 + parity) * 2 * keep
-            real.append(early_ref[at : at + keep] + (out[:keep, :lanes] + out[keep:, lanes:]))
-            imag.append(early_ref[at + keep : at + 2 * keep] + (out[:keep, lanes:] - out[keep:, :lanes]))
-        for q, s in enumerate((real, imag)):
-            inner = (fx * s[0] + fy * s[1] + fz * s[2]) * inverse
-            for c, k in enumerate((fx, fy, fz)):
+                for q in range(2)
+            ]
+            sums.append(z_sums(keep, lanes, table_ref, jnp.concatenate(columns, axis=1)))
+        for q in range(2):
+            for c, value in enumerate(projected([s[q] for s in sums], waves, mask, inverse)):
                 where = pl.ds(c * keep * 4 + parity * 2 + q, keep, 4)
-                out_ref[where, :] = mask * (s[c] - k * inner) - damp * modes_ref[where, :]
+                out_ref[where, :] = value + early_ref[where, :]
 
 
 def call(kernel, outs, flops=0, scratch=(), spaces=None, limit=40 << 20):
@@ -305,25 +326,32 @@
     late = lax.all_to_all(
         packed.reshape(dests, per, lanes), GROUP, 0, 0, axis_index_groups=[order.tolist()], tiled=True
     )
-    turned = call(turn_kernel, [(NZ * kinds, lanes)] * NXY, 0, [VMEM((NZ * kinds * NXY, lanes), jnp.float32)])(*arrived)
-    spread = [turned[0]] + [from_shift(turned[d], d // NX, 0, d % NX) for d in range(1, NXY)]
+    turned = call(
+        turn_x_kernel, [(NZ * kinds * NY, lanes)] * NX, 0, [VMEM((NZ * kinds * NXY, lanes), jnp.float32)]
+    )(*arrived)
+    turned = [turned[0]] + [from_shift(turned[d], 0, 0, d) for d in range(1, NX)]
+    turned = call(turn_y_kernel, [(NX * NZ * kinds, lanes)] * NY)(*turned)
+    spread = [turned[0]] + [from_shift(turned[d], d, 0, 0) for d in range(1, NY)]
     early = call(
         functools.partial(early_kernel, keep),
-        [(kinds * keep, lanes)],
+        [(3 * keep * 4, lanes)],
         2 * 6 * 2 * keep * 3 * dests * keep,
         [VMEM((kinds * dests, lanes), jnp.float32)],
-    )(*spread, jnp.asarray(z_table(cells, keep, planes * xy_major_groups())))
+    )(
+        *spread,
+        velocity_modes.reshape(3 * keep * 4, lanes),
+        jnp.asarray(z_table(cells, keep, planes * xy_major_groups())),
+    )
     rest = np.concatenate([planes * order + p for p in range(1, planes)])
+    table_z = jnp.asarray(z_table(cells, keep, rest))
     out = call(
         functools.partial(z_kernel, planes - 1, keep),
         [(3 * keep * 4, lanes)],
         2 * 6 * 2 * keep * 3 * (planes - 1) * dests * keep,
-    )(
-        late.reshape(dests * per, lanes),
-        early,
-        velocity_modes.reshape(3 * keep * 4, lanes),
-        jnp.asarray(z_table(cells, keep, rest)),
-    )
+        [VMEM(table_z.shape, jnp.bfloat16), pltpu.SemaphoreType.DMA],
+        [VMEM, VMEM, pltpu.HBM],
+        40 << 20,
+    )(late.reshape(dests * per, lanes), early, table_z)
     return out.reshape(3, keep, rows_ky, 2, lanes)
 
 

time: 128 us -> 120 us (0.938)
  starting transfers between devices: 63.2 us -> 43.6 us
  waiting for transfers between devices: 46.9 us -> 58.8 us
  local copies, waits for them, and re-layouts: 3.59 us -> 2.19 us
    ppermute x22 -> x13, starting transfers between devices: 47.5 us -> 27.9 us  [from_shift(): return lax.ppermute(value, GROUP, pairs)]
    ppermute x22 -> x13, waiting for transfers between devices: 43.7 us -> 55.6 us  [from_shift(): return lax.ppermute(value, GROUP, pairs)]
    unnamed x10, local copies, waits for them, and re-layouts: 3.59 us -> 2.19 us
    pallas_call x7 -> x8, Pallas kernels: 14 us -> 13.9 us  [run(): pl.pallas_call(kernel, out_shape=shapes[0] if single else shapes, in_spec...]
  transfers between devices with their start and end apart: 25 -> 16, of which waited for: 8 -> 11; matrix products, arithmetic and copies ran while one was open for 0% -> 0% of each run, Pallas kernels for 2% -> 2%
where the time goes in v1:
time: 120 us; the launch traced here: 119 us
  waiting for transfers between devices  58.8 us (49%)
  starting transfers between devices  43.6 us (36%)
  Pallas kernels  13.9 us (12%)
  local copies, waits for them, and re-layouts  2.19 us (2%)
    ppermute x13, waiting for transfers between devices, from_shift(): return lax.ppermute(value, GROUP, pairs)  55.6 us
    ppermute x13, starting transfers between devices, from_shift(): return lax.ppermute(value, GROUP, pairs)  27.9 us
    all_to_all x1, starting transfers between devices, per_device(): lax.all_to_all(packed.reshape(dests, per, lanes), GROUP, 0, 0, axis_index...  15.1 us
    pallas_call x8, Pallas kernels, run(): pl.pallas_call(kernel, out_shape=shapes[0] if single else shapes, in_spec...  13.9 us
    ppermute x2, waiting for transfers between devices, per_device(): gots.append(lax.ppermute(other, 'slab', [(0, 1), (1, 0)]))  3.18 us
  transfers between devices with their start and end apart: 16, of which 11 were waited for; matrix products, arithmetic and copies ran while one was open for 0% of the time, Pallas kernels for 2%

profile of v1, /device:TPU:32, one launch (start us, length us, event | category | flops | bytes accessed | tf_op | source)
XLA Modules:
  0.0 118.7 jit_solution(10799847740341642005)
XLA Ops:
  1.1 2.4 %shard_map.73 = (f32[576,256]{1,0:T(8,128)S(1)}, f32[576,256]{1,0:T(8,128)S(1)}) custom-call(f32[3,3,192,384]{3,2,1,0:T(8,128)} %v_hbm.3, f32[3,3,192,384]{3,2,1,0:T(8,128)} %w_hbm.3, bf16[768,512]{1,0:T(8,128)(2,1)S(1)} %copy-done, f32[3,3,192,384]{3,2,1,0:T(8,128)} %w_hbm.3), custom_call_target="tpu_custom_call" | custom-call | flops 679477248 | bytes 9928704 | tf_op jit(solution)/shard_map/pallas_call | solution.py:255
  3.6 3.5 %shard_map.74 = (f32[1152,256]{1,0:T(8,128)S(1)}, f32[1152,256]{1,0:T(8,128)S(1)}) custom-call(f32[3,3,192,384]{3,2,1,0:T(8,128)} %v_hbm.3, f32[3,3,192,384]{3,2,1,0:T(8,128)} %w_hbm.3, bf16[768,512]{1,0:T(8,128)(2,1)S(1)} %copy-done, f32[576,256]{1,0:T(8,128)S(1)} %get-tuple-element.25._.keep_ref), custom_call_target="tpu_custom_call" | custom-call | flops 1358954496 | bytes 9043968 | tf_op jit(solution)/shard_map/pallas_call | solution.py:255
  7.6 3.2 %collective-permute-done.1.got_ref = f32[576,256]{1,0:T(8,128)S(1)} collective-permute-done((f32[576,256]{1,0:T(8,128)S(1)}, f32[576,256]{1,0:T(8,128)S(1)}, u32[]{:S(2)}, u32[]{:S(2)}) %collective-permute-start.1) | collective-permute-done | bytes 589856 | tf_op jit(solution)/shard_map/ppermute | solution.py:307
  11.7 2.7 %shard_map.76 = f32[3072,128]{1,0:T(8,128)} custom-call(f32[1152,256]{1,0:T(8,128)S(1)} %get-tuple-element.26.keep_ref, f32[1152,256]{1,0:T(8,128)S(1)} %collective-permute-done.got_ref, bf16[2,2,256,192]{3,2,1,0:T(8,128)(2,1)S(1)} %copy-done.1, f32[192,128]{1,0:T(8,128)S(1)} %get-tuple-element.29._.refs_0_), custom_call_target="tpu_custom_call" | custom-call | flops 905969664 | bytes 4423680 | tf_op jit(solution)/shard_map/pallas_call | solution.py:255
  14.4 15.1 %all-to-all-start = ((f32[128,24,128]{2,1,0:T(8,128)}), f32[128,24,128]{2,1,0:T(8,128)S(1)}, u32[]{:S(2)}, u32[]{:S(2)}) async-start(f32[128,24,128]{2,1,0:T(8,128)} %bitcast), calls=%async_computation | async-start | bytes 3145728 | tf_op jit(solution)/shard_map/all_to_all | solution.py:326
  30.5 3.8 %collective-permute-start.3 = (f32[192,128]{1,0:T(8,128)S(1)}, f32[192,128]{1,0:T(8,128)S(1)}, u32[]{:S(2)}, u32[]{:S(2)}) collective-permute-start(f32[192,128]{1,0:T(8,128)S(1)} %get-tuple-element.31), channel_id=1, source_target_pairs={{16,0},{18,2},{20,4},{22,6},{24,8},{26,10},{28,12},{30,14},{32,16}... | collective-permute-start | bytes 294920 | tf_op jit(solution)/shard_map/ppermute | solution.py:279
  34.3 2.0 %collective-permute-start.4 = (f32[192,128]{1,0:T(8,128)S(1)}, f32[192,128]{1,0:T(8,128)S(1)}, u32[]{:S(2)}, u32[]{:S(2)}) collective-permute-start(f32[192,128]{1,0:T(8,128)S(1)} %get-tuple-element.32), channel_id=1, source_target_pairs={{24,0},{26,2},{28,4},{30,6},{32,8},{34,10},{36,12},{38,14},{40,16}... | collective-permute-start | bytes 294920 | tf_op jit(solution)/shard_map/ppermute | solution.py:279
  36.3 3.1 %collective-permute-start.5 = (f32[192,128]{1,0:T(8,128)S(1)}, f32[192,128]{1,0:T(8,128)S(1)}, u32[]{:S(2)}, u32[]{:S(2)}) collective-permute-start(f32[192,128]{1,0:T(8,128)S(1)} %get-tuple-element.33), channel_id=1, source_target_pairs={{32,0},{34,2},{36,4},{38,6},{40,8},{42,10},{44,12},{46,14},{48,16}... | collective-permute-start | bytes 294920 | tf_op jit(solution)/shard_map/ppermute | solution.py:279
  39.4 1.8 %collective-permute-start.6 = (f32[192,128]{1,0:T(8,128)S(1)}, f32[192,128]{1,0:T(8,128)S(1)}, u32[]{:S(2)}, u32[]{:S(2)}) collective-permute-start(f32[192,128]{1,0:T(8,128)S(1)} %get-tuple-element.34), channel_id=1, source_target_pairs={{40,0},{42,2},{44,4},{46,6},{48,8},{50,10},{52,12},{54,14},{56,16}... | collective-permute-start | bytes 294920 | tf_op jit(solution)/shard_map/ppermute | solution.py:279
  41.2 28.5 %collective-permute-done.2.refs_1_ = f32[192,128]{1,0:T(8,128)S(1)} collective-permute-done((f32[192,128]{1,0:T(8,128)S(1)}, f32[192,128]{1,0:T(8,128)S(1)}, u32[]{:S(2)}, u32[]{:S(2)}) %collective-permute-start.2) | collective-permute-done | bytes 98336 | tf_op jit(solution)/shard_map/ppermute | solution.py:279
  69.8 1.8 %collective-permute-start.7 = (f32[192,128]{1,0:T(8,128)S(1)}, f32[192,128]{1,0:T(8,128)S(1)}, u32[]{:S(2)}, u32[]{:S(2)}) collective-permute-start(f32[192,128]{1,0:T(8,128)S(1)} %get-tuple-element.35), channel_id=1, source_target_pairs={{48,0},{50,2},{52,4},{54,6},{56,8},{58,10},{60,12},{62,14},{0,16},... | collective-permute-start | bytes 294920 | tf_op jit(solution)/shard_map/ppermute | solution.py:279
  71.9 5.1 %collective-permute-start.8 = (f32[192,128]{1,0:T(8,128)S(1)}, f32[192,128]{1,0:T(8,128)S(1)}, u32[]{:S(2)}, u32[]{:S(2)}) collective-permute-start(f32[192,128]{1,0:T(8,128)S(1)} %get-tuple-element.36), channel_id=1, source_target_pairs={{56,0},{58,2},{60,4},{62,6},{0,8},{2,10},{4,12},{6,14},{8,16},{10,... | collective-permute-start | bytes 294920 | tf_op jit(solution)/shard_map/ppermute | solution.py:279
  77.1 2.9 %collective-permute-done.4.refs_3_ = f32[192,128]{1,0:T(8,128)S(1)} collective-permute-done((f32[192,128]{1,0:T(8,128)S(1)}, f32[192,128]{1,0:T(8,128)S(1)}, u32[]{:S(2)}, u32[]{:S(2)}) %collective-permute-start.4) | collective-permute-done | bytes 98336 | tf_op jit(solution)/shard_map/ppermute | solution.py:279
  79.9 4.5 %collective-permute-done.5.refs_4_ = f32[192,128]{1,0:T(8,128)S(1)} collective-permute-done((f32[192,128]{1,0:T(8,128)S(1)}, f32[192,128]{1,0:T(8,128)S(1)}, u32[]{:S(2)}, u32[]{:S(2)}) %collective-permute-start.5) | collective-permute-done | bytes 98336 | tf_op jit(solution)/shard_map/ppermute | solution.py:279
  84.6 3.1 %collective-permute-start.9 = (f32[384,128]{1,0:T(8,128)S(1)}, f32[384,128]{1,0:T(8,128)S(1)}, u32[]{:S(2)}, u32[]{:S(2)}) collective-permute-start(f32[384,128]{1,0:T(8,128)S(1)} %get-tuple-element.38), channel_id=1, source_target_pairs={{2,0},{4,2},{6,4},{0,6},{10,8},{12,10},{14,12},{8,14},{18,16},{20,... | collective-permute-start | bytes 589832 | tf_op jit(solution)/shard_map/ppermute | solution.py:279
  89.4 5.5 %collective-permute-done.9.refs_1_ = f32[384,128]{1,0:T(8,128)S(1)} collective-permute-done((f32[384,128]{1,0:T(8,128)S(1)}, f32[384,128]{1,0:T(8,128)S(1)}, u32[]{:S(2)}, u32[]{:S(2)}) %collective-permute-start.9) | collective-permute-done | bytes 196640 | tf_op jit(solution)/shard_map/ppermute | solution.py:279
  94.9 1.6 %collective-permute-done.10.refs_2_ = f32[384,128]{1,0:T(8,128)S(1)} collective-permute-done((f32[384,128]{1,0:T(8,128)S(1)}, f32[384,128]{1,0:T(8,128)S(1)}, u32[]{:S(2)}, u32[]{:S(2)}) %collective-permute-start.10) | collective-permute-done | bytes 196640 | tf_op jit(solution)/shard_map/ppermute | solution.py:279
  96.5 2.1 %collective-permute-done.11.refs_3_ = f32[384,128]{1,0:T(8,128)S(1)} collective-permute-done((f32[384,128]{1,0:T(8,128)S(1)}, f32[384,128]{1,0:T(8,128)S(1)}, u32[]{:S(2)}, u32[]{:S(2)}) %collective-permute-start.11) | collective-permute-done | bytes 196640 | tf_op jit(solution)/shard_map/ppermute | solution.py:279
  98.7 2.9 %collective-permute-start.12 = (f32[384,128]{1,0:T(8,128)S(1)}, f32[384,128]{1,0:T(8,128)S(1)}, u32[]{:S(2)}, u32[]{:S(2)}) collective-permute-start(f32[384,128]{1,0:T(8,128)S(1)} %get-tuple-element.42), channel_id=1, source_target_pairs={{64,0},{66,2},{68,4},{70,6},{72,8},{74,10},{76,12},{78,14},{80,16}... | collective-permute-start | bytes 589832 | tf_op jit(solution)/shard_map/ppermute | solution.py:279
  103.2 6.4 %collective-permute-done.12.refs_1_ = f32[384,128]{1,0:T(8,128)S(1)} collective-permute-done((f32[384,128]{1,0:T(8,128)S(1)}, f32[384,128]{1,0:T(8,128)S(1)}, u32[]{:S(2)}, u32[]{:S(2)}) %collective-permute-start.12) | collective-permute-done | bytes 196640 | tf_op jit(solution)/shard_map/ppermute | solution.py:279
  109.6 1.3 %collective-permute-done.13.refs_2_ = f32[384,128]{1,0:T(8,128)S(1)} collective-permute-done((f32[384,128]{1,0:T(8,128)S(1)}, f32[384,128]{1,0:T(8,128)S(1)}, u32[]{:S(2)}, u32[]{:S(2)}) %collective-permute-start.13) | collective-permute-done | bytes 196640 | tf_op jit(solution)/shard_map/ppermute | solution.py:279
  110.9 2.4 %collective-permute-done.14.refs_3_ = f32[384,128]{1,0:T(8,128)S(1)} collective-permute-done((f32[384,128]{1,0:T(8,128)S(1)}, f32[384,128]{1,0:T(8,128)S(1)}, u32[]{:S(2)}, u32[]{:S(2)}) %collective-permute-start.14) | collective-permute-done | bytes 196640 | tf_op jit(solution)/shard_map/ppermute | solution.py:279
  113.3 1.2 %shard_map.79.early_ref = f32[3072,128]{1,0:T(8,128)S(1)} custom-call(f32[384,128]{1,0:T(8,128)S(1)} %get-tuple-element.41.refs_0_, f32[384,128]{1,0:T(8,128)S(1)} %collective-permute-done.12.refs_1_, f32[384,128]{1,0:T(8,128)S(1)} %collective-permute-done.13.refs_2_, f32[384,128]{1,0:T(8,128)S(1)} %collective-permute-done.14.refs_3_, ...), custom_call_target="tpu_custom_call" | custom-call | flops 603979776 | bytes 4194304 | tf_op jit(solution)/shard_map/pallas_call | solution.py:255
  115.6 3.0 %shard_map.80 = f32[3072,128]{1,0:T(8,128)} custom-call(f32[3072,128]{1,0:T(8,128)S(1)} %bitcast.4, f32[3072,128]{1,0:T(8,128)S(1)} %shard_map.79.early_ref, bf16[2,512,256]{2,1,0:T(8,128)(2,1)S(1)} %copy-done.3), custom_call_target="tpu_custom_call" | custom-call | flops 1207959552 | bytes 5242880 | tf_op jit(solution)/shard_map/pallas_call | solution.py:255
  (26 shorter events, 8.5 us)
Async XLA Ops:
  0.0 1.1 copy-start
  3.5 7.3 %copy-start.1 = (bf16[2,2,256,192]{3,2,1,0:T(8,128)(2,1)S(1)}, bf16[2,2,256,192]{3,2,1,0:T(8,128)(2,1)}, u32[]{:S(2)}) copy-start(bf16[2,2,256,192]{3,2,1,0:T(8,128)(2,1)} %constant.8.clone.table_ref) | copy-start | bytes 1179652
  7.0 4.7 %collective-permute-start = (f32[1152,256]{1,0:T(8,128)S(1)}, f32[1152,256]{1,0:T(8,128)S(1)}, u32[]{:S(2)}, u32[]{:S(2)}) collective-permute-start(f32[1152,256]{1,0:T(8,128)S(1)} %get-tuple-element.27), channel_id=1, source_target_pairs={{0,1},{1,0},{2,3},{3,2},{4,5},{5,4},{6,7},{7,6},{8,9},{9,8},{10,11... | collective-permute-start | bytes 3538952 | tf_op jit(solution)/shard_map/ppermute | solution.py:307
  7.1 3.7 %collective-permute-start.1 = (f32[576,256]{1,0:T(8,128)S(1)}, f32[576,256]{1,0:T(8,128)S(1)}, u32[]{:S(2)}, u32[]{:S(2)}) collective-permute-start(f32[576,256]{1,0:T(8,128)S(1)} %get-tuple-element.28), channel_id=1, source_target_pairs={{0,1},{1,0},{2,3},{3,2},{4,5},{5,4},{6,7},{7,6},{8,9},{9,8},{10,11... | collective-permute-start | bytes 1769480 | tf_op jit(solution)/shard_map/ppermute | solution.py:307
  14.4 98.9 %copy-start.4 = (bf16[2,512,128]{2,1,0:T(8,128)(2,1)S(1)}, bf16[2,512,128]{2,1,0:T(8,128)(2,1)}, u32[]{:S(2)}) copy-start(bf16[2,512,128]{2,1,0:T(8,128)(2,1)} %constant.10.clone.refs_5_) | copy-start | bytes 786436
  14.4 100.2 %all-to-all-start = ((f32[128,24,128]{2,1,0:T(8,128)}), f32[128,24,128]{2,1,0:T(8,128)S(1)}, u32[]{:S(2)}, u32[]{:S(2)}) async-start(f32[128,24,128]{2,1,0:T(8,128)} %bitcast), calls=%async_computation | async-start | bytes 3145728 | tf_op jit(solution)/shard_map/all_to_all | solution.py:326
  29.5 83.8 %copy-start.2 = (f32[3,256,2,2,128]{4,3,2,1,0:T(2,128)S(1)}, f32[3,256,2,2,128]{4,3,2,1,0:T(2,128)}, u32[]{:S(2)}) copy-start(f32[3,256,2,2,128]{4,3,2,1,0:T(2,128)} %param.9) | copy-start | bytes 4718596
  29.5 40.2 %collective-permute-start.2 = (f32[192,128]{1,0:T(8,128)S(1)}, f32[192,128]{1,0:T(8,128)S(1)}, u32[]{:S(2)}, u32[]{:S(2)}) collective-permute-start(f32[192,128]{1,0:T(8,128)S(1)} %get-tuple-element.30), channel_id=1, source_target_pairs={{8,0},{10,2},{12,4},{14,6},{16,8},{18,10},{20,12},{22,14},{24,16},... | collective-permute-start | bytes 294920 | tf_op jit(solution)/shard_map/ppermute | solution.py:279
  30.5 41.4 %collective-permute-start.3 = (f32[192,128]{1,0:T(8,128)S(1)}, f32[192,128]{1,0:T(8,128)S(1)}, u32[]{:S(2)}, u32[]{:S(2)}) collective-permute-start(f32[192,128]{1,0:T(8,128)S(1)} %get-tuple-element.31), channel_id=1, source_target_pairs={{16,0},{18,2},{20,4},{22,6},{24,8},{26,10},{28,12},{30,14},{32,16}... | collective-permute-start | bytes 294920 | tf_op jit(solution)/shard_map/ppermute | solution.py:279
  34.3 45.6 %collective-permute-start.4 = (f32[192,128]{1,0:T(8,128)S(1)}, f32[192,128]{1,0:T(8,128)S(1)}, u32[]{:S(2)}, u32[]{:S(2)}) collective-permute-start(f32[192,128]{1,0:T(8,128)S(1)} %get-tuple-element.32), channel_id=1, source_target_pairs={{24,0},{26,2},{28,4},{30,6},{32,8},{34,10},{36,12},{38,14},{40,16}... | collective-permute-start | bytes 294920 | tf_op jit(solution)/shard_map/ppermute | solution.py:279
  36.3 48.1 %collective-permute-start.5 = (f32[192,128]{1,0:T(8,128)S(1)}, f32[192,128]{1,0:T(8,128)S(1)}, u32[]{:S(2)}, u32[]{:S(2)}) collective-permute-start(f32[192,128]{1,0:T(8,128)S(1)} %get-tuple-element.33), channel_id=1, source_target_pairs={{32,0},{34,2},{36,4},{38,6},{40,8},{42,10},{44,12},{46,14},{48,16}... | collective-permute-start | bytes 294920 | tf_op jit(solution)/shard_map/ppermute | solution.py:279
  39.4 45.0 %collective-permute-start.6 = (f32[192,128]{1,0:T(8,128)S(1)}, f32[192,128]{1,0:T(8,128)S(1)}, u32[]{:S(2)}, u32[]{:S(2)}) collective-permute-start(f32[192,128]{1,0:T(8,128)S(1)} %get-tuple-element.34), channel_id=1, source_target_pairs={{40,0},{42,2},{44,4},{46,6},{48,8},{50,10},{52,12},{54,14},{56,16}... | collective-permute-start | bytes 294920 | tf_op jit(solution)/shard_map/ppermute | solution.py:279
  69.8 14.6 %collective-permute-start.7 = (f32[192,128]{1,0:T(8,128)S(1)}, f32[192,128]{1,0:T(8,128)S(1)}, u32[]{:S(2)}, u32[]{:S(2)}) collective-permute-start(f32[192,128]{1,0:T(8,128)S(1)} %get-tuple-element.35), channel_id=1, source_target_pairs={{48,0},{50,2},{52,4},{54,6},{56,8},{58,10},{60,12},{62,14},{0,16},... | collective-permute-start | bytes 294920 | tf_op jit(solution)/shard_map/ppermute | solution.py:279
  71.9 12.5 %collective-permute-start.8 = (f32[192,128]{1,0:T(8,128)S(1)}, f32[192,128]{1,0:T(8,128)S(1)}, u32[]{:S(2)}, u32[]{:S(2)}) collective-permute-start(f32[192,128]{1,0:T(8,128)S(1)} %get-tuple-element.36), channel_id=1, source_target_pairs={{56,0},{58,2},{60,4},{62,6},{0,8},{2,10},{4,12},{6,14},{8,16},{10,... | collective-permute-start | bytes 294920 | tf_op jit(solution)/shard_map/ppermute | solution.py:279
  84.6 10.3 %collective-permute-start.9 = (f32[384,128]{1,0:T(8,128)S(1)}, f32[384,128]{1,0:T(8,128)S(1)}, u32[]{:S(2)}, u32[]{:S(2)}) collective-permute-start(f32[384,128]{1,0:T(8,128)S(1)} %get-tuple-element.38), channel_id=1, source_target_pairs={{2,0},{4,2},{6,4},{0,6},{10,8},{12,10},{14,12},{8,14},{18,16},{20,... | collective-permute-start | bytes 589832 | tf_op jit(solution)/shard_map/ppermute | solution.py:279
  87.7 8.8 %collective-permute-start.10 = (f32[384,128]{1,0:T(8,128)S(1)}, f32[384,128]{1,0:T(8,128)S(1)}, u32[]{:S(2)}, u32[]{:S(2)}) collective-permute-start(f32[384,128]{1,0:T(8,128)S(1)} %get-tuple-element.39), channel_id=1, source_target_pairs={{4,0},{6,2},{0,4},{2,6},{12,8},{14,10},{8,12},{10,14},{20,16},{22,... | collective-permute-start | bytes 589832 | tf_op jit(solution)/shard_map/ppermute | solution.py:279
  88.6 10.1 %collective-permute-start.11 = (f32[384,128]{1,0:T(8,128)S(1)}, f32[384,128]{1,0:T(8,128)S(1)}, u32[]{:S(2)}, u32[]{:S(2)}) collective-permute-start(f32[384,128]{1,0:T(8,128)S(1)} %get-tuple-element.40), channel_id=1, source_target_pairs={{6,0},{0,2},{2,4},{4,6},{14,8},{8,10},{10,12},{12,14},{22,16},{16,... | collective-permute-start | bytes 589832 | tf_op jit(solution)/shard_map/ppermute | solution.py:279
  98.7 10.9 %collective-permute-start.12 = (f32[384,128]{1,0:T(8,128)S(1)}, f32[384,128]{1,0:T(8,128)S(1)}, u32[]{:S(2)}, u32[]{:S(2)}) collective-permute-start(f32[384,128]{1,0:T(8,128)S(1)} %get-tuple-element.42), channel_id=1, source_target_pairs={{64,0},{66,2},{68,4},{70,6},{72,8},{74,10},{76,12},{78,14},{80,16}... | collective-permute-start | bytes 589832 | tf_op jit(solution)/shard_map/ppermute | solution.py:279
  101.6 9.3 %collective-permute-start.13 = (f32[384,128]{1,0:T(8,128)S(1)}, f32[384,128]{1,0:T(8,128)S(1)}, u32[]{:S(2)}, u32[]{:S(2)}) collective-permute-start(f32[384,128]{1,0:T(8,128)S(1)} %get-tuple-element.43), channel_id=1, source_target_pairs={{128,0},{130,2},{132,4},{134,6},{136,8},{138,10},{140,12},{142,14}... | collective-permute-start | bytes 589832 | tf_op jit(solution)/shard_map/ppermute | solution.py:279
  102.5 10.9 %collective-permute-start.14 = (f32[384,128]{1,0:T(8,128)S(1)}, f32[384,128]{1,0:T(8,128)S(1)}, u32[]{:S(2)}, u32[]{:S(2)}) collective-permute-start(f32[384,128]{1,0:T(8,128)S(1)} %get-tuple-element.44), channel_id=1, source_target_pairs={{192,0},{194,2},{196,4},{198,6},{200,8},{202,10},{204,12},{206,14}... | collective-permute-start | bytes 589832 | tf_op jit(solution)/shard_map/ppermute | solution.py:279
  114.6 1.0 copy-start.3

commit v2 on v1

--- a/solution.py
+++ b/solution.py
@@ -88,32 +88,47 @@
     return y, z, x
 
 
-def x_kernel(planes, v_hbm, w_hbm, table_hbm, _, keep_ref, send_ref, v_ref, w_ref, table_ref, sems):
-    rows = v_ref.shape[2]
-    half = keep_ref.shape[-1]
-    copies = []
-    for i, plane in enumerate(planes):
-        for c in range(3):
-            copies.append(pltpu.make_async_copy(v_hbm.at[c, plane], v_ref.at[i, c], sems.at[i * 6 + c]))
-            copies.append(pltpu.make_async_copy(w_hbm.at[c, plane], w_ref.at[i, c], sems.at[i * 6 + 3 + c]))
-        if i == 0:
-            copies.append(pltpu.make_async_copy(table_hbm, table_ref, sems.at[len(planes) * 6]))
-    for copy in copies:
-        copy.start()
-    mine = lax.axis_index("slab") == 0
-    deep = table_ref.shape[0] // 2
-    for i in range(len(planes)):
-        for copy in copies[:7] if i == 0 else copies[7 + (i - 1) * 6 : 7 + i * 6]:
+def cross_kernel(v_hbm, w_hbm, *refs):
+    outs, (v_ref, w_ref, sems) = refs[:-3], refs[-3:]
+    rows, cells = v_ref.shape[2:]
+    copies = [
+        [
+            copy
+            for c in range(3)
+            for copy in (
+                pltpu.make_async_copy(v_hbm.at[c, plane], v_ref.at[plane, c], sems.at[plane * 6 + c]),
+                pltpu.make_async_copy(w_hbm.at[c, plane], w_ref.at[plane, c], sems.at[plane * 6 + 3 + c]),
+            )
+        ]
+        for plane in range(len(outs))
+    ]
+    for group in copies:
+        for copy in group:
+            copy.start()
+    for plane, out_ref in enumerate(outs):
+        for copy in copies[plane]:
             copy.wait()
-        table = jnp.concatenate([table_ref[:deep], table_ref[:deep], table_ref[deep:]], axis=0)
         for c in range(3):
             a, b = (c + 1) % 3, (c + 2) % 3
-            high, low = split(v_ref[i, a] * w_ref[i, b] - v_ref[i, b] * w_ref[i, a])
-            out = product(jnp.concatenate([high, low, high], axis=1), table)
-            first, second = out[:, :half], out[:, half:]
-            here = slice((i * 3 + c) * rows, (i * 3 + c + 1) * rows)
-            keep_ref[here] = jnp.where(mine, first, second)
-            send_ref[here] = jnp.where(mine, second, first)
+            high, low = split(v_ref[plane, a] * w_ref[plane, b] - v_ref[plane, b] * w_ref[plane, a])
+            out_ref[c * rows : (c + 1) * rows, :cells] = high
+            out_ref[c * rows : (c + 1) * rows, cells:] = low
+
+
+def x_kernel(*refs):
+    planes, (table_ref, keep_ref, send_ref) = refs[:-3], refs[-3:]
+    cells = planes[0].shape[1] // 2
+    rows = planes[0].shape[0]
+    half = keep_ref.shape[-1]
+    mine = lax.axis_index("slab") == 0
+    table = jnp.concatenate([table_ref[:cells], table_ref[:cells], table_ref[cells:]], axis=0)
+    for i, ref in enumerate(planes):
+        both = ref[...]
+        out = product(jnp.concatenate([both, both[:, :cells]], axis=1), table)
+        first, second = out[:, :half], out[:, half:]
+        here = slice(i * rows, (i + 1) * rows)
+        keep_ref[here] = jnp.where(mine, first, second)
+        send_ref[here] = jnp.where(mine, second, first)
 
 
 def y_blocks(keep_ref, got_ref, table_ref, rows):
@@ -150,35 +165,26 @@
             outs[shift][k * NXY : (k + 1) * NXY] = all_ref[pl.ds(pl.multiple_of(k * dests + to * NXY, NXY), NXY), :]
 
 
-def turn_x_kernel(*refs):
+def turn_kernel(*refs):
     gots, outs, all_ref = refs[:NZ], refs[NZ:-1], refs[-1]
-    _, z, x = place()
+    y, z, x = place()
     size = gots[0].shape[0]
     for shift in range(NZ):
         source = lax.rem(z + shift, NZ)
         all_ref[pl.ds(pl.multiple_of(source * size, size), size), :] = gots[shift][...]
-    for shift in range(NX):
-        to = lax.rem(x - shift + NX, NX)
-        outs[shift][...] = all_ref[pl.ds(to, all_ref.shape[0] // NX, NX), :]
-
-
-def turn_y_kernel(*refs):
-    gots, outs = refs[:NX], refs[NX:]
-    y, _, x = place()
-    size = gots[0].shape[0] // NY
-    for dx in range(NX):
-        at = pl.multiple_of(lax.rem(x + dx, NX) * size, size)
-        for dy in range(NY):
-            to = lax.rem(y - dy + NY, NY)
-            outs[dy][pl.ds(at, size), :] = gots[dx][pl.ds(to, size, NY), :]
-
-
-def wave_numbers(keep, lanes):
+    count = all_ref.shape[0] // NXY
+    for dy in range(NY):
+        for dx in range(NX):
+            to = lax.rem(y - dy + NY, NY) * NX + lax.rem(x - dx + NX, NX)
+            outs[dy * NX + dx][...] = all_ref[pl.ds(to, count, NXY), :]
+
+
+def wave_numbers(keep, lanes, first, count):
     group = lax.axis_index("section") * lax.axis_size("pen") + lax.axis_index("pen")
     limit = -(keep // 2)
     visc = 0.5 / (keep // 2) ** 2
-    row = lax.broadcasted_iota(jnp.int32, (keep, lanes), 0)
-    col = lax.broadcasted_iota(jnp.int32, (keep, lanes), 1) + lax.axis_index("slab") * lanes
+    row = lax.broadcasted_iota(jnp.int32, (count, lanes), 0) + first
+    col = lax.broadcasted_iota(jnp.int32, (count, lanes), 1) + lax.axis_index("slab") * lanes
     kz = jnp.where(row < keep // 2, row, row - keep)
     kx = jnp.where(col < keep // 2, col, col - keep)
     for parity in range(2):
@@ -201,17 +207,18 @@
 
 
 def early_kernel(keep, *refs):
-    gots, (modes_ref, table_ref, out_ref, all_ref) = refs[:NY], refs[NY:]
-    y, _, _ = place()
+    gots, (modes_ref, table_ref, out_ref, all_ref) = refs[:NXY], refs[NXY:]
+    y, _, x = place()
     lanes = out_ref.shape[1]
-    kinds = gots[0].shape[0] // (NX * NZ)
-    sources = NY * NX * NZ
+    kinds = gots[0].shape[0] // NZ
+    sources = NXY * NZ
     for dy in range(NY):
-        source = lax.rem(y + dy, NY) * (NX * NZ)
-        for k in range(kinds):
-            at = pl.multiple_of(k * sources + source, NX * NZ)
-            all_ref[pl.ds(at, NX * NZ), :] = gots[dy][pl.ds(k, NX * NZ, kinds), :]
-    for parity, waves, mask, inverse, damp in wave_numbers(keep, lanes):
+        for dx in range(NX):
+            source = lax.rem(y + dy, NY) * NX + lax.rem(x + dx, NX)
+            for k in range(kinds):
+                at = pl.multiple_of(k * sources + source * NZ, NZ)
+                all_ref[pl.ds(at, NZ), :] = gots[dy * NX + dx][pl.ds(k, NZ, kinds), :]
+    for parity, waves, mask, inverse, damp in wave_numbers(keep, lanes, 0, keep):
         sums = []
         for c in range(3):
             base = c * 4 + parity * 2
@@ -223,15 +230,11 @@
                 out_ref[where, :] = value - damp * modes_ref[where, :]
 
 
-def z_kernel(planes, keep, x_ref, early_ref, table_hbm, out_ref, table_ref, sem):
-    copy = pltpu.make_async_copy(table_hbm, table_ref, sem)
-    copy.start()
+def z_kernel(planes, keep, x_ref, early_ref, table_ref, out_hbm, sums_ref, out_ref, sems):
     lanes = x_ref.shape[1]
     per = 3 * planes * 4
     sources = x_ref.shape[0] // per
-    copy.wait()
-    for parity, waves, mask, inverse, _ in wave_numbers(keep, lanes):
-        sums = []
+    for parity in range(2):
         for c in range(3):
             columns = [
                 jnp.concatenate(
@@ -239,23 +242,38 @@
                 )
                 for q in range(2)
             ]
-            sums.append(z_sums(keep, lanes, table_ref, jnp.concatenate(columns, axis=1)))
-        for q in range(2):
-            for c, value in enumerate(projected([s[q] for s in sums], waves, mask, inverse)):
-                where = pl.ds(c * keep * 4 + parity * 2 + q, keep, 4)
-                out_ref[where, :] = value + early_ref[where, :]
-
-
-def call(kernel, outs, flops=0, scratch=(), spaces=None, limit=40 << 20):
+            pair = z_sums(keep, lanes, table_ref, jnp.concatenate(columns, axis=1))
+            for q in range(2):
+                sums_ref[parity, q, c] = pair[q]
+    count = sems.shape[0] // 3
+    part = keep // count
+    copies = []
+    for h in range(count):
+        here = slice(h * part, (h + 1) * part)
+        for parity, waves, mask, inverse, _ in wave_numbers(keep, lanes, h * part, part):
+            for q in range(2):
+                values = projected([sums_ref[parity, q, c, here] for c in range(3)], waves, mask, inverse)
+                for c, value in enumerate(values):
+                    where = pl.ds((c * keep + h * part) * 4 + parity * 2 + q, part, 4)
+                    out_ref[where, :] = value + early_ref[where, :]
+        for c in range(3):
+            rows = pl.ds((c * keep + h * part) * 4, part * 4)
+            copies.append(pltpu.make_async_copy(out_ref.at[rows], out_hbm.at[rows], sems.at[h * 3 + c]))
+            copies[-1].start()
+    for copy in copies:
+        copy.wait()
+
+
+def call(kernel, outs, flops=0, scratch=(), space=VMEM, out_space=VMEM, limit=40 << 20, kind=jnp.float32):
     def run(*args):
         size = sum(a.size * a.dtype.itemsize for a in args) + sum(4 * math.prod(o) for o in outs)
-        shapes = [jax.ShapeDtypeStruct(o, jnp.float32) for o in outs]
-        specs = [pl.BlockSpec(memory_space=VMEM)] * len(outs)
+        shapes = [jax.ShapeDtypeStruct(o, kind) for o in outs]
+        specs = [pl.BlockSpec(memory_space=out_space)] * len(outs)
         single = len(outs) == 1
         return pl.pallas_call(
             kernel,
             out_shape=shapes[0] if single else shapes,
-            in_specs=[pl.BlockSpec(memory_space=s) for s in spaces or [VMEM] * len(args)],
+            in_specs=[pl.BlockSpec(memory_space=space)] * len(args),
             out_specs=specs[0] if single else specs,
             scratch_shapes=list(scratch),
             cost_estimate=pl.CostEstimate(flops=flops, bytes_accessed=size, transcendentals=0),
@@ -286,23 +304,20 @@
     order = z_major_groups()
     table_y = jnp.asarray(y_table(cells, keep, order))
     table_x = jnp.asarray(x_table(cells, keep))
+    crosses = call(
+        cross_kernel,
+        [(3 * rows_y, 2 * cells)] * planes,
+        6 * planes * 3 * rows_y * cells,
+        [VMEM((planes, 3, rows_y, cells), jnp.float32)] * 2 + [pltpu.SemaphoreType.DMA((6 * planes,))],
+        pltpu.HBM,
+        limit=50 << 20,
+        kind=jnp.bfloat16,
+    )(velocity, vorticity)
     keeps, gots = [], []
-    for held in ([0], list(range(1, planes))):
+    for held in (crosses[:1], crosses[1:]):
         n = len(held)
-        run = call(
-            functools.partial(x_kernel, held),
-            [(3 * n * rows_y, keep)] * 2,
-            2 * 9 * n * rows_y * cells * 2 * keep,
-            [
-                VMEM((n, 3, rows_y, cells), jnp.float32),
-                VMEM((n, 3, rows_y, cells), jnp.float32),
-                VMEM(table_x.shape, jnp.bfloat16),
-                pltpu.SemaphoreType.DMA((6 * n + 1,)),
-            ],
-            [pltpu.HBM] * 4,
-            50 << 20,
-        )
-        mine, other = run(velocity, vorticity, table_x, keeps[0] if keeps else vorticity)
+        run = call(x_kernel, [(3 * n * rows_y, keep)] * 2, 2 * 9 * n * rows_y * cells * 2 * keep)
+        mine, other = run(*held, table_x)
         keeps.append(mine)
         gots.append(lax.ppermute(other, "slab", [(0, 1), (1, 0)]))
     flops = 2 * 3 * 2 * keep * 3 * rows_y * keep
@@ -318,20 +333,13 @@
         arrived.append(from_shift(sent[s], 0, s, 0))
     per = (planes - 1) * kinds
     packed = call(
-        functools.partial(y_pack_kernel, rows_y),
-        [(dests * per, lanes)],
-        flops * (planes - 1),
-        spaces=[VMEM] * 3 + [pl.ANY],
+        functools.partial(y_pack_kernel, rows_y), [(dests * per, lanes)], flops * (planes - 1)
     )(keeps[1], gots[1], table_y, sent[0])
     late = lax.all_to_all(
         packed.reshape(dests, per, lanes), GROUP, 0, 0, axis_index_groups=[order.tolist()], tiled=True
     )
-    turned = call(
-        turn_x_kernel, [(NZ * kinds * NY, lanes)] * NX, 0, [VMEM((NZ * kinds * NXY, lanes), jnp.float32)]
-    )(*arrived)
-    turned = [turned[0]] + [from_shift(turned[d], 0, 0, d) for d in range(1, NX)]
-    turned = call(turn_y_kernel, [(NX * NZ * kinds, lanes)] * NY)(*turned)
-    spread = [turned[0]] + [from_shift(turned[d], d, 0, 0) for d in range(1, NY)]
+    turned = call(turn_kernel, [(NZ * kinds, lanes)] * NXY, 0, [VMEM((NZ * kinds * NXY, lanes), jnp.float32)])(*arrived)
+    spread = [turned[0]] + [from_shift(turned[d], d // NX, 0, d % NX) for d in range(1, NXY)]
     early = call(
         functools.partial(early_kernel, keep),
         [(3 * keep * 4, lanes)],
@@ -348,9 +356,12 @@
         functools.partial(z_kernel, planes - 1, keep),
         [(3 * keep * 4, lanes)],
         2 * 6 * 2 * keep * 3 * (planes - 1) * dests * keep,
-        [VMEM(table_z.shape, jnp.bfloat16), pltpu.SemaphoreType.DMA],
-        [VMEM, VMEM, pltpu.HBM],
-        40 << 20,
+        [
+            VMEM((2, 2, 3, keep, lanes), jnp.float32),
+            VMEM((3 * keep * 4, lanes), jnp.float32),
+            pltpu.SemaphoreType.DMA((6,)),
+        ],
+        out_space=pltpu.HBM,
     )(late.reshape(dests * per, lanes), early, table_z)
     return out.reshape(3, keep, rows_ky, 2, lanes)
 

time: 120 us -> 126 us (1.050)
  starting transfers between devices: 43.6 us -> 63.2 us
  waiting for transfers between devices: 58.8 us -> 45.9 us
    ppermute x13 -> x22, starting transfers between devices: 27.9 us -> 47.4 us  [from_shift(): return lax.ppermute(value, GROUP, pairs)]
    ppermute x13 -> x22, waiting for transfers between devices: 55.6 us -> 43.7 us  [from_shift(): return lax.ppermute(value, GROUP, pairs)]
  transfers between devices with their start and end apart: 16 -> 25, of which waited for: 11 -> 8; matrix products, arithmetic and copies ran while one was open for 0% -> 0% of each run, Pallas kernels for 2% -> 3%
where the time goes in v2:
time: 126 us
  starting transfers between devices  63.2 us (50%)
  waiting for transfers between devices  45.9 us (36%)
  Pallas kernels  13.7 us (11%)
  local copies, waits for them, and re-layouts  2.46 us (2%)
    ppermute x22, starting transfers between devices, from_shift(): return lax.ppermute(value, GROUP, pairs)  47.4 us
    ppermute x22, waiting for transfers between devices, from_shift(): return lax.ppermute(value, GROUP, pairs)  43.7 us
    all_to_all x1, starting transfers between devices, per_device(): lax.all_to_all(packed.reshape(dests, per, lanes), GROUP, 0, 0, axis_index...  15.1 us
    pallas_call x8, Pallas kernels, run(): pl.pallas_call(kernel, out_shape=shapes[0] if single else shapes, in_spec...  13.7 us
  transfers between devices with their start and end apart: 25, of which 8 were waited for; matrix products, arithmetic and copies ran while one was open for 0% of the time, Pallas kernels for 3%

profile of v2, /device:TPU:32, one launch (start us, length us, event | category | flops | bytes accessed | tf_op | source)
XLA Modules:
  0.0 125.6 jit_solution(7796628261649125132)
XLA Ops:
  0.0 2.9 %shard_map.73 = (bf16[576,768]{1,0:T(8,128)(2,1)S(1)}, bf16[576,768]{1,0:T(8,128)(2,1)S(1)}, bf16[576,768]{1,0:T(8,128)(2,1)S(1)}) custom-call(f32[3,3,192,384]{3,2,1,0:T(8,128)} %v_hbm.1, f32[3,3,192,384]{3,2,1,0:T(8,128)} %w_hbm.1), custom_call_target="tpu_custom_call" | custom-call | flops 3981312 | bytes 10616832 | tf_op jit(solution)/shard_map/pallas_call | solution.py:273
  6.3 2.2 %collective-permute-done.1.got_ref = f32[576,256]{1,0:T(8,128)S(1)} collective-permute-done((f32[576,256]{1,0:T(8,128)S(1)}, f32[576,256]{1,0:T(8,128)S(1)}, u32[]{:S(2)}, u32[]{:S(2)}) %collective-permute-start.1) | collective-permute-done | bytes 589856 | tf_op jit(solution)/shard_map/ppermute | solution.py:322
  9.3 2.7 %shard_map.77 = f32[3072,128]{1,0:T(8,128)} custom-call(f32[1152,256]{1,0:T(8,128)S(1)} %get-tuple-element.38.keep_ref, f32[1152,256]{1,0:T(8,128)S(1)} %collective-permute-done.got_ref, bf16[2,2,256,192]{3,2,1,0:T(8,128)(2,1)S(1)} %copy-done, f32[192,128]{1,0:T(8,128)S(1)} %get-tuple-element.43._.refs_0_), custom_call_target="tpu_custom_call" | custom-call | flops 905969664 | bytes 4423680 | tf_op jit(solution)/shard_map/pallas_call | solution.py:273
  12.0 15.1 %all-to-all-start = ((f32[128,24,128]{2,1,0:T(8,128)}), f32[128,24,128]{2,1,0:T(8,128)S(1)}, u32[]{:S(2)}, u32[]{:S(2)}) async-start(f32[128,24,128]{2,1,0:T(8,128)} %bitcast), calls=%async_computation | async-start | bytes 3145728 | tf_op jit(solution)/shard_map/all_to_all | solution.py:338
  28.1 3.8 %collective-permute-start.3 = (f32[192,128]{1,0:T(8,128)S(1)}, f32[192,128]{1,0:T(8,128)S(1)}, u32[]{:S(2)}, u32[]{:S(2)}) collective-permute-start(f32[192,128]{1,0:T(8,128)S(1)} %get-tuple-element.45), channel_id=1, source_target_pairs={{16,0},{18,2},{20,4},{22,6},{24,8},{26,10},{28,12},{30,14},{32,16}... | collective-permute-start | bytes 294920 | tf_op jit(solution)/shard_map/ppermute | solution.py:297
  31.9 2.0 %collective-permute-start.4 = (f32[192,128]{1,0:T(8,128)S(1)}, f32[192,128]{1,0:T(8,128)S(1)}, u32[]{:S(2)}, u32[]{:S(2)}) collective-permute-start(f32[192,128]{1,0:T(8,128)S(1)} %get-tuple-element.46), channel_id=1, source_target_pairs={{24,0},{26,2},{28,4},{30,6},{32,8},{34,10},{36,12},{38,14},{40,16}... | collective-permute-start | bytes 294920 | tf_op jit(solution)/shard_map/ppermute | solution.py:297
  33.9 3.1 %collective-permute-start.5 = (f32[192,128]{1,0:T(8,128)S(1)}, f32[192,128]{1,0:T(8,128)S(1)}, u32[]{:S(2)}, u32[]{:S(2)}) collective-permute-start(f32[192,128]{1,0:T(8,128)S(1)} %get-tuple-element.47), channel_id=1, source_target_pairs={{32,0},{34,2},{36,4},{38,6},{40,8},{42,10},{44,12},{46,14},{48,16}... | collective-permute-start | bytes 294920 | tf_op jit(solution)/shard_map/ppermute | solution.py:297
  37.0 1.8 %collective-permute-start.6 = (f32[192,128]{1,0:T(8,128)S(1)}, f32[192,128]{1,0:T(8,128)S(1)}, u32[]{:S(2)}, u32[]{:S(2)}) collective-permute-start(f32[192,128]{1,0:T(8,128)S(1)} %get-tuple-element.48), channel_id=1, source_target_pairs={{40,0},{42,2},{44,4},{46,6},{48,8},{50,10},{52,12},{54,14},{56,16}... | collective-permute-start | bytes 294920 | tf_op jit(solution)/shard_map/ppermute | solution.py:297
  38.8 28.5 %collective-permute-done.2.refs_1_ = f32[192,128]{1,0:T(8,128)S(1)} collective-permute-done((f32[192,128]{1,0:T(8,128)S(1)}, f32[192,128]{1,0:T(8,128)S(1)}, u32[]{:S(2)}, u32[]{:S(2)}) %collective-permute-start.2) | collective-permute-done | bytes 98336 | tf_op jit(solution)/shard_map/ppermute | solution.py:297
  67.4 1.8 %collective-permute-start.7 = (f32[192,128]{1,0:T(8,128)S(1)}, f32[192,128]{1,0:T(8,128)S(1)}, u32[]{:S(2)}, u32[]{:S(2)}) collective-permute-start(f32[192,128]{1,0:T(8,128)S(1)} %get-tuple-element.49), channel_id=1, source_target_pairs={{48,0},{50,2},{52,4},{54,6},{56,8},{58,10},{60,12},{62,14},{0,16},... | collective-permute-start | bytes 294920 | tf_op jit(solution)/shard_map/ppermute | solution.py:297
  69.6 5.1 %collective-permute-start.8 = (f32[192,128]{1,0:T(8,128)S(1)}, f32[192,128]{1,0:T(8,128)S(1)}, u32[]{:S(2)}, u32[]{:S(2)}) collective-permute-start(f32[192,128]{1,0:T(8,128)S(1)} %get-tuple-element.50), channel_id=1, source_target_pairs={{56,0},{58,2},{60,4},{62,6},{0,8},{2,10},{4,12},{6,14},{8,16},{10,... | collective-permute-start | bytes 294920 | tf_op jit(solution)/shard_map/ppermute | solution.py:297
  74.6 2.9 %collective-permute-done.4.refs_3_ = f32[192,128]{1,0:T(8,128)S(1)} collective-permute-done((f32[192,128]{1,0:T(8,128)S(1)}, f32[192,128]{1,0:T(8,128)S(1)}, u32[]{:S(2)}, u32[]{:S(2)}) %collective-permute-start.4) | collective-permute-done | bytes 98336 | tf_op jit(solution)/shard_map/ppermute | solution.py:297
  77.5 4.5 %collective-permute-done.5.refs_4_ = f32[192,128]{1,0:T(8,128)S(1)} collective-permute-done((f32[192,128]{1,0:T(8,128)S(1)}, f32[192,128]{1,0:T(8,128)S(1)}, u32[]{:S(2)}, u32[]{:S(2)}) %collective-permute-start.5) | collective-permute-done | bytes 98336 | tf_op jit(solution)/shard_map/ppermute | solution.py:297
  82.5 3.1 %collective-permute-start.9 = (f32[96,128]{1,0:T(8,128)S(1)}, f32[96,128]{1,0:T(8,128)S(1)}, u32[]{:S(2)}, u32[]{:S(2)}) collective-permute-start(f32[96,128]{1,0:T(8,128)S(1)} %get-tuple-element.52), channel_id=1, source_target_pairs={{2,0},{4,2},{6,4},{0,6},{10,8},{12,10},{14,12},{8,14},{18,16},{20,... | collective-permute-start | bytes 147464 | tf_op jit(solution)/shard_map/ppermute | solution.py:297
  87.3 2.8 %collective-permute-start.12 = (f32[96,128]{1,0:T(8,128)S(1)}, f32[96,128]{1,0:T(8,128)S(1)}, u32[]{:S(2)}, u32[]{:S(2)}) collective-permute-start(f32[96,128]{1,0:T(8,128)S(1)} %get-tuple-element.55), channel_id=1, source_target_pairs={{64,0},{66,2},{68,4},{70,6},{72,8},{74,10},{76,12},{78,14},{80,16}... | collective-permute-start | bytes 147464 | tf_op jit(solution)/shard_map/ppermute | solution.py:297
  90.1 2.6 %collective-permute-start.13 = (f32[96,128]{1,0:T(8,128)S(1)}, f32[96,128]{1,0:T(8,128)S(1)}, u32[]{:S(2)}, u32[]{:S(2)}) collective-permute-start(f32[96,128]{1,0:T(8,128)S(1)} %get-tuple-element.56), channel_id=1, source_target_pairs={{66,0},{68,2},{70,4},{64,6},{74,8},{76,10},{78,12},{72,14},{82,16}... | collective-permute-start | bytes 147464 | tf_op jit(solution)/shard_map/ppermute | solution.py:297
  94.2 2.8 %collective-permute-start.16 = (f32[96,128]{1,0:T(8,128)S(1)}, f32[96,128]{1,0:T(8,128)S(1)}, u32[]{:S(2)}, u32[]{:S(2)}) collective-permute-start(f32[96,128]{1,0:T(8,128)S(1)} %get-tuple-element.59), channel_id=1, source_target_pairs={{128,0},{130,2},{132,4},{134,6},{136,8},{138,10},{140,12},{142,14}... | collective-permute-start | bytes 147464 | tf_op jit(solution)/shard_map/ppermute | solution.py:297
  97.0 3.4 %collective-permute-start.17 = (f32[96,128]{1,0:T(8,128)S(1)}, f32[96,128]{1,0:T(8,128)S(1)}, u32[]{:S(2)}, u32[]{:S(2)}) collective-permute-start(f32[96,128]{1,0:T(8,128)S(1)} %get-tuple-element.60), channel_id=1, source_target_pairs={{130,0},{132,2},{134,4},{128,6},{138,8},{140,10},{142,12},{136,14}... | collective-permute-start | bytes 147464 | tf_op jit(solution)/shard_map/ppermute | solution.py:297
  100.4 3.3 %collective-permute-start.18 = (f32[96,128]{1,0:T(8,128)S(1)}, f32[96,128]{1,0:T(8,128)S(1)}, u32[]{:S(2)}, u32[]{:S(2)}) collective-permute-start(f32[96,128]{1,0:T(8,128)S(1)} %get-tuple-element.61), channel_id=1, source_target_pairs={{132,0},{134,2},{128,4},{130,6},{140,8},{142,10},{136,12},{138,14}... | collective-permute-start | bytes 147464 | tf_op jit(solution)/shard_map/ppermute | solution.py:297
  104.8 4.5 %collective-permute-start.21 = (f32[96,128]{1,0:T(8,128)S(1)}, f32[96,128]{1,0:T(8,128)S(1)}, u32[]{:S(2)}, u32[]{:S(2)}) collective-permute-start(f32[96,128]{1,0:T(8,128)S(1)} %get-tuple-element.64), channel_id=1, source_target_pairs={{194,0},{196,2},{198,4},{192,6},{202,8},{204,10},{206,12},{200,14}... | collective-permute-start | bytes 147464 | tf_op jit(solution)/shard_map/ppermute | solution.py:297
  109.3 2.1 %collective-permute-start.22 = (f32[96,128]{1,0:T(8,128)S(1)}, f32[96,128]{1,0:T(8,128)S(1)}, u32[]{:S(2)}, u32[]{:S(2)}) collective-permute-start(f32[96,128]{1,0:T(8,128)S(1)} %get-tuple-element.65), channel_id=1, source_target_pairs={{196,0},{198,2},{192,4},{194,6},{204,8},{206,10},{200,12},{202,14}... | collective-permute-start | bytes 147464 | tf_op jit(solution)/shard_map/ppermute | solution.py:297
  112.1 4.9 %collective-permute-done.22.refs_14_ = f32[96,128]{1,0:T(8,128)S(1)} collective-permute-done((f32[96,128]{1,0:T(8,128)S(1)}, f32[96,128]{1,0:T(8,128)S(1)}, u32[]{:S(2)}, u32[]{:S(2)}) %collective-permute-start.22) | collective-permute-done | bytes 49184 | tf_op jit(solution)/shard_map/ppermute | solution.py:297
  117.0 1.8 %collective-permute-done.23.refs_15_ = f32[96,128]{1,0:T(8,128)S(1)} collective-permute-done((f32[96,128]{1,0:T(8,128)S(1)}, f32[96,128]{1,0:T(8,128)S(1)}, u32[]{:S(2)}, u32[]{:S(2)}) %collective-permute-start.23) | collective-permute-done | bytes 49184 | tf_op jit(solution)/shard_map/ppermute | solution.py:297
  122.5 2.9 %shard_map.80 = f32[3072,128]{1,0:T(8,128)} custom-call(f32[3072,128]{1,0:T(8,128)S(1)} %bitcast.4, f32[3072,128]{1,0:T(8,128)S(1)} %shard_map.79.early_ref, bf16[2,512,256]{2,1,0:T(8,128)(2,1)S(1)} %copy-done.2), custom_call_target="tpu_custom_call" | custom-call | flops 1207959552 | bytes 5242880 | tf_op jit(solution)/shard_map/pallas_call | solution.py:273
  (44 shorter events, 14.7 us)
Async XLA Ops:
  4.6 4.7 %collective-permute-start = (f32[1152,256]{1,0:T(8,128)S(1)}, f32[1152,256]{1,0:T(8,128)S(1)}, u32[]{:S(2)}, u32[]{:S(2)}) collective-permute-start(f32[1152,256]{1,0:T(8,128)S(1)} %get-tuple-element.39), channel_id=1, source_target_pairs={{0,1},{1,0},{2,3},{3,2},{4,5},{5,4},{6,7},{7,6},{8,9},{9,8},{10,11... | collective-permute-start | bytes 3538952 | tf_op jit(solution)/shard_map/ppermute | solution.py:322
  12.0 109.5 %all-to-all-start = ((f32[128,24,128]{2,1,0:T(8,128)}), f32[128,24,128]{2,1,0:T(8,128)S(1)}, u32[]{:S(2)}, u32[]{:S(2)}) async-start(f32[128,24,128]{2,1,0:T(8,128)} %bitcast), calls=%async_computation | async-start | bytes 3145728 | tf_op jit(solution)/shard_map/all_to_all | solution.py:338
  27.1 40.2 %collective-permute-start.2 = (f32[192,128]{1,0:T(8,128)S(1)}, f32[192,128]{1,0:T(8,128)S(1)}, u32[]{:S(2)}, u32[]{:S(2)}) collective-permute-start(f32[192,128]{1,0:T(8,128)S(1)} %get-tuple-element.44), channel_id=1, source_target_pairs={{8,0},{10,2},{12,4},{14,6},{16,8},{18,10},{20,12},{22,14},{24,16},... | collective-permute-start | bytes 294920 | tf_op jit(solution)/shard_map/ppermute | solution.py:297
  28.1 41.5 %collective-permute-start.3 = (f32[192,128]{1,0:T(8,128)S(1)}, f32[192,128]{1,0:T(8,128)S(1)}, u32[]{:S(2)}, u32[]{:S(2)}) collective-permute-start(f32[192,128]{1,0:T(8,128)S(1)} %get-tuple-element.45), channel_id=1, source_target_pairs={{16,0},{18,2},{20,4},{22,6},{24,8},{26,10},{28,12},{30,14},{32,16}... | collective-permute-start | bytes 294920 | tf_op jit(solution)/shard_map/ppermute | solution.py:297
  31.9 45.7 %collective-permute-start.4 = (f32[192,128]{1,0:T(8,128)S(1)}, f32[192,128]{1,0:T(8,128)S(1)}, u32[]{:S(2)}, u32[]{:S(2)}) collective-permute-start(f32[192,128]{1,0:T(8,128)S(1)} %get-tuple-element.46), channel_id=1, source_target_pairs={{24,0},{26,2},{28,4},{30,6},{32,8},{34,10},{36,12},{38,14},{40,16}... | collective-permute-start | bytes 294920 | tf_op jit(solution)/shard_map/ppermute | solution.py:297
  33.9 48.1 %collective-permute-start.5 = (f32[192,128]{1,0:T(8,128)S(1)}, f32[192,128]{1,0:T(8,128)S(1)}, u32[]{:S(2)}, u32[]{:S(2)}) collective-permute-start(f32[192,128]{1,0:T(8,128)S(1)} %get-tuple-element.47), channel_id=1, source_target_pairs={{32,0},{34,2},{36,4},{38,6},{40,8},{42,10},{44,12},{46,14},{48,16}... | collective-permute-start | bytes 294920 | tf_op jit(solution)/shard_map/ppermute | solution.py:297
  37.0 45.0 %collective-permute-start.6 = (f32[192,128]{1,0:T(8,128)S(1)}, f32[192,128]{1,0:T(8,128)S(1)}, u32[]{:S(2)}, u32[]{:S(2)}) collective-permute-start(f32[192,128]{1,0:T(8,128)S(1)} %get-tuple-element.48), channel_id=1, source_target_pairs={{40,0},{42,2},{44,4},{46,6},{48,8},{50,10},{52,12},{54,14},{56,16}... | collective-permute-start | bytes 294920 | tf_op jit(solution)/shard_map/ppermute | solution.py:297
  67.4 14.7 %collective-permute-start.7 = (f32[192,128]{1,0:T(8,128)S(1)}, f32[192,128]{1,0:T(8,128)S(1)}, u32[]{:S(2)}, u32[]{:S(2)}) collective-permute-start(f32[192,128]{1,0:T(8,128)S(1)} %get-tuple-element.49), channel_id=1, source_target_pairs={{48,0},{50,2},{52,4},{54,6},{56,8},{58,10},{60,12},{62,14},{0,16},... | collective-permute-start | bytes 294920 | tf_op jit(solution)/shard_map/ppermute | solution.py:297
  69.6 12.5 %collective-permute-start.8 = (f32[192,128]{1,0:T(8,128)S(1)}, f32[192,128]{1,0:T(8,128)S(1)}, u32[]{:S(2)}, u32[]{:S(2)}) collective-permute-start(f32[192,128]{1,0:T(8,128)S(1)} %get-tuple-element.50), channel_id=1, source_target_pairs={{56,0},{58,2},{60,4},{62,6},{0,8},{2,10},{4,12},{6,14},{8,16},{10,... | collective-permute-start | bytes 294920 | tf_op jit(solution)/shard_map/ppermute | solution.py:297
  82.5 10.2 %collective-permute-start.9 = (f32[96,128]{1,0:T(8,128)S(1)}, f32[96,128]{1,0:T(8,128)S(1)}, u32[]{:S(2)}, u32[]{:S(2)}) collective-permute-start(f32[96,128]{1,0:T(8,128)S(1)} %get-tuple-element.52), channel_id=1, source_target_pairs={{2,0},{4,2},{6,4},{0,6},{10,8},{12,10},{14,12},{8,14},{18,16},{20,... | collective-permute-start | bytes 147464 | tf_op jit(solution)/shard_map/ppermute | solution.py:297
  85.6 8.6 %collective-permute-start.10 = (f32[96,128]{1,0:T(8,128)S(1)}, f32[96,128]{1,0:T(8,128)S(1)}, u32[]{:S(2)}, u32[]{:S(2)}) collective-permute-start(f32[96,128]{1,0:T(8,128)S(1)} %get-tuple-element.53), channel_id=1, source_target_pairs={{4,0},{6,2},{0,4},{2,6},{12,8},{14,10},{8,12},{10,14},{20,16},{22,... | collective-permute-start | bytes 147464 | tf_op jit(solution)/shard_map/ppermute | solution.py:297
  86.5 7.8 %collective-permute-start.11 = (f32[96,128]{1,0:T(8,128)S(1)}, f32[96,128]{1,0:T(8,128)S(1)}, u32[]{:S(2)}, u32[]{:S(2)}) collective-permute-start(f32[96,128]{1,0:T(8,128)S(1)} %get-tuple-element.54), channel_id=1, source_target_pairs={{6,0},{0,2},{2,4},{4,6},{14,8},{8,10},{10,12},{12,14},{22,16},{16,... | collective-permute-start | bytes 147464 | tf_op jit(solution)/shard_map/ppermute | solution.py:297
  87.3 9.7 %collective-permute-start.12 = (f32[96,128]{1,0:T(8,128)S(1)}, f32[96,128]{1,0:T(8,128)S(1)}, u32[]{:S(2)}, u32[]{:S(2)}) collective-permute-start(f32[96,128]{1,0:T(8,128)S(1)} %get-tuple-element.55), channel_id=1, source_target_pairs={{64,0},{66,2},{68,4},{70,6},{72,8},{74,10},{76,12},{78,14},{80,16}... | collective-permute-start | bytes 147464 | tf_op jit(solution)/shard_map/ppermute | solution.py:297
  90.1 10.3 %collective-permute-start.13 = (f32[96,128]{1,0:T(8,128)S(1)}, f32[96,128]{1,0:T(8,128)S(1)}, u32[]{:S(2)}, u32[]{:S(2)}) collective-permute-start(f32[96,128]{1,0:T(8,128)S(1)} %get-tuple-element.56), channel_id=1, source_target_pairs={{66,0},{68,2},{70,4},{64,6},{74,8},{76,10},{78,12},{72,14},{82,16}... | collective-permute-start | bytes 147464 | tf_op jit(solution)/shard_map/ppermute | solution.py:297
  92.7 10.9 %collective-permute-start.14 = (f32[96,128]{1,0:T(8,128)S(1)}, f32[96,128]{1,0:T(8,128)S(1)}, u32[]{:S(2)}, u32[]{:S(2)}) collective-permute-start(f32[96,128]{1,0:T(8,128)S(1)} %get-tuple-element.57), channel_id=1, source_target_pairs={{68,0},{70,2},{64,4},{66,6},{76,8},{78,10},{72,12},{74,14},{84,16}... | collective-permute-start | bytes 147464 | tf_op jit(solution)/shard_map/ppermute | solution.py:297
  94.2 9.6 %collective-permute-start.15 = (f32[96,128]{1,0:T(8,128)S(1)}, f32[96,128]{1,0:T(8,128)S(1)}, u32[]{:S(2)}, u32[]{:S(2)}) collective-permute-start(f32[96,128]{1,0:T(8,128)S(1)} %get-tuple-element.58), channel_id=1, source_target_pairs={{70,0},{64,2},{66,4},{68,6},{78,8},{72,10},{74,12},{76,14},{86,16}... | collective-permute-start | bytes 147464 | tf_op jit(solution)/shard_map/ppermute | solution.py:297
  94.2 10.5 %collective-permute-start.16 = (f32[96,128]{1,0:T(8,128)S(1)}, f32[96,128]{1,0:T(8,128)S(1)}, u32[]{:S(2)}, u32[]{:S(2)}) collective-permute-start(f32[96,128]{1,0:T(8,128)S(1)} %get-tuple-element.59), channel_id=1, source_target_pairs={{128,0},{130,2},{132,4},{134,6},{136,8},{138,10},{140,12},{142,14}... | collective-permute-start | bytes 147464 | tf_op jit(solution)/shard_map/ppermute | solution.py:297
  97.0 12.3 %collective-permute-start.17 = (f32[96,128]{1,0:T(8,128)S(1)}, f32[96,128]{1,0:T(8,128)S(1)}, u32[]{:S(2)}, u32[]{:S(2)}) collective-permute-start(f32[96,128]{1,0:T(8,128)S(1)} %get-tuple-element.60), channel_id=1, source_target_pairs={{130,0},{132,2},{134,4},{128,6},{138,8},{140,10},{142,12},{136,14}... | collective-permute-start | bytes 147464 | tf_op jit(solution)/shard_map/ppermute | solution.py:297
  100.4 11.0 %collective-permute-start.18 = (f32[96,128]{1,0:T(8,128)S(1)}, f32[96,128]{1,0:T(8,128)S(1)}, u32[]{:S(2)}, u32[]{:S(2)}) collective-permute-start(f32[96,128]{1,0:T(8,128)S(1)} %get-tuple-element.61), channel_id=1, source_target_pairs={{132,0},{134,2},{128,4},{130,6},{140,8},{142,10},{136,12},{138,14}... | collective-permute-start | bytes 147464 | tf_op jit(solution)/shard_map/ppermute | solution.py:297
  103.7 8.4 %collective-permute-start.19 = (f32[96,128]{1,0:T(8,128)S(1)}, f32[96,128]{1,0:T(8,128)S(1)}, u32[]{:S(2)}, u32[]{:S(2)}) collective-permute-start(f32[96,128]{1,0:T(8,128)S(1)} %get-tuple-element.62), channel_id=1, source_target_pairs={{134,0},{128,2},{130,4},{132,6},{142,8},{136,10},{138,12},{140,14}... | collective-permute-start | bytes 147464 | tf_op jit(solution)/shard_map/ppermute | solution.py:297
  103.8 8.3 %collective-permute-start.20 = (f32[96,128]{1,0:T(8,128)S(1)}, f32[96,128]{1,0:T(8,128)S(1)}, u32[]{:S(2)}, u32[]{:S(2)}) collective-permute-start(f32[96,128]{1,0:T(8,128)S(1)} %get-tuple-element.63), channel_id=1, source_target_pairs={{192,0},{194,2},{196,4},{198,6},{200,8},{202,10},{204,12},{206,14}... | collective-permute-start | bytes 147464 | tf_op jit(solution)/shard_map/ppermute | solution.py:297
  104.8 7.3 %collective-permute-start.21 = (f32[96,128]{1,0:T(8,128)S(1)}, f32[96,128]{1,0:T(8,128)S(1)}, u32[]{:S(2)}, u32[]{:S(2)}) collective-permute-start(f32[96,128]{1,0:T(8,128)S(1)} %get-tuple-element.64), channel_id=1, source_target_pairs={{194,0},{196,2},{198,4},{192,6},{202,8},{204,10},{206,12},{200,14}... | collective-permute-start | bytes 147464 | tf_op jit(solution)/shard_map/ppermute | solution.py:297
  109.3 7.7 %collective-permute-start.22 = (f32[96,128]{1,0:T(8,128)S(1)}, f32[96,128]{1,0:T(8,128)S(1)}, u32[]{:S(2)}, u32[]{:S(2)}) collective-permute-start(f32[96,128]{1,0:T(8,128)S(1)} %get-tuple-element.65), channel_id=1, source_target_pairs={{196,0},{198,2},{192,4},{194,6},{204,8},{206,10},{200,12},{202,14}... | collective-permute-start | bytes 147464 | tf_op jit(solution)/shard_map/ppermute | solution.py:297
  111.4 7.4 %collective-permute-start.23 = (f32[96,128]{1,0:T(8,128)S(1)}, f32[96,128]{1,0:T(8,128)S(1)}, u32[]{:S(2)}, u32[]{:S(2)}) collective-permute-start(f32[96,128]{1,0:T(8,128)S(1)} %get-tuple-element.66), channel_id=1, source_target_pairs={{198,0},{192,2},{194,4},{196,6},{206,8},{200,10},{202,12},{204,14}... | collective-permute-start | bytes 147464 | tf_op jit(solution)/shard_map/ppermute | solution.py:297
  (6 other events, 118.8 us)

commit v3 on v2

--- a/solution.py
+++ b/solution.py
@@ -57,6 +57,11 @@
     return np.stack(
         [rows_of(angles(modes[parity::2][order], np.arange(cells // 2), cells), cells) for parity in range(2)]
     )
+
+
+def folded_z_table(cells, keep, positions):
+    modes = signed(np.arange(keep), keep)
+    return np.stack([rows_of(angles(modes[parity::2], positions, cells), cells) for parity in range(2)])
 
 
 def z_table(cells, keep, positions):
@@ -179,11 +184,11 @@
             outs[dy * NX + dx][...] = all_ref[pl.ds(to, count, NXY), :]
 
 
-def wave_numbers(keep, lanes, first, count):
+def wave_numbers(keep, lanes, first, count, step):
     group = lax.axis_index("section") * lax.axis_size("pen") + lax.axis_index("pen")
     limit = -(keep // 2)
     visc = 0.5 / (keep // 2) ** 2
-    row = lax.broadcasted_iota(jnp.int32, (count, lanes), 0) + first
+    row = lax.broadcasted_iota(jnp.int32, (count, lanes), 0) * step + first
     col = lax.broadcasted_iota(jnp.int32, (count, lanes), 1) + lax.axis_index("slab") * lanes
     kz = jnp.where(row < keep // 2, row, row - keep)
     kx = jnp.where(col < keep // 2, col, col - keep)
@@ -207,7 +212,9 @@
 
 
 def early_kernel(keep, *refs):
-    gots, (modes_ref, table_ref, out_ref, all_ref) = refs[:NXY], refs[NXY:]
+    gots, (modes_hbm, table_ref, out_ref, all_ref, modes_ref, sem) = refs[:NXY], refs[NXY:]
+    copy = pltpu.make_async_copy(modes_hbm, modes_ref, sem)
+    copy.start()
     y, _, x = place()
     lanes = out_ref.shape[1]
     kinds = gots[0].shape[0] // NZ
@@ -218,7 +225,8 @@
             for k in range(kinds):
                 at = pl.multiple_of(k * sources + source * NZ, NZ)
                 all_ref[pl.ds(at, NZ), :] = gots[dy * NX + dx][pl.ds(k, NZ, kinds), :]
-    for parity, waves, mask, inverse, damp in wave_numbers(keep, lanes, 0, keep):
+    copy.wait()
+    for parity, waves, mask, inverse, damp in wave_numbers(keep, lanes, 0, keep, 1):
         sums = []
         for c in range(3):
             base = c * 4 + parity * 2
@@ -234,30 +242,34 @@
     lanes = x_ref.shape[1]
     per = 3 * planes * 4
     sources = x_ref.shape[0] // per
+    run = NXY // 2
     for parity in range(2):
         for c in range(3):
-            columns = [
-                jnp.concatenate(
-                    [x_ref[pl.ds((p * 3 + c) * 4 + parity * 2 + q, sources, per), :] for p in range(planes)], axis=0
-                )
-                for q in range(2)
-            ]
-            pair = z_sums(keep, lanes, table_ref, jnp.concatenate(columns, axis=1))
-            for q in range(2):
-                sums_ref[parity, q, c] = pair[q]
+            sums, differences = [], []
+            for p in range(planes):
+                at = (p * 3 + c) * 4 + parity * 2
+                both = jnp.concatenate([x_ref[pl.ds(at + q, sources, per), :] for q in range(2)], axis=1)
+                both = both.reshape(NZ, 2, run, 2 * lanes)
+                sums.append((both[:, 0] + both[:, 1]).reshape(NZ * run, 2 * lanes))
+                differences.append((both[:, 0] - both[:, 1]).reshape(NZ * run, 2 * lanes))
+            for e, folded in enumerate((sums, differences)):
+                pair = z_sums(keep // 2, lanes, table_ref.at[e], jnp.concatenate(folded, axis=0))
+                for q in range(2):
+                    sums_ref[parity, q, c, e] = pair[q]
     count = sems.shape[0] // 3
-    part = keep // count
+    part = keep // 2 // count
     copies = []
     for h in range(count):
         here = slice(h * part, (h + 1) * part)
-        for parity, waves, mask, inverse, _ in wave_numbers(keep, lanes, h * part, part):
-            for q in range(2):
-                values = projected([sums_ref[parity, q, c, here] for c in range(3)], waves, mask, inverse)
-                for c, value in enumerate(values):
-                    where = pl.ds((c * keep + h * part) * 4 + parity * 2 + q, part, 4)
-                    out_ref[where, :] = value + early_ref[where, :]
+        for e in range(2):
+            for parity, waves, mask, inverse, _ in wave_numbers(keep, lanes, h * part * 2 + e, part, 2):
+                for q in range(2):
+                    values = projected([sums_ref[parity, q, c, e, here] for c in range(3)], waves, mask, inverse)
+                    for c, value in enumerate(values):
+                        where = pl.ds((c * keep + h * part * 2 + e) * 4 + parity * 2 + q, part, 8)
+                        out_ref[where, :] = value + early_ref[where, :]
         for c in range(3):
-            rows = pl.ds((c * keep + h * part) * 4, part * 4)
+            rows = pl.ds((c * keep + h * part * 2) * 4, part * 8)
             copies.append(pltpu.make_async_copy(out_ref.at[rows], out_hbm.at[rows], sems.at[h * 3 + c]))
             copies[-1].start()
     for copy in copies:
@@ -273,7 +285,7 @@
         return pl.pallas_call(
             kernel,
             out_shape=shapes[0] if single else shapes,
-            in_specs=[pl.BlockSpec(memory_space=space)] * len(args),
+            in_specs=[pl.BlockSpec(memory_space=m) for m in (space if isinstance(space, list) else [space] * len(args))],
             out_specs=specs[0] if single else specs,
             scratch_shapes=list(scratch),
             cost_estimate=pl.CostEstimate(flops=flops, bytes_accessed=size, transcendentals=0),
@@ -344,20 +356,27 @@
         functools.partial(early_kernel, keep),
         [(3 * keep * 4, lanes)],
         2 * 6 * 2 * keep * 3 * dests * keep,
-        [VMEM((kinds * dests, lanes), jnp.float32)],
+        [
+            VMEM((kinds * dests, lanes), jnp.float32),
+            VMEM((3 * keep * 4, lanes), jnp.float32),
+            pltpu.SemaphoreType.DMA,
+        ],
+        [VMEM] * NXY + [pltpu.HBM, VMEM],
+        limit=50 << 20,
     )(
         *spread,
         velocity_modes.reshape(3 * keep * 4, lanes),
         jnp.asarray(z_table(cells, keep, planes * xy_major_groups())),
     )
-    rest = np.concatenate([planes * order + p for p in range(1, planes)])
-    table_z = jnp.asarray(z_table(cells, keep, rest))
+    near = order.reshape(NZ, 2, -1)[:, 0].reshape(-1)
+    rest = np.concatenate([planes * near + p for p in range(1, planes)])
+    table_z = jnp.asarray(folded_z_table(cells, keep, rest))
     out = call(
         functools.partial(z_kernel, planes - 1, keep),
         [(3 * keep * 4, lanes)],
-        2 * 6 * 2 * keep * 3 * (planes - 1) * dests * keep,
+        6 * 2 * keep * 3 * (planes - 1) * dests * keep,
         [
-            VMEM((2, 2, 3, keep, lanes), jnp.float32),
+            VMEM((2, 2, 3, 2, keep // 2, lanes), jnp.float32),
             VMEM((3 * keep * 4, lanes), jnp.float32),
             pltpu.SemaphoreType.DMA((6,)),
         ],

time: 126 us -> 125 us (level)
  local copies, waits for them, and re-layouts: 2.46 us -> 0.96 us
  Pallas kernels: 13.7 us -> 15 us
    unnamed x10 -> x8, local copies, waits for them, and re-layouts: 2.46 us -> 0.96 us
    pallas_call x8, Pallas kernels: 13.7 us -> 15 us  [run(): pl.pallas_call(kernel, out_shape=shapes[0] if single else shapes, in_spec...]
  transfers between devices with their start and end apart: 25 -> 25, of which waited for: 8 -> 8; matrix products, arithmetic and copies ran while one was open for 0% -> 0% of each run, Pallas kernels for 3% -> 4%
where the time goes in v3:
time: 125 us
  starting transfers between devices  63.1 us (50%)
  waiting for transfers between devices  45.9 us (37%)
  Pallas kernels  15 us (12%)
    ppermute x22, starting transfers between devices, from_shift(): return lax.ppermute(value, GROUP, pairs)  47.4 us
    ppermute x22, waiting for transfers between devices, from_shift(): return lax.ppermute(value, GROUP, pairs)  43.7 us
    all_to_all x1, starting transfers between devices, per_device(): lax.all_to_all(packed.reshape(dests, per, lanes), GROUP, 0, 0, axis_index...  15 us
    pallas_call x8, Pallas kernels, run(): pl.pallas_call(kernel, out_shape=shapes[0] if single else shapes, in_spec...  15 us
  transfers between devices with their start and end apart: 25, of which 8 were waited for; matrix products, arithmetic and copies ran while one was open for 0% of the time, Pallas kernels for 4%

profile of v3, /device:TPU:32, one launch (start us, length us, event | category | flops | bytes accessed | tf_op | source)
XLA Modules:
  0.0 125.3 jit_solution(15510254661163080059)
XLA Ops:
  0.0 2.9 %shard_map.73 = (bf16[576,768]{1,0:T(8,128)(2,1)S(1)}, bf16[576,768]{1,0:T(8,128)(2,1)S(1)}, bf16[576,768]{1,0:T(8,128)(2,1)S(1)}) custom-call(f32[3,3,192,384]{3,2,1,0:T(8,128)} %v_hbm.1, f32[3,3,192,384]{3,2,1,0:T(8,128)} %w_hbm.1), custom_call_target="tpu_custom_call" | custom-call | flops 3981312 | bytes 10616832 | tf_op jit(solution)/shard_map/pallas_call | solution.py:285
  6.3 2.2 %collective-permute-done.1.got_ref = f32[576,256]{1,0:T(8,128)S(1)} collective-permute-done((f32[576,256]{1,0:T(8,128)S(1)}, f32[576,256]{1,0:T(8,128)S(1)}, u32[]{:S(2)}, u32[]{:S(2)}) %collective-permute-start.1) | collective-permute-done | bytes 589856 | tf_op jit(solution)/shard_map/ppermute | solution.py:334
  9.3 2.7 %shard_map.77 = f32[3072,128]{1,0:T(8,128)} custom-call(f32[1152,256]{1,0:T(8,128)S(1)} %get-tuple-element.38.keep_ref, f32[1152,256]{1,0:T(8,128)S(1)} %collective-permute-done.got_ref, bf16[2,2,256,192]{3,2,1,0:T(8,128)(2,1)S(1)} %copy-done, f32[192,128]{1,0:T(8,128)S(1)} %get-tuple-element.43._.refs_0_), custom_call_target="tpu_custom_call" | custom-call | flops 905969664 | bytes 4423680 | tf_op jit(solution)/shard_map/pallas_call | solution.py:285
  12.0 15.0 %all-to-all-start = ((f32[128,24,128]{2,1,0:T(8,128)}), f32[128,24,128]{2,1,0:T(8,128)S(1)}, u32[]{:S(2)}, u32[]{:S(2)}) async-start(f32[128,24,128]{2,1,0:T(8,128)} %bitcast), calls=%async_computation | async-start | bytes 3145728 | tf_op jit(solution)/shard_map/all_to_all | solution.py:350
  28.0 3.8 %collective-permute-start.3 = (f32[192,128]{1,0:T(8,128)S(1)}, f32[192,128]{1,0:T(8,128)S(1)}, u32[]{:S(2)}, u32[]{:S(2)}) collective-permute-start(f32[192,128]{1,0:T(8,128)S(1)} %get-tuple-element.45), channel_id=1, source_target_pairs={{16,0},{18,2},{20,4},{22,6},{24,8},{26,10},{28,12},{30,14},{32,16}... | collective-permute-start | bytes 294920 | tf_op jit(solution)/shard_map/ppermute | solution.py:309
  31.7 2.0 %collective-permute-start.4 = (f32[192,128]{1,0:T(8,128)S(1)}, f32[192,128]{1,0:T(8,128)S(1)}, u32[]{:S(2)}, u32[]{:S(2)}) collective-permute-start(f32[192,128]{1,0:T(8,128)S(1)} %get-tuple-element.46), channel_id=1, source_target_pairs={{24,0},{26,2},{28,4},{30,6},{32,8},{34,10},{36,12},{38,14},{40,16}... | collective-permute-start | bytes 294920 | tf_op jit(solution)/shard_map/ppermute | solution.py:309
  33.8 3.1 %collective-permute-start.5 = (f32[192,128]{1,0:T(8,128)S(1)}, f32[192,128]{1,0:T(8,128)S(1)}, u32[]{:S(2)}, u32[]{:S(2)}) collective-permute-start(f32[192,128]{1,0:T(8,128)S(1)} %get-tuple-element.47), channel_id=1, source_target_pairs={{32,0},{34,2},{36,4},{38,6},{40,8},{42,10},{44,12},{46,14},{48,16}... | collective-permute-start | bytes 294920 | tf_op jit(solution)/shard_map/ppermute | solution.py:309
  38.7 28.5 %collective-permute-done.2.refs_1_ = f32[192,128]{1,0:T(8,128)S(1)} collective-permute-done((f32[192,128]{1,0:T(8,128)S(1)}, f32[192,128]{1,0:T(8,128)S(1)}, u32[]{:S(2)}, u32[]{:S(2)}) %collective-permute-start.2) | collective-permute-done | bytes 98336 | tf_op jit(solution)/shard_map/ppermute | solution.py:309
  67.2 1.8 %collective-permute-start.7 = (f32[192,128]{1,0:T(8,128)S(1)}, f32[192,128]{1,0:T(8,128)S(1)}, u32[]{:S(2)}, u32[]{:S(2)}) collective-permute-start(f32[192,128]{1,0:T(8,128)S(1)} %get-tuple-element.49), channel_id=1, source_target_pairs={{48,0},{50,2},{52,4},{54,6},{56,8},{58,10},{60,12},{62,14},{0,16},... | collective-permute-start | bytes 294920 | tf_op jit(solution)/shard_map/ppermute | solution.py:309
  69.4 5.1 %collective-permute-start.8 = (f32[192,128]{1,0:T(8,128)S(1)}, f32[192,128]{1,0:T(8,128)S(1)}, u32[]{:S(2)}, u32[]{:S(2)}) collective-permute-start(f32[192,128]{1,0:T(8,128)S(1)} %get-tuple-element.50), channel_id=1, source_target_pairs={{56,0},{58,2},{60,4},{62,6},{0,8},{2,10},{4,12},{6,14},{8,16},{10,... | collective-permute-start | bytes 294920 | tf_op jit(solution)/shard_map/ppermute | solution.py:309
  74.5 2.9 %collective-permute-done.4.refs_3_ = f32[192,128]{1,0:T(8,128)S(1)} collective-permute-done((f32[192,128]{1,0:T(8,128)S(1)}, f32[192,128]{1,0:T(8,128)S(1)}, u32[]{:S(2)}, u32[]{:S(2)}) %collective-permute-start.4) | collective-permute-done | bytes 98336 | tf_op jit(solution)/shard_map/ppermute | solution.py:309
  77.4 4.5 %collective-permute-done.5.refs_4_ = f32[192,128]{1,0:T(8,128)S(1)} collective-permute-done((f32[192,128]{1,0:T(8,128)S(1)}, f32[192,128]{1,0:T(8,128)S(1)}, u32[]{:S(2)}, u32[]{:S(2)}) %collective-permute-start.5) | collective-permute-done | bytes 98336 | tf_op jit(solution)/shard_map/ppermute | solution.py:309
  82.4 3.1 %collective-permute-start.9 = (f32[96,128]{1,0:T(8,128)S(1)}, f32[96,128]{1,0:T(8,128)S(1)}, u32[]{:S(2)}, u32[]{:S(2)}) collective-permute-start(f32[96,128]{1,0:T(8,128)S(1)} %get-tuple-element.52), channel_id=1, source_target_pairs={{2,0},{4,2},{6,4},{0,6},{10,8},{12,10},{14,12},{8,14},{18,16},{20,... | collective-permute-start | bytes 147464 | tf_op jit(solution)/shard_map/ppermute | solution.py:309
  87.2 2.8 %collective-permute-start.12 = (f32[96,128]{1,0:T(8,128)S(1)}, f32[96,128]{1,0:T(8,128)S(1)}, u32[]{:S(2)}, u32[]{:S(2)}) collective-permute-start(f32[96,128]{1,0:T(8,128)S(1)} %get-tuple-element.55), channel_id=1, source_target_pairs={{64,0},{66,2},{68,4},{70,6},{72,8},{74,10},{76,12},{78,14},{80,16}... | collective-permute-start | bytes 147464 | tf_op jit(solution)/shard_map/ppermute | solution.py:309
  90.0 2.6 %collective-permute-start.13 = (f32[96,128]{1,0:T(8,128)S(1)}, f32[96,128]{1,0:T(8,128)S(1)}, u32[]{:S(2)}, u32[]{:S(2)}) collective-permute-start(f32[96,128]{1,0:T(8,128)S(1)} %get-tuple-element.56), channel_id=1, source_target_pairs={{66,0},{68,2},{70,4},{64,6},{74,8},{76,10},{78,12},{72,14},{82,16}... | collective-permute-start | bytes 147464 | tf_op jit(solution)/shard_map/ppermute | solution.py:309
  94.1 2.8 %collective-permute-start.16 = (f32[96,128]{1,0:T(8,128)S(1)}, f32[96,128]{1,0:T(8,128)S(1)}, u32[]{:S(2)}, u32[]{:S(2)}) collective-permute-start(f32[96,128]{1,0:T(8,128)S(1)} %get-tuple-element.59), channel_id=1, source_target_pairs={{128,0},{130,2},{132,4},{134,6},{136,8},{138,10},{140,12},{142,14}... | collective-permute-start | bytes 147464 | tf_op jit(solution)/shard_map/ppermute | solution.py:309
  96.9 3.4 %collective-permute-start.17 = (f32[96,128]{1,0:T(8,128)S(1)}, f32[96,128]{1,0:T(8,128)S(1)}, u32[]{:S(2)}, u32[]{:S(2)}) collective-permute-start(f32[96,128]{1,0:T(8,128)S(1)} %get-tuple-element.60), channel_id=1, source_target_pairs={{130,0},{132,2},{134,4},{128,6},{138,8},{140,10},{142,12},{136,14}... | collective-permute-start | bytes 147464 | tf_op jit(solution)/shard_map/ppermute | solution.py:309
  100.2 3.3 %collective-permute-start.18 = (f32[96,128]{1,0:T(8,128)S(1)}, f32[96,128]{1,0:T(8,128)S(1)}, u32[]{:S(2)}, u32[]{:S(2)}) collective-permute-start(f32[96,128]{1,0:T(8,128)S(1)} %get-tuple-element.61), channel_id=1, source_target_pairs={{132,0},{134,2},{128,4},{130,6},{140,8},{142,10},{136,12},{138,14}... | collective-permute-start | bytes 147464 | tf_op jit(solution)/shard_map/ppermute | solution.py:309
  104.6 4.5 %collective-permute-start.21 = (f32[96,128]{1,0:T(8,128)S(1)}, f32[96,128]{1,0:T(8,128)S(1)}, u32[]{:S(2)}, u32[]{:S(2)}) collective-permute-start(f32[96,128]{1,0:T(8,128)S(1)} %get-tuple-element.64), channel_id=1, source_target_pairs={{194,0},{196,2},{198,4},{192,6},{202,8},{204,10},{206,12},{200,14}... | collective-permute-start | bytes 147464 | tf_op jit(solution)/shard_map/ppermute | solution.py:309
  109.2 2.1 %collective-permute-start.22 = (f32[96,128]{1,0:T(8,128)S(1)}, f32[96,128]{1,0:T(8,128)S(1)}, u32[]{:S(2)}, u32[]{:S(2)}) collective-permute-start(f32[96,128]{1,0:T(8,128)S(1)} %get-tuple-element.65), channel_id=1, source_target_pairs={{196,0},{198,2},{192,4},{194,6},{204,8},{206,10},{200,12},{202,14}... | collective-permute-start | bytes 147464 | tf_op jit(solution)/shard_map/ppermute | solution.py:309
  111.9 4.9 %collective-permute-done.22.refs_14_ = f32[96,128]{1,0:T(8,128)S(1)} collective-permute-done((f32[96,128]{1,0:T(8,128)S(1)}, f32[96,128]{1,0:T(8,128)S(1)}, u32[]{:S(2)}, u32[]{:S(2)}) %collective-permute-start.22) | collective-permute-done | bytes 49184 | tf_op jit(solution)/shard_map/ppermute | solution.py:309
  116.9 1.8 %collective-permute-done.23.refs_15_ = f32[96,128]{1,0:T(8,128)S(1)} collective-permute-done((f32[96,128]{1,0:T(8,128)S(1)}, f32[96,128]{1,0:T(8,128)S(1)}, u32[]{:S(2)}, u32[]{:S(2)}) %collective-permute-start.23) | collective-permute-done | bytes 49184 | tf_op jit(solution)/shard_map/ppermute | solution.py:309
  119.6 2.7 %shard_map.79.early_ref = f32[3072,128]{1,0:T(8,128)S(1)} custom-call(f32[96,128]{1,0:T(8,128)S(1)} %get-tuple-element.51.refs_0_, f32[96,128]{1,0:T(8,128)S(1)} %collective-permute-done.9.refs_1_, f32[96,128]{1,0:T(8,128)S(1)} %collective-permute-done.10.refs_2_, f32[96,128]{1,0:T(8,128)S(1)} %collective-permute-done.11.refs_3_, ...), custom_call_target="tpu_custom_call" | custom-call | flops 603979776 | bytes 4194304 | tf_op jit(solution)/shard_map/pallas_call | solution.py:285
  122.3 2.8 %shard_map.80 = f32[3072,128]{1,0:T(8,128)} custom-call(f32[3072,128]{1,0:T(8,128)S(1)} %bitcast.4, f32[3072,128]{1,0:T(8,128)S(1)} %shard_map.79.early_ref, bf16[2,2,256,128]{3,2,1,0:T(8,128)(2,1)S(1)} %copy-done.1), custom_call_target="tpu_custom_call" | custom-call | flops 603979776 | bytes 4980736 | tf_op jit(solution)/shard_map/pallas_call | solution.py:285
  (42 shorter events, 13.8 us)
Async XLA Ops:
  4.6 4.7 %collective-permute-start = (f32[1152,256]{1,0:T(8,128)S(1)}, f32[1152,256]{1,0:T(8,128)S(1)}, u32[]{:S(2)}, u32[]{:S(2)}) collective-permute-start(f32[1152,256]{1,0:T(8,128)S(1)} %get-tuple-element.39), channel_id=1, source_target_pairs={{0,1},{1,0},{2,3},{3,2},{4,5},{5,4},{6,7},{7,6},{8,9},{9,8},{10,11... | collective-permute-start | bytes 3538952 | tf_op jit(solution)/shard_map/ppermute | solution.py:334
  12.0 110.3 %all-to-all-start = ((f32[128,24,128]{2,1,0:T(8,128)}), f32[128,24,128]{2,1,0:T(8,128)S(1)}, u32[]{:S(2)}, u32[]{:S(2)}) async-start(f32[128,24,128]{2,1,0:T(8,128)} %bitcast), calls=%async_computation | async-start | bytes 3145728 | tf_op jit(solution)/shard_map/all_to_all | solution.py:350
  27.0 40.2 %collective-permute-start.2 = (f32[192,128]{1,0:T(8,128)S(1)}, f32[192,128]{1,0:T(8,128)S(1)}, u32[]{:S(2)}, u32[]{:S(2)}) collective-permute-start(f32[192,128]{1,0:T(8,128)S(1)} %get-tuple-element.44), channel_id=1, source_target_pairs={{8,0},{10,2},{12,4},{14,6},{16,8},{18,10},{20,12},{22,14},{24,16},... | collective-permute-start | bytes 294920 | tf_op jit(solution)/shard_map/ppermute | solution.py:309
  28.0 41.5 %collective-permute-start.3 = (f32[192,128]{1,0:T(8,128)S(1)}, f32[192,128]{1,0:T(8,128)S(1)}, u32[]{:S(2)}, u32[]{:S(2)}) collective-permute-start(f32[192,128]{1,0:T(8,128)S(1)} %get-tuple-element.45), channel_id=1, source_target_pairs={{16,0},{18,2},{20,4},{22,6},{24,8},{26,10},{28,12},{30,14},{32,16}... | collective-permute-start | bytes 294920 | tf_op jit(solution)/shard_map/ppermute | solution.py:309
  31.7 45.7 %collective-permute-start.4 = (f32[192,128]{1,0:T(8,128)S(1)}, f32[192,128]{1,0:T(8,128)S(1)}, u32[]{:S(2)}, u32[]{:S(2)}) collective-permute-start(f32[192,128]{1,0:T(8,128)S(1)} %get-tuple-element.46), channel_id=1, source_target_pairs={{24,0},{26,2},{28,4},{30,6},{32,8},{34,10},{36,12},{38,14},{40,16}... | collective-permute-start | bytes 294920 | tf_op jit(solution)/shard_map/ppermute | solution.py:309
  33.8 48.1 %collective-permute-start.5 = (f32[192,128]{1,0:T(8,128)S(1)}, f32[192,128]{1,0:T(8,128)S(1)}, u32[]{:S(2)}, u32[]{:S(2)}) collective-permute-start(f32[192,128]{1,0:T(8,128)S(1)} %get-tuple-element.47), channel_id=1, source_target_pairs={{32,0},{34,2},{36,4},{38,6},{40,8},{42,10},{44,12},{46,14},{48,16}... | collective-permute-start | bytes 294920 | tf_op jit(solution)/shard_map/ppermute | solution.py:309
  36.9 45.0 %collective-permute-start.6 = (f32[192,128]{1,0:T(8,128)S(1)}, f32[192,128]{1,0:T(8,128)S(1)}, u32[]{:S(2)}, u32[]{:S(2)}) collective-permute-start(f32[192,128]{1,0:T(8,128)S(1)} %get-tuple-element.48), channel_id=1, source_target_pairs={{40,0},{42,2},{44,4},{46,6},{48,8},{50,10},{52,12},{54,14},{56,16}... | collective-permute-start | bytes 294920 | tf_op jit(solution)/shard_map/ppermute | solution.py:309
  67.2 14.7 %collective-permute-start.7 = (f32[192,128]{1,0:T(8,128)S(1)}, f32[192,128]{1,0:T(8,128)S(1)}, u32[]{:S(2)}, u32[]{:S(2)}) collective-permute-start(f32[192,128]{1,0:T(8,128)S(1)} %get-tuple-element.49), channel_id=1, source_target_pairs={{48,0},{50,2},{52,4},{54,6},{56,8},{58,10},{60,12},{62,14},{0,16},... | collective-permute-start | bytes 294920 | tf_op jit(solution)/shard_map/ppermute | solution.py:309
  69.4 12.5 %collective-permute-start.8 = (f32[192,128]{1,0:T(8,128)S(1)}, f32[192,128]{1,0:T(8,128)S(1)}, u32[]{:S(2)}, u32[]{:S(2)}) collective-permute-start(f32[192,128]{1,0:T(8,128)S(1)} %get-tuple-element.50), channel_id=1, source_target_pairs={{56,0},{58,2},{60,4},{62,6},{0,8},{2,10},{4,12},{6,14},{8,16},{10,... | collective-permute-start | bytes 294920 | tf_op jit(solution)/shard_map/ppermute | solution.py:309
  82.4 10.2 %collective-permute-start.9 = (f32[96,128]{1,0:T(8,128)S(1)}, f32[96,128]{1,0:T(8,128)S(1)}, u32[]{:S(2)}, u32[]{:S(2)}) collective-permute-start(f32[96,128]{1,0:T(8,128)S(1)} %get-tuple-element.52), channel_id=1, source_target_pairs={{2,0},{4,2},{6,4},{0,6},{10,8},{12,10},{14,12},{8,14},{18,16},{20,... | collective-permute-start | bytes 147464 | tf_op jit(solution)/shard_map/ppermute | solution.py:309
  85.5 8.6 %collective-permute-start.10 = (f32[96,128]{1,0:T(8,128)S(1)}, f32[96,128]{1,0:T(8,128)S(1)}, u32[]{:S(2)}, u32[]{:S(2)}) collective-permute-start(f32[96,128]{1,0:T(8,128)S(1)} %get-tuple-element.53), channel_id=1, source_target_pairs={{4,0},{6,2},{0,4},{2,6},{12,8},{14,10},{8,12},{10,14},{20,16},{22,... | collective-permute-start | bytes 147464 | tf_op jit(solution)/shard_map/ppermute | solution.py:309
  86.3 7.8 %collective-permute-start.11 = (f32[96,128]{1,0:T(8,128)S(1)}, f32[96,128]{1,0:T(8,128)S(1)}, u32[]{:S(2)}, u32[]{:S(2)}) collective-permute-start(f32[96,128]{1,0:T(8,128)S(1)} %get-tuple-element.54), channel_id=1, source_target_pairs={{6,0},{0,2},{2,4},{4,6},{14,8},{8,10},{10,12},{12,14},{22,16},{16,... | collective-permute-start | bytes 147464 | tf_op jit(solution)/shard_map/ppermute | solution.py:309
  87.2 9.7 %collective-permute-start.12 = (f32[96,128]{1,0:T(8,128)S(1)}, f32[96,128]{1,0:T(8,128)S(1)}, u32[]{:S(2)}, u32[]{:S(2)}) collective-permute-start(f32[96,128]{1,0:T(8,128)S(1)} %get-tuple-element.55), channel_id=1, source_target_pairs={{64,0},{66,2},{68,4},{70,6},{72,8},{74,10},{76,12},{78,14},{80,16}... | collective-permute-start | bytes 147464 | tf_op jit(solution)/shard_map/ppermute | solution.py:309
  90.0 10.3 %collective-permute-start.13 = (f32[96,128]{1,0:T(8,128)S(1)}, f32[96,128]{1,0:T(8,128)S(1)}, u32[]{:S(2)}, u32[]{:S(2)}) collective-permute-start(f32[96,128]{1,0:T(8,128)S(1)} %get-tuple-element.56), channel_id=1, source_target_pairs={{66,0},{68,2},{70,4},{64,6},{74,8},{76,10},{78,12},{72,14},{82,16}... | collective-permute-start | bytes 147464 | tf_op jit(solution)/shard_map/ppermute | solution.py:309
  92.6 10.9 %collective-permute-start.14 = (f32[96,128]{1,0:T(8,128)S(1)}, f32[96,128]{1,0:T(8,128)S(1)}, u32[]{:S(2)}, u32[]{:S(2)}) collective-permute-start(f32[96,128]{1,0:T(8,128)S(1)} %get-tuple-element.57), channel_id=1, source_target_pairs={{68,0},{70,2},{64,4},{66,6},{76,8},{78,10},{72,12},{74,14},{84,16}... | collective-permute-start | bytes 147464 | tf_op jit(solution)/shard_map/ppermute | solution.py:309
  94.0 9.6 %collective-permute-start.15 = (f32[96,128]{1,0:T(8,128)S(1)}, f32[96,128]{1,0:T(8,128)S(1)}, u32[]{:S(2)}, u32[]{:S(2)}) collective-permute-start(f32[96,128]{1,0:T(8,128)S(1)} %get-tuple-element.58), channel_id=1, source_target_pairs={{70,0},{64,2},{66,4},{68,6},{78,8},{72,10},{74,12},{76,14},{86,16}... | collective-permute-start | bytes 147464 | tf_op jit(solution)/shard_map/ppermute | solution.py:309
  94.1 10.5 %collective-permute-start.16 = (f32[96,128]{1,0:T(8,128)S(1)}, f32[96,128]{1,0:T(8,128)S(1)}, u32[]{:S(2)}, u32[]{:S(2)}) collective-permute-start(f32[96,128]{1,0:T(8,128)S(1)} %get-tuple-element.59), channel_id=1, source_target_pairs={{128,0},{130,2},{132,4},{134,6},{136,8},{138,10},{140,12},{142,14}... | collective-permute-start | bytes 147464 | tf_op jit(solution)/shard_map/ppermute | solution.py:309
  96.9 12.3 %collective-permute-start.17 = (f32[96,128]{1,0:T(8,128)S(1)}, f32[96,128]{1,0:T(8,128)S(1)}, u32[]{:S(2)}, u32[]{:S(2)}) collective-permute-start(f32[96,128]{1,0:T(8,128)S(1)} %get-tuple-element.60), channel_id=1, source_target_pairs={{130,0},{132,2},{134,4},{128,6},{138,8},{140,10},{142,12},{136,14}... | collective-permute-start | bytes 147464 | tf_op jit(solution)/shard_map/ppermute | solution.py:309
  100.2 11.0 %collective-permute-start.18 = (f32[96,128]{1,0:T(8,128)S(1)}, f32[96,128]{1,0:T(8,128)S(1)}, u32[]{:S(2)}, u32[]{:S(2)}) collective-permute-start(f32[96,128]{1,0:T(8,128)S(1)} %get-tuple-element.61), channel_id=1, source_target_pairs={{132,0},{134,2},{128,4},{130,6},{140,8},{142,10},{136,12},{138,14}... | collective-permute-start | bytes 147464 | tf_op jit(solution)/shard_map/ppermute | solution.py:309
  103.5 8.4 %collective-permute-start.19 = (f32[96,128]{1,0:T(8,128)S(1)}, f32[96,128]{1,0:T(8,128)S(1)}, u32[]{:S(2)}, u32[]{:S(2)}) collective-permute-start(f32[96,128]{1,0:T(8,128)S(1)} %get-tuple-element.62), channel_id=1, source_target_pairs={{134,0},{128,2},{130,4},{132,6},{142,8},{136,10},{138,12},{140,14}... | collective-permute-start | bytes 147464 | tf_op jit(solution)/shard_map/ppermute | solution.py:309
  103.7 8.3 %collective-permute-start.20 = (f32[96,128]{1,0:T(8,128)S(1)}, f32[96,128]{1,0:T(8,128)S(1)}, u32[]{:S(2)}, u32[]{:S(2)}) collective-permute-start(f32[96,128]{1,0:T(8,128)S(1)} %get-tuple-element.63), channel_id=1, source_target_pairs={{192,0},{194,2},{196,4},{198,6},{200,8},{202,10},{204,12},{206,14}... | collective-permute-start | bytes 147464 | tf_op jit(solution)/shard_map/ppermute | solution.py:309
  104.6 7.3 %collective-permute-start.21 = (f32[96,128]{1,0:T(8,128)S(1)}, f32[96,128]{1,0:T(8,128)S(1)}, u32[]{:S(2)}, u32[]{:S(2)}) collective-permute-start(f32[96,128]{1,0:T(8,128)S(1)} %get-tuple-element.64), channel_id=1, source_target_pairs={{194,0},{196,2},{198,4},{192,6},{202,8},{204,10},{206,12},{200,14}... | collective-permute-start | bytes 147464 | tf_op jit(solution)/shard_map/ppermute | solution.py:309
  109.2 7.7 %collective-permute-start.22 = (f32[96,128]{1,0:T(8,128)S(1)}, f32[96,128]{1,0:T(8,128)S(1)}, u32[]{:S(2)}, u32[]{:S(2)}) collective-permute-start(f32[96,128]{1,0:T(8,128)S(1)} %get-tuple-element.65), channel_id=1, source_target_pairs={{196,0},{198,2},{192,4},{194,6},{204,8},{206,10},{200,12},{202,14}... | collective-permute-start | bytes 147464 | tf_op jit(solution)/shard_map/ppermute | solution.py:309
  111.3 7.4 %collective-permute-start.23 = (f32[96,128]{1,0:T(8,128)S(1)}, f32[96,128]{1,0:T(8,128)S(1)}, u32[]{:S(2)}, u32[]{:S(2)}) collective-permute-start(f32[96,128]{1,0:T(8,128)S(1)} %get-tuple-element.66), channel_id=1, source_target_pairs={{198,0},{192,2},{194,4},{196,6},{206,8},{200,10},{202,12},{204,14}... | collective-permute-start | bytes 147464 | tf_op jit(solution)/shard_map/ppermute | solution.py:309
  (5 other events, 13.1 us)

commit v4 on v3

--- a/solution.py
+++ b/solution.py
@@ -14,6 +14,7 @@
 GROUP = ("section", "pen")
 NY, NZ, NX = 4, 8, 4
 NXY = NX * NY
+EARLY = 4
 
 
 def signed(index, count):
@@ -62,10 +63,6 @@
 def folded_z_table(cells, keep, positions):
     modes = signed(np.arange(keep), keep)
     return np.stack([rows_of(angles(modes[parity::2], positions, cells), cells) for parity in range(2)])
-
-
-def z_table(cells, keep, positions):
-    return rows_of(angles(signed(np.arange(keep), keep), positions, cells), cells)
 
 
 def split(x):
@@ -120,20 +117,21 @@
             out_ref[c * rows : (c + 1) * rows, cells:] = low
 
 
-def x_kernel(*refs):
-    planes, (table_ref, keep_ref, send_ref) = refs[:-3], refs[-3:]
-    cells = planes[0].shape[1] // 2
-    rows = planes[0].shape[0]
+def x_kernel(spans, *refs):
+    inputs, (table_ref, keep_ref, send_ref) = refs[:-3], refs[-3:]
+    cells = inputs[0].shape[1] // 2
     half = keep_ref.shape[-1]
     mine = lax.axis_index("slab") == 0
     table = jnp.concatenate([table_ref[:cells], table_ref[:cells], table_ref[cells:]], axis=0)
-    for i, ref in enumerate(planes):
-        both = ref[...]
+    at = 0
+    for ref, (first_row, last_row) in zip(inputs, spans):
+        both = ref[first_row:last_row]
         out = product(jnp.concatenate([both, both[:, :cells]], axis=1), table)
         first, second = out[:, :half], out[:, half:]
-        here = slice(i * rows, (i + 1) * rows)
+        here = slice(at, at + last_row - first_row)
         keep_ref[here] = jnp.where(mine, first, second)
         send_ref[here] = jnp.where(mine, second, first)
+        at += last_row - first_row
 
 
 def y_blocks(keep_ref, got_ref, table_ref, rows):
@@ -201,18 +199,25 @@
         yield parity, waves, mask, 1.0 / jnp.maximum(ksq, 1.0), visc * ksq
 
 
-def projected(s, waves, mask, inverse):
-    inner = (waves[0] * s[0] + waves[1] * s[1] + waves[2] * s[2]) * inverse
-    return [mask * (s[c] - waves[c] * inner) for c in range(3)]
-
-
 def z_sums(keep, lanes, table, columns):
-    out = transformed(table[0], table[1], columns)
+    depth = columns.shape[0]
+    out = transformed(table[0, :, :depth], table[1, :, :depth], columns)
     return out[:keep, :lanes] + out[keep:, lanes:], out[:keep, lanes:] - out[keep:, :lanes]
 
 
-def early_kernel(keep, *refs):
-    gots, (modes_hbm, table_ref, out_ref, all_ref, modes_ref, sem) = refs[:NXY], refs[NXY:]
+def project_out(keep, lanes, sums_ref, start, count, put):
+    for e in range(2):
+        for parity, waves, mask, inverse, damp in wave_numbers(keep, lanes, start * 2 + e, count, 2):
+            for q in range(2):
+                s = [sums_ref[parity, q, c, e, start : start + count] for c in range(3)]
+                inner = (waves[0] * s[0] + waves[1] * s[1] + waves[2] * s[2]) * inverse
+                for c in range(3):
+                    where = pl.ds((c * keep + start * 2 + e) * 4 + parity * 2 + q, count, 8)
+                    put(where, mask * (s[c] - waves[c] * inner), damp)
+
+
+def early_kernel(keep, units, *refs):
+    gots, (modes_hbm, table_ref, out_ref, all_ref, sums_ref, modes_ref, sem) = refs[:NXY], refs[NXY:]
     copy = pltpu.make_async_copy(modes_hbm, modes_ref, sem)
     copy.start()
     y, _, x = place()
@@ -225,49 +230,55 @@
             for k in range(kinds):
                 at = pl.multiple_of(k * sources + source * NZ, NZ)
                 all_ref[pl.ds(at, NZ), :] = gots[dy * NX + dx][pl.ds(k, NZ, kinds), :]
+    near = sources // 2
+    for parity in range(2):
+        for c in range(3):
+            folded = [[], []]
+            for unit in units[c]:
+                base = [(unit * 4 + parity * 2 + q) * sources for q in range(2)]
+                one = jnp.concatenate([all_ref[b : b + near] for b in base], axis=1)
+                two = jnp.concatenate([all_ref[b + near : b + sources] for b in base], axis=1)
+                folded[0].append(one + two)
+                folded[1].append(one - two)
+            for e in range(2):
+                pair = z_sums(keep // 2, lanes, table_ref.at[e], jnp.concatenate(folded[e], axis=0))
+                for q in range(2):
+                    sums_ref[parity, q, c, e] = pair[q]
     copy.wait()
-    for parity, waves, mask, inverse, damp in wave_numbers(keep, lanes, 0, keep, 1):
-        sums = []
-        for c in range(3):
-            base = c * 4 + parity * 2
-            both = [all_ref[(base + q) * sources : (base + q + 1) * sources] for q in range(2)]
-            sums.append(z_sums(keep, lanes, table_ref, jnp.concatenate(both, axis=1)))
-        for q in range(2):
-            for c, value in enumerate(projected([s[q] for s in sums], waves, mask, inverse)):
-                where = pl.ds(c * keep * 4 + parity * 2 + q, keep, 4)
-                out_ref[where, :] = value - damp * modes_ref[where, :]
-
-
-def z_kernel(planes, keep, x_ref, early_ref, table_ref, out_hbm, sums_ref, out_ref, sems):
+
+    def put(where, value, damp):
+        out_ref[where, :] = value - damp * modes_ref[where, :]
+
+    project_out(keep, lanes, sums_ref, 0, keep // 2, put)
+
+
+def z_kernel(keep, units, x_ref, early_ref, table_ref, out_hbm, sums_ref, out_ref, sems):
     lanes = x_ref.shape[1]
-    per = 3 * planes * 4
-    sources = x_ref.shape[0] // per
+    sources = NXY * NZ
+    per = x_ref.shape[0] // sources
     run = NXY // 2
     for parity in range(2):
         for c in range(3):
-            sums, differences = [], []
-            for p in range(planes):
-                at = (p * 3 + c) * 4 + parity * 2
+            folded = [[], []]
+            for unit in units[c]:
+                at = unit * 4 + parity * 2
                 both = jnp.concatenate([x_ref[pl.ds(at + q, sources, per), :] for q in range(2)], axis=1)
                 both = both.reshape(NZ, 2, run, 2 * lanes)
-                sums.append((both[:, 0] + both[:, 1]).reshape(NZ * run, 2 * lanes))
-                differences.append((both[:, 0] - both[:, 1]).reshape(NZ * run, 2 * lanes))
-            for e, folded in enumerate((sums, differences)):
-                pair = z_sums(keep // 2, lanes, table_ref.at[e], jnp.concatenate(folded, axis=0))
+                folded[0].append((both[:, 0] + both[:, 1]).reshape(NZ * run, 2 * lanes))
+                folded[1].append((both[:, 0] - both[:, 1]).reshape(NZ * run, 2 * lanes))
+            for e in range(2):
+                pair = z_sums(keep // 2, lanes, table_ref.at[e], jnp.concatenate(folded[e], axis=0))
                 for q in range(2):
                     sums_ref[parity, q, c, e] = pair[q]
+
+    def put(where, value, damp):
+        out_ref[where, :] = value + early_ref[where, :]
+
     count = sems.shape[0] // 3
     part = keep // 2 // count
     copies = []
     for h in range(count):
-        here = slice(h * part, (h + 1) * part)
-        for e in range(2):
-            for parity, waves, mask, inverse, _ in wave_numbers(keep, lanes, h * part * 2 + e, part, 2):
-                for q in range(2):
-                    values = projected([sums_ref[parity, q, c, e, here] for c in range(3)], waves, mask, inverse)
-                    for c, value in enumerate(values):
-                        where = pl.ds((c * keep + h * part * 2 + e) * 4 + parity * 2 + q, part, 8)
-                        out_ref[where, :] = value + early_ref[where, :]
+        project_out(keep, lanes, sums_ref, h * part, part, put)
         for c in range(3):
             rows = pl.ds((c * keep + h * part * 2) * 4, part * 8)
             copies.append(pltpu.make_async_copy(out_ref.at[rows], out_hbm.at[rows], sems.at[h * 3 + c]))
@@ -325,63 +336,66 @@
         limit=50 << 20,
         kind=jnp.bfloat16,
     )(velocity, vorticity)
+    pieces = [(p, c) for p in range(planes) for c in range(3)]
+    groups = (pieces[:EARLY], pieces[EARLY:])
     keeps, gots = [], []
-    for held in (crosses[:1], crosses[1:]):
-        n = len(held)
-        run = call(x_kernel, [(3 * n * rows_y, keep)] * 2, 2 * 9 * n * rows_y * cells * 2 * keep)
-        mine, other = run(*held, table_x)
+    for group in groups:
+        held = sorted({p for p, _ in group})
+        spans = []
+        for p in held:
+            parts = [c for q, c in group if q == p]
+            spans.append((parts[0] * rows_y, (parts[-1] + 1) * rows_y))
+        n = len(group) * rows_y
+        run = call(functools.partial(x_kernel, spans), [(n, keep)] * 2, 12 * n * cells * keep)
+        mine, other = run(*[crosses[p] for p in held], table_x)
         keeps.append(mine)
         gots.append(lax.ppermute(other, "slab", [(0, 1), (1, 0)]))
-    flops = 2 * 3 * 2 * keep * 3 * rows_y * keep
-    kinds = 3 * 4
+    flops = 2 * 2 * keep * 3 * rows_y * keep
+    kinds = EARLY * 4
     sent = call(
         functools.partial(y_send_kernel, rows_y),
         [(kinds * NXY, lanes)] * NZ,
-        flops,
+        flops * EARLY,
         [VMEM((kinds * dests, lanes), jnp.float32)],
     )(keeps[0], gots[0], table_y)
     arrived = [sent[0]]
     for s in range(1, NZ):
         arrived.append(from_shift(sent[s], 0, s, 0))
-    per = (planes - 1) * kinds
+    per = len(groups[1]) * 4
     packed = call(
-        functools.partial(y_pack_kernel, rows_y), [(dests * per, lanes)], flops * (planes - 1)
+        functools.partial(y_pack_kernel, rows_y), [(dests * per, lanes)], flops * len(groups[1])
     )(keeps[1], gots[1], table_y, sent[0])
     late = lax.all_to_all(
-        packed.reshape(dests, per, lanes), GROUP, 0, 0, axis_index_groups=[order.tolist()], tiled=True
+        packed.reshape(dests, per // 4, 4, lanes), GROUP, 0, 0, axis_index_groups=[order.tolist()], tiled=True
     )
     turned = call(turn_kernel, [(NZ * kinds, lanes)] * NXY, 0, [VMEM((NZ * kinds * NXY, lanes), jnp.float32)])(*arrived)
     spread = [turned[0]] + [from_shift(turned[d], d // NX, 0, d % NX) for d in range(1, NXY)]
+    early_units = [[groups[0].index((p, c)) for p in range(planes) if (p, c) in groups[0]] for c in range(3)]
+    late_units = [[groups[1].index((p, c)) for p in reversed(range(planes)) if (p, c) in groups[1]] for c in range(3)]
+    most = [max(len(u) for u in units) for units in (early_units, late_units)]
+    xy = xy_major_groups()[: dests // 2]
+    near = order.reshape(NZ, 2, -1)[:, 0].reshape(-1)
+    early_table = folded_z_table(cells, keep, np.concatenate([planes * xy + p for p in range(most[0])]))
+    late_table = folded_z_table(
+        cells, keep, np.concatenate([planes * near + planes - 1 - p for p in range(most[1])])
+    )
+    sums = VMEM((2, 2, 3, 2, keep // 2, lanes), jnp.float32)
+    result = VMEM((3 * keep * 4, lanes), jnp.float32)
     early = call(
-        functools.partial(early_kernel, keep),
+        functools.partial(early_kernel, keep, early_units),
         [(3 * keep * 4, lanes)],
-        2 * 6 * 2 * keep * 3 * dests * keep,
-        [
-            VMEM((kinds * dests, lanes), jnp.float32),
-            VMEM((3 * keep * 4, lanes), jnp.float32),
-            pltpu.SemaphoreType.DMA,
-        ],
+        4 * EARLY * keep * 3 * dests * keep,
+        [VMEM((kinds * dests, lanes), jnp.float32), sums, result, pltpu.SemaphoreType.DMA],
         [VMEM] * NXY + [pltpu.HBM, VMEM],
         limit=50 << 20,
-    )(
-        *spread,
-        velocity_modes.reshape(3 * keep * 4, lanes),
-        jnp.asarray(z_table(cells, keep, planes * xy_major_groups())),
-    )
-    near = order.reshape(NZ, 2, -1)[:, 0].reshape(-1)
-    rest = np.concatenate([planes * near + p for p in range(1, planes)])
-    table_z = jnp.asarray(folded_z_table(cells, keep, rest))
+    )(*spread, velocity_modes.reshape(3 * keep * 4, lanes), jnp.asarray(early_table))
     out = call(
-        functools.partial(z_kernel, planes - 1, keep),
+        functools.partial(z_kernel, keep, late_units),
         [(3 * keep * 4, lanes)],
-        6 * 2 * keep * 3 * (planes - 1) * dests * keep,
-        [
-            VMEM((2, 2, 3, 2, keep // 2, lanes), jnp.float32),
-            VMEM((3 * keep * 4, lanes), jnp.float32),
-            pltpu.SemaphoreType.DMA((6,)),
-        ],
+        4 * len(groups[1]) * keep * 3 * dests * keep,
+        [sums, result, pltpu.SemaphoreType.DMA((6,))],
         out_space=pltpu.HBM,
-    )(late.reshape(dests * per, lanes), early, table_z)
+    )(late.reshape(dests * per, lanes), early, jnp.asarray(late_table))
     return out.reshape(3, keep, rows_ky, 2, lanes)
 
 

time: 125 us -> 125 us (level)
  starting transfers between devices: 63.1 us -> 65.3 us
  waiting for transfers between devices: 45.9 us -> 44 us
    ppermute x22, starting transfers between devices: 47.4 us -> 49.5 us  [from_shift(): return lax.ppermute(value, GROUP, pairs)]
    ppermute x22, waiting for transfers between devices: 43.7 us -> 42.1 us  [from_shift(): return lax.ppermute(value, GROUP, pairs)]
  transfers between devices with their start and end apart: 25 -> 25, of which waited for: 8 -> 8; matrix products, arithmetic and copies ran while one was open for 0% -> 0% of each run, Pallas kernels for 4% -> 5%
where the time goes in v4:
time: 125 us
  starting transfers between devices  65.3 us (52%)
  waiting for transfers between devices  44 us (35%)
  Pallas kernels  15.3 us (12%)
    ppermute x22, starting transfers between devices, from_shift(): return lax.ppermute(value, GROUP, pairs)  49.5 us
    ppermute x22, waiting for transfers between devices, from_shift(): return lax.ppermute(value, GROUP, pairs)  42.1 us
    pallas_call x8, Pallas kernels, run(): pl.pallas_call(kernel, out_shape=shapes[0] if single else shapes, in_spec...  15.3 us
    all_to_all x1, starting transfers between devices, per_device(): lax.all_to_all(packed.reshape(dests, per // 4, 4, lanes), GROUP, 0, 0, ax...  15.1 us
  transfers between devices with their start and end apart: 25, of which 8 were waited for; matrix products, arithmetic and copies ran while one was open for 0% of the time, Pallas kernels for 5%

profile of v4, /device:TPU:32, one launch (start us, length us, event | category | flops | bytes accessed | tf_op | source)
XLA Modules:
  0.0 124.9 jit_solution(5065265165171996710)
XLA Ops:
  0.0 2.9 %shard_map.73 = (bf16[576,768]{1,0:T(8,128)(2,1)S(1)}, bf16[576,768]{1,0:T(8,128)(2,1)S(1)}, bf16[576,768]{1,0:T(8,128)(2,1)S(1)}) custom-call(f32[3,3,192,384]{3,2,1,0:T(8,128)} %v_hbm.1, f32[3,3,192,384]{3,2,1,0:T(8,128)} %w_hbm.1), custom_call_target="tpu_custom_call" | custom-call | flops 3981312 | bytes 10616832 | tf_op jit(solution)/shard_map/pallas_call | solution.py:296
  6.2 1.9 %collective-permute-done.1.got_ref = f32[768,256]{1,0:T(8,128)S(1)} collective-permute-done((f32[768,256]{1,0:T(8,128)S(1)}, f32[768,256]{1,0:T(8,128)S(1)}, u32[]{:S(2)}, u32[]{:S(2)}) %collective-permute-start.1) | collective-permute-done | bytes 786464 | tf_op jit(solution)/shard_map/ppermute | solution.py:352
  9.3 2.3 %shard_map.77 = f32[2560,128]{1,0:T(8,128)} custom-call(f32[960,256]{1,0:T(8,128)S(1)} %get-tuple-element.38.keep_ref, f32[960,256]{1,0:T(8,128)S(1)} %collective-permute-done.got_ref, bf16[2,2,256,192]{3,2,1,0:T(8,128)(2,1)S(1)} %copy-done, f32[256,128]{1,0:T(8,128)S(1)} %get-tuple-element.43._.refs_0_), custom_call_target="tpu_custom_call" | custom-call | flops 754974720 | bytes 3801088 | tf_op jit(solution)/shard_map/pallas_call | solution.py:296
  11.6 15.1 %all-to-all-start = ((f32[128,5,4,128]{3,2,1,0:T(4,128)}), f32[128,5,4,128]{3,2,1,0:T(4,128)S(1)}, u32[]{:S(2)}, u32[]{:S(2)}) async-start(f32[128,5,4,128]{3,2,1,0:T(4,128)} %bitcast), calls=%async_computation | async-start | bytes 2621440 | tf_op jit(solution)/shard_map/all_to_all | solution.py:368
  27.7 3.8 %collective-permute-start.3 = (f32[256,128]{1,0:T(8,128)S(1)}, f32[256,128]{1,0:T(8,128)S(1)}, u32[]{:S(2)}, u32[]{:S(2)}) collective-permute-start(f32[256,128]{1,0:T(8,128)S(1)} %get-tuple-element.45), channel_id=1, source_target_pairs={{16,0},{18,2},{20,4},{22,6},{24,8},{26,10},{28,12},{30,14},{32,16}... | collective-permute-start | bytes 393224 | tf_op jit(solution)/shard_map/ppermute | solution.py:320
  31.5 2.0 %collective-permute-start.4 = (f32[256,128]{1,0:T(8,128)S(1)}, f32[256,128]{1,0:T(8,128)S(1)}, u32[]{:S(2)}, u32[]{:S(2)}) collective-permute-start(f32[256,128]{1,0:T(8,128)S(1)} %get-tuple-element.46), channel_id=1, source_target_pairs={{24,0},{26,2},{28,4},{30,6},{32,8},{34,10},{36,12},{38,14},{40,16}... | collective-permute-start | bytes 393224 | tf_op jit(solution)/shard_map/ppermute | solution.py:320
  33.5 3.1 %collective-permute-start.5 = (f32[256,128]{1,0:T(8,128)S(1)}, f32[256,128]{1,0:T(8,128)S(1)}, u32[]{:S(2)}, u32[]{:S(2)}) collective-permute-start(f32[256,128]{1,0:T(8,128)S(1)} %get-tuple-element.47), channel_id=1, source_target_pairs={{32,0},{34,2},{36,4},{38,6},{40,8},{42,10},{44,12},{46,14},{48,16}... | collective-permute-start | bytes 393224 | tf_op jit(solution)/shard_map/ppermute | solution.py:320
  38.4 22.4 %collective-permute-done.2.refs_1_ = f32[256,128]{1,0:T(8,128)S(1)} collective-permute-done((f32[256,128]{1,0:T(8,128)S(1)}, f32[256,128]{1,0:T(8,128)S(1)}, u32[]{:S(2)}, u32[]{:S(2)}) %collective-permute-start.2) | collective-permute-done | bytes 131104 | tf_op jit(solution)/shard_map/ppermute | solution.py:320
  60.8 3.1 %collective-permute-start.7 = (f32[256,128]{1,0:T(8,128)S(1)}, f32[256,128]{1,0:T(8,128)S(1)}, u32[]{:S(2)}, u32[]{:S(2)}) collective-permute-start(f32[256,128]{1,0:T(8,128)S(1)} %get-tuple-element.49), channel_id=1, source_target_pairs={{48,0},{50,2},{52,4},{54,6},{56,8},{58,10},{60,12},{62,14},{0,16},... | collective-permute-start | bytes 393224 | tf_op jit(solution)/shard_map/ppermute | solution.py:320
  65.2 6.2 %collective-permute-start.8 = (f32[256,128]{1,0:T(8,128)S(1)}, f32[256,128]{1,0:T(8,128)S(1)}, u32[]{:S(2)}, u32[]{:S(2)}) collective-permute-start(f32[256,128]{1,0:T(8,128)S(1)} %get-tuple-element.50), channel_id=1, source_target_pairs={{56,0},{58,2},{60,4},{62,6},{0,8},{2,10},{4,12},{6,14},{8,16},{10,... | collective-permute-start | bytes 393224 | tf_op jit(solution)/shard_map/ppermute | solution.py:320
  71.4 3.8 %collective-permute-done.4.refs_3_ = f32[256,128]{1,0:T(8,128)S(1)} collective-permute-done((f32[256,128]{1,0:T(8,128)S(1)}, f32[256,128]{1,0:T(8,128)S(1)}, u32[]{:S(2)}, u32[]{:S(2)}) %collective-permute-start.4) | collective-permute-done | bytes 131104 | tf_op jit(solution)/shard_map/ppermute | solution.py:320
  75.2 7.0 %collective-permute-done.5.refs_4_ = f32[256,128]{1,0:T(8,128)S(1)} collective-permute-done((f32[256,128]{1,0:T(8,128)S(1)}, f32[256,128]{1,0:T(8,128)S(1)}, u32[]{:S(2)}, u32[]{:S(2)}) %collective-permute-start.5) | collective-permute-done | bytes 131104 | tf_op jit(solution)/shard_map/ppermute | solution.py:320
  82.8 2.8 %collective-permute-start.9 = (f32[128,128]{1,0:T(8,128)S(1)}, f32[128,128]{1,0:T(8,128)S(1)}, u32[]{:S(2)}, u32[]{:S(2)}) collective-permute-start(f32[128,128]{1,0:T(8,128)S(1)} %get-tuple-element.52), channel_id=1, source_target_pairs={{2,0},{4,2},{6,4},{0,6},{10,8},{12,10},{14,12},{8,14},{18,16},{20,... | collective-permute-start | bytes 196616 | tf_op jit(solution)/shard_map/ppermute | solution.py:320
  87.3 2.8 %collective-permute-start.12 = (f32[128,128]{1,0:T(8,128)S(1)}, f32[128,128]{1,0:T(8,128)S(1)}, u32[]{:S(2)}, u32[]{:S(2)}) collective-permute-start(f32[128,128]{1,0:T(8,128)S(1)} %get-tuple-element.55), channel_id=1, source_target_pairs={{64,0},{66,2},{68,4},{70,6},{72,8},{74,10},{76,12},{78,14},{80,16}... | collective-permute-start | bytes 196616 | tf_op jit(solution)/shard_map/ppermute | solution.py:320
  90.1 2.6 %collective-permute-start.13 = (f32[128,128]{1,0:T(8,128)S(1)}, f32[128,128]{1,0:T(8,128)S(1)}, u32[]{:S(2)}, u32[]{:S(2)}) collective-permute-start(f32[128,128]{1,0:T(8,128)S(1)} %get-tuple-element.56), channel_id=1, source_target_pairs={{66,0},{68,2},{70,4},{64,6},{74,8},{76,10},{78,12},{72,14},{82,16}... | collective-permute-start | bytes 196616 | tf_op jit(solution)/shard_map/ppermute | solution.py:320
  94.6 2.4 %collective-permute-start.16 = (f32[128,128]{1,0:T(8,128)S(1)}, f32[128,128]{1,0:T(8,128)S(1)}, u32[]{:S(2)}, u32[]{:S(2)}) collective-permute-start(f32[128,128]{1,0:T(8,128)S(1)} %get-tuple-element.59), channel_id=1, source_target_pairs={{128,0},{130,2},{132,4},{134,6},{136,8},{138,10},{140,12},{142,14}... | collective-permute-start | bytes 196616 | tf_op jit(solution)/shard_map/ppermute | solution.py:320
  97.0 3.4 %collective-permute-start.17 = (f32[128,128]{1,0:T(8,128)S(1)}, f32[128,128]{1,0:T(8,128)S(1)}, u32[]{:S(2)}, u32[]{:S(2)}) collective-permute-start(f32[128,128]{1,0:T(8,128)S(1)} %get-tuple-element.60), channel_id=1, source_target_pairs={{130,0},{132,2},{134,4},{128,6},{138,8},{140,10},{142,12},{136,14}... | collective-permute-start | bytes 196616 | tf_op jit(solution)/shard_map/ppermute | solution.py:320
  100.4 3.3 %collective-permute-start.18 = (f32[128,128]{1,0:T(8,128)S(1)}, f32[128,128]{1,0:T(8,128)S(1)}, u32[]{:S(2)}, u32[]{:S(2)}) collective-permute-start(f32[128,128]{1,0:T(8,128)S(1)} %get-tuple-element.61), channel_id=1, source_target_pairs={{132,0},{134,2},{128,4},{130,6},{140,8},{142,10},{136,12},{138,14}... | collective-permute-start | bytes 196616 | tf_op jit(solution)/shard_map/ppermute | solution.py:320
  104.8 4.5 %collective-permute-start.21 = (f32[128,128]{1,0:T(8,128)S(1)}, f32[128,128]{1,0:T(8,128)S(1)}, u32[]{:S(2)}, u32[]{:S(2)}) collective-permute-start(f32[128,128]{1,0:T(8,128)S(1)} %get-tuple-element.64), channel_id=1, source_target_pairs={{194,0},{196,2},{198,4},{192,6},{202,8},{204,10},{206,12},{200,14}... | collective-permute-start | bytes 196616 | tf_op jit(solution)/shard_map/ppermute | solution.py:320
  109.3 2.1 %collective-permute-start.22 = (f32[128,128]{1,0:T(8,128)S(1)}, f32[128,128]{1,0:T(8,128)S(1)}, u32[]{:S(2)}, u32[]{:S(2)}) collective-permute-start(f32[128,128]{1,0:T(8,128)S(1)} %get-tuple-element.65), channel_id=1, source_target_pairs={{196,0},{198,2},{192,4},{194,6},{204,8},{206,10},{200,12},{202,14}... | collective-permute-start | bytes 196616 | tf_op jit(solution)/shard_map/ppermute | solution.py:320
  113.0 4.2 %collective-permute-done.22.refs_14_ = f32[128,128]{1,0:T(8,128)S(1)} collective-permute-done((f32[128,128]{1,0:T(8,128)S(1)}, f32[128,128]{1,0:T(8,128)S(1)}, u32[]{:S(2)}, u32[]{:S(2)}) %collective-permute-start.22) | collective-permute-done | bytes 65568 | tf_op jit(solution)/shard_map/ppermute | solution.py:320
  117.2 1.8 %collective-permute-done.23.refs_15_ = f32[128,128]{1,0:T(8,128)S(1)} collective-permute-done((f32[128,128]{1,0:T(8,128)S(1)}, f32[128,128]{1,0:T(8,128)S(1)}, u32[]{:S(2)}, u32[]{:S(2)}) %collective-permute-start.23) | collective-permute-done | bytes 65568 | tf_op jit(solution)/shard_map/ppermute | solution.py:320
  119.0 3.2 %shard_map.79.early_ref = f32[3072,128]{1,0:T(8,128)S(1)} custom-call(f32[128,128]{1,0:T(8,128)S(1)} %get-tuple-element.51.refs_0_, f32[128,128]{1,0:T(8,128)S(1)} %collective-permute-done.9.refs_1_, f32[128,128]{1,0:T(8,128)S(1)} %collective-permute-done.10.refs_2_, f32[128,128]{1,0:T(8,128)S(1)} %collective-permute-done.11.refs_3_, ...), custom_call_target="tpu_custom_call" | custom-call | flops 402653184 | bytes 4456448 | tf_op jit(solution)/shard_map/pallas_call | solution.py:296
  122.2 2.6 %shard_map.80 = f32[3072,128]{1,0:T(8,128)} custom-call(f32[2560,128]{1,0:T(8,128)S(1)} %bitcast.4, f32[3072,128]{1,0:T(8,128)S(1)} %shard_map.79.early_ref, bf16[2,2,256,128]{3,2,1,0:T(8,128)(2,1)S(1)} %copy-done.1), custom_call_target="tpu_custom_call" | custom-call | flops 503316480 | bytes 4718592 | tf_op jit(solution)/shard_map/pallas_call | solution.py:296
  (42 shorter events, 15.4 us)
Async XLA Ops:
  4.4 4.9 %collective-permute-start = (f32[960,256]{1,0:T(8,128)S(1)}, f32[960,256]{1,0:T(8,128)S(1)}, u32[]{:S(2)}, u32[]{:S(2)}) collective-permute-start(f32[960,256]{1,0:T(8,128)S(1)} %get-tuple-element.39), channel_id=1, source_target_pairs={{0,1},{1,0},{2,3},{3,2},{4,5},{5,4},{6,7},{7,6},{8,9},{9,8},{10,11... | collective-permute-start | bytes 2949128 | tf_op jit(solution)/shard_map/ppermute | solution.py:352
  11.6 110.6 %all-to-all-start = ((f32[128,5,4,128]{3,2,1,0:T(4,128)}), f32[128,5,4,128]{3,2,1,0:T(4,128)S(1)}, u32[]{:S(2)}, u32[]{:S(2)}) async-start(f32[128,5,4,128]{3,2,1,0:T(4,128)} %bitcast), calls=%async_computation | async-start | bytes 2621440 | tf_op jit(solution)/shard_map/all_to_all | solution.py:368
  26.7 34.1 %collective-permute-start.2 = (f32[256,128]{1,0:T(8,128)S(1)}, f32[256,128]{1,0:T(8,128)S(1)}, u32[]{:S(2)}, u32[]{:S(2)}) collective-permute-start(f32[256,128]{1,0:T(8,128)S(1)} %get-tuple-element.44), channel_id=1, source_target_pairs={{8,0},{10,2},{12,4},{14,6},{16,8},{18,10},{20,12},{22,14},{24,16},... | collective-permute-start | bytes 393224 | tf_op jit(solution)/shard_map/ppermute | solution.py:320
  27.7 37.5 %collective-permute-start.3 = (f32[256,128]{1,0:T(8,128)S(1)}, f32[256,128]{1,0:T(8,128)S(1)}, u32[]{:S(2)}, u32[]{:S(2)}) collective-permute-start(f32[256,128]{1,0:T(8,128)S(1)} %get-tuple-element.45), channel_id=1, source_target_pairs={{16,0},{18,2},{20,4},{22,6},{24,8},{26,10},{28,12},{30,14},{32,16}... | collective-permute-start | bytes 393224 | tf_op jit(solution)/shard_map/ppermute | solution.py:320
  31.5 43.7 %collective-permute-start.4 = (f32[256,128]{1,0:T(8,128)S(1)}, f32[256,128]{1,0:T(8,128)S(1)}, u32[]{:S(2)}, u32[]{:S(2)}) collective-permute-start(f32[256,128]{1,0:T(8,128)S(1)} %get-tuple-element.46), channel_id=1, source_target_pairs={{24,0},{26,2},{28,4},{30,6},{32,8},{34,10},{36,12},{38,14},{40,16}... | collective-permute-start | bytes 393224 | tf_op jit(solution)/shard_map/ppermute | solution.py:320
  33.5 48.7 %collective-permute-start.5 = (f32[256,128]{1,0:T(8,128)S(1)}, f32[256,128]{1,0:T(8,128)S(1)}, u32[]{:S(2)}, u32[]{:S(2)}) collective-permute-start(f32[256,128]{1,0:T(8,128)S(1)} %get-tuple-element.47), channel_id=1, source_target_pairs={{32,0},{34,2},{36,4},{38,6},{40,8},{42,10},{44,12},{46,14},{48,16}... | collective-permute-start | bytes 393224 | tf_op jit(solution)/shard_map/ppermute | solution.py:320
  36.6 45.6 %collective-permute-start.6 = (f32[256,128]{1,0:T(8,128)S(1)}, f32[256,128]{1,0:T(8,128)S(1)}, u32[]{:S(2)}, u32[]{:S(2)}) collective-permute-start(f32[256,128]{1,0:T(8,128)S(1)} %get-tuple-element.48), channel_id=1, source_target_pairs={{40,0},{42,2},{44,4},{46,6},{48,8},{50,10},{52,12},{54,14},{56,16}... | collective-permute-start | bytes 393224 | tf_op jit(solution)/shard_map/ppermute | solution.py:320
  60.8 21.4 %collective-permute-start.7 = (f32[256,128]{1,0:T(8,128)S(1)}, f32[256,128]{1,0:T(8,128)S(1)}, u32[]{:S(2)}, u32[]{:S(2)}) collective-permute-start(f32[256,128]{1,0:T(8,128)S(1)} %get-tuple-element.49), channel_id=1, source_target_pairs={{48,0},{50,2},{52,4},{54,6},{56,8},{58,10},{60,12},{62,14},{0,16},... | collective-permute-start | bytes 393224 | tf_op jit(solution)/shard_map/ppermute | solution.py:320
  65.2 17.0 %collective-permute-start.8 = (f32[256,128]{1,0:T(8,128)S(1)}, f32[256,128]{1,0:T(8,128)S(1)}, u32[]{:S(2)}, u32[]{:S(2)}) collective-permute-start(f32[256,128]{1,0:T(8,128)S(1)} %get-tuple-element.50), channel_id=1, source_target_pairs={{56,0},{58,2},{60,4},{62,6},{0,8},{2,10},{4,12},{6,14},{8,16},{10,... | collective-permute-start | bytes 393224 | tf_op jit(solution)/shard_map/ppermute | solution.py:320
  82.8 9.9 %collective-permute-start.9 = (f32[128,128]{1,0:T(8,128)S(1)}, f32[128,128]{1,0:T(8,128)S(1)}, u32[]{:S(2)}, u32[]{:S(2)}) collective-permute-start(f32[128,128]{1,0:T(8,128)S(1)} %get-tuple-element.52), channel_id=1, source_target_pairs={{2,0},{4,2},{6,4},{0,6},{10,8},{12,10},{14,12},{8,14},{18,16},{20,... | collective-permute-start | bytes 196616 | tf_op jit(solution)/shard_map/ppermute | solution.py:320
  85.6 8.6 %collective-permute-start.10 = (f32[128,128]{1,0:T(8,128)S(1)}, f32[128,128]{1,0:T(8,128)S(1)}, u32[]{:S(2)}, u32[]{:S(2)}) collective-permute-start(f32[128,128]{1,0:T(8,128)S(1)} %get-tuple-element.53), channel_id=1, source_target_pairs={{4,0},{6,2},{0,4},{2,6},{12,8},{14,10},{8,12},{10,14},{20,16},{22,... | collective-permute-start | bytes 196616 | tf_op jit(solution)/shard_map/ppermute | solution.py:320
  86.5 8.1 %collective-permute-start.11 = (f32[128,128]{1,0:T(8,128)S(1)}, f32[128,128]{1,0:T(8,128)S(1)}, u32[]{:S(2)}, u32[]{:S(2)}) collective-permute-start(f32[128,128]{1,0:T(8,128)S(1)} %get-tuple-element.54), channel_id=1, source_target_pairs={{6,0},{0,2},{2,4},{4,6},{14,8},{8,10},{10,12},{12,14},{22,16},{16,... | collective-permute-start | bytes 196616 | tf_op jit(solution)/shard_map/ppermute | solution.py:320
  87.3 9.7 %collective-permute-start.12 = (f32[128,128]{1,0:T(8,128)S(1)}, f32[128,128]{1,0:T(8,128)S(1)}, u32[]{:S(2)}, u32[]{:S(2)}) collective-permute-start(f32[128,128]{1,0:T(8,128)S(1)} %get-tuple-element.55), channel_id=1, source_target_pairs={{64,0},{66,2},{68,4},{70,6},{72,8},{74,10},{76,12},{78,14},{80,16}... | collective-permute-start | bytes 196616 | tf_op jit(solution)/shard_map/ppermute | solution.py:320
  90.1 10.3 %collective-permute-start.13 = (f32[128,128]{1,0:T(8,128)S(1)}, f32[128,128]{1,0:T(8,128)S(1)}, u32[]{:S(2)}, u32[]{:S(2)}) collective-permute-start(f32[128,128]{1,0:T(8,128)S(1)} %get-tuple-element.56), channel_id=1, source_target_pairs={{66,0},{68,2},{70,4},{64,6},{74,8},{76,10},{78,12},{72,14},{82,16}... | collective-permute-start | bytes 196616 | tf_op jit(solution)/shard_map/ppermute | solution.py:320
  92.7 10.9 %collective-permute-start.14 = (f32[128,128]{1,0:T(8,128)S(1)}, f32[128,128]{1,0:T(8,128)S(1)}, u32[]{:S(2)}, u32[]{:S(2)}) collective-permute-start(f32[128,128]{1,0:T(8,128)S(1)} %get-tuple-element.57), channel_id=1, source_target_pairs={{68,0},{70,2},{64,4},{66,6},{76,8},{78,10},{72,12},{74,14},{84,16}... | collective-permute-start | bytes 196616 | tf_op jit(solution)/shard_map/ppermute | solution.py:320
  94.2 9.6 %collective-permute-start.15 = (f32[128,128]{1,0:T(8,128)S(1)}, f32[128,128]{1,0:T(8,128)S(1)}, u32[]{:S(2)}, u32[]{:S(2)}) collective-permute-start(f32[128,128]{1,0:T(8,128)S(1)} %get-tuple-element.58), channel_id=1, source_target_pairs={{70,0},{64,2},{66,4},{68,6},{78,8},{72,10},{74,12},{76,14},{86,16}... | collective-permute-start | bytes 196616 | tf_op jit(solution)/shard_map/ppermute | solution.py:320
  94.6 10.2 %collective-permute-start.16 = (f32[128,128]{1,0:T(8,128)S(1)}, f32[128,128]{1,0:T(8,128)S(1)}, u32[]{:S(2)}, u32[]{:S(2)}) collective-permute-start(f32[128,128]{1,0:T(8,128)S(1)} %get-tuple-element.59), channel_id=1, source_target_pairs={{128,0},{130,2},{132,4},{134,6},{136,8},{138,10},{140,12},{142,14}... | collective-permute-start | bytes 196616 | tf_op jit(solution)/shard_map/ppermute | solution.py:320
  97.0 12.3 %collective-permute-start.17 = (f32[128,128]{1,0:T(8,128)S(1)}, f32[128,128]{1,0:T(8,128)S(1)}, u32[]{:S(2)}, u32[]{:S(2)}) collective-permute-start(f32[128,128]{1,0:T(8,128)S(1)} %get-tuple-element.60), channel_id=1, source_target_pairs={{130,0},{132,2},{134,4},{128,6},{138,8},{140,10},{142,12},{136,14}... | collective-permute-start | bytes 196616 | tf_op jit(solution)/shard_map/ppermute | solution.py:320
  100.4 11.0 %collective-permute-start.18 = (f32[128,128]{1,0:T(8,128)S(1)}, f32[128,128]{1,0:T(8,128)S(1)}, u32[]{:S(2)}, u32[]{:S(2)}) collective-permute-start(f32[128,128]{1,0:T(8,128)S(1)} %get-tuple-element.61), channel_id=1, source_target_pairs={{132,0},{134,2},{128,4},{130,6},{140,8},{142,10},{136,12},{138,14}... | collective-permute-start | bytes 196616 | tf_op jit(solution)/shard_map/ppermute | solution.py:320
  103.7 9.3 %collective-permute-start.19 = (f32[128,128]{1,0:T(8,128)S(1)}, f32[128,128]{1,0:T(8,128)S(1)}, u32[]{:S(2)}, u32[]{:S(2)}) collective-permute-start(f32[128,128]{1,0:T(8,128)S(1)} %get-tuple-element.62), channel_id=1, source_target_pairs={{134,0},{128,2},{130,4},{132,6},{142,8},{136,10},{138,12},{140,14}... | collective-permute-start | bytes 196616 | tf_op jit(solution)/shard_map/ppermute | solution.py:320
  103.8 9.2 %collective-permute-start.20 = (f32[128,128]{1,0:T(8,128)S(1)}, f32[128,128]{1,0:T(8,128)S(1)}, u32[]{:S(2)}, u32[]{:S(2)}) collective-permute-start(f32[128,128]{1,0:T(8,128)S(1)} %get-tuple-element.63), channel_id=1, source_target_pairs={{192,0},{194,2},{196,4},{198,6},{200,8},{202,10},{204,12},{206,14}... | collective-permute-start | bytes 196616 | tf_op jit(solution)/shard_map/ppermute | solution.py:320
  104.8 8.2 %collective-permute-start.21 = (f32[128,128]{1,0:T(8,128)S(1)}, f32[128,128]{1,0:T(8,128)S(1)}, u32[]{:S(2)}, u32[]{:S(2)}) collective-permute-start(f32[128,128]{1,0:T(8,128)S(1)} %get-tuple-element.64), channel_id=1, source_target_pairs={{194,0},{196,2},{198,4},{192,6},{202,8},{204,10},{206,12},{200,14}... | collective-permute-start | bytes 196616 | tf_op jit(solution)/shard_map/ppermute | solution.py:320
  109.3 7.9 %collective-permute-start.22 = (f32[128,128]{1,0:T(8,128)S(1)}, f32[128,128]{1,0:T(8,128)S(1)}, u32[]{:S(2)}, u32[]{:S(2)}) collective-permute-start(f32[128,128]{1,0:T(8,128)S(1)} %get-tuple-element.65), channel_id=1, source_target_pairs={{196,0},{198,2},{192,4},{194,6},{204,8},{206,10},{200,12},{202,14}... | collective-permute-start | bytes 196616 | tf_op jit(solution)/shard_map/ppermute | solution.py:320
  111.4 7.6 %collective-permute-start.23 = (f32[128,128]{1,0:T(8,128)S(1)}, f32[128,128]{1,0:T(8,128)S(1)}, u32[]{:S(2)}, u32[]{:S(2)}) collective-permute-start(f32[128,128]{1,0:T(8,128)S(1)} %get-tuple-element.66), channel_id=1, source_target_pairs={{198,0},{192,2},{194,4},{196,6},{206,8},{200,10},{202,12},{204,14}... | collective-permute-start | bytes 196616 | tf_op jit(solution)/shard_map/ppermute | solution.py:320
  (5 other events, 119.7 us)

commit v5 on v3

--- a/solution.py
+++ b/solution.py
@@ -212,9 +212,13 @@
 
 
 def early_kernel(keep, *refs):
-    gots, (modes_hbm, table_ref, out_ref, all_ref, modes_ref, sem) = refs[:NXY], refs[NXY:]
-    copy = pltpu.make_async_copy(modes_hbm, modes_ref, sem)
-    copy.start()
+    gots, (modes_hbm, table_ref, out_ref, all_ref, modes_ref, sems) = refs[:NXY], refs[NXY:]
+    copies = []
+    part = modes_ref.shape[0] // sems.shape[0]
+    for i in range(sems.shape[0]):
+        rows = pl.ds(i * part, part)
+        copies.append(pltpu.make_async_copy(modes_hbm.at[rows], modes_ref.at[rows], sems.at[i]))
+        copies[-1].start()
     y, _, x = place()
     lanes = out_ref.shape[1]
     kinds = gots[0].shape[0] // NZ
@@ -225,17 +229,21 @@
             for k in range(kinds):
                 at = pl.multiple_of(k * sources + source * NZ, NZ)
                 all_ref[pl.ds(at, NZ), :] = gots[dy * NX + dx][pl.ds(k, NZ, kinds), :]
-    copy.wait()
-    for parity, waves, mask, inverse, damp in wave_numbers(keep, lanes, 0, keep, 1):
-        sums = []
+    sums = []
+    for parity in range(2):
         for c in range(3):
             base = c * 4 + parity * 2
             both = [all_ref[(base + q) * sources : (base + q + 1) * sources] for q in range(2)]
             sums.append(z_sums(keep, lanes, table_ref, jnp.concatenate(both, axis=1)))
+    for copy in copies:
+        copy.wait()
+    for parity, waves, mask, inverse, damp in wave_numbers(keep, lanes, 0, keep, 1):
         for q in range(2):
-            for c, value in enumerate(projected([s[q] for s in sums], waves, mask, inverse)):
+            s = [sums[parity * 3 + c][q] for c in range(3)]
+            for c, value in enumerate(projected(s, waves, mask, inverse)):
                 where = pl.ds(c * keep * 4 + parity * 2 + q, keep, 4)
-                out_ref[where, :] = value - damp * modes_ref[where, :]
+                at = ((c * 2 + parity) * 2 + q) * keep
+                out_ref[at : at + keep] = value - damp * modes_ref[where, :]
 
 
 def z_kernel(planes, keep, x_ref, early_ref, table_ref, out_hbm, sums_ref, out_ref, sems):
@@ -267,7 +275,8 @@
                     values = projected([sums_ref[parity, q, c, e, here] for c in range(3)], waves, mask, inverse)
                     for c, value in enumerate(values):
                         where = pl.ds((c * keep + h * part * 2 + e) * 4 + parity * 2 + q, part, 8)
-                        out_ref[where, :] = value + early_ref[where, :]
+                        at = ((c * 2 + parity) * 2 + q) * keep + h * part * 2 + e
+                        out_ref[where, :] = value + early_ref[pl.ds(at, part, 2), :]
         for c in range(3):
             rows = pl.ds((c * keep + h * part * 2) * 4, part * 8)
             copies.append(pltpu.make_async_copy(out_ref.at[rows], out_hbm.at[rows], sems.at[h * 3 + c]))
@@ -359,7 +368,7 @@
         [
             VMEM((kinds * dests, lanes), jnp.float32),
             VMEM((3 * keep * 4, lanes), jnp.float32),
-            pltpu.SemaphoreType.DMA,
+            pltpu.SemaphoreType.DMA((6,)),
         ],
         [VMEM] * NXY + [pltpu.HBM, VMEM],
         limit=50 << 20,

time: 125 us -> 126 us (level)
  no operation moved by 1% of the time
where the time goes in v5:
time: 126 us; the launch traced here: 125 us
  starting transfers between devices  63.1 us (50%)
  waiting for transfers between devices  45.9 us (36%)
  Pallas kernels  15 us (12%)
    ppermute x22, starting transfers between devices, from_shift(): return lax.ppermute(value, GROUP, pairs)  47.4 us
    ppermute x22, waiting for transfers between devices, from_shift(): return lax.ppermute(value, GROUP, pairs)  43.7 us
    pallas_call x8, Pallas kernels, run(): pl.pallas_call(kernel, out_shape=shapes[0] if single else shapes, in_spec...  15 us
    all_to_all x1, starting transfers between devices, per_device(): lax.all_to_all(packed.reshape(dests, per, lanes), GROUP, 0, 0, axis_index...  15 us
  transfers between devices with their start and end apart: 25, of which 8 were waited for; matrix products, arithmetic and copies ran while one was open for 0% of the time, Pallas kernels for 4%

profile of v5, /device:TPU:32, one launch (start us, length us, event | category | flops | bytes accessed | tf_op | source)
XLA Modules:
  0.0 125.3 jit_solution(8082066141096995475)
XLA Ops:
  0.0 2.9 %shard_map.73 = (bf16[576,768]{1,0:T(8,128)(2,1)S(1)}, bf16[576,768]{1,0:T(8,128)(2,1)S(1)}, bf16[576,768]{1,0:T(8,128)(2,1)S(1)}) custom-call(f32[3,3,192,384]{3,2,1,0:T(8,128)} %v_hbm.1, f32[3,3,192,384]{3,2,1,0:T(8,128)} %w_hbm.1), custom_call_target="tpu_custom_call" | custom-call | flops 3981312 | bytes 10616832 | tf_op jit(solution)/shard_map/pallas_call | solution.py:294
  6.3 2.2 %collective-permute-done.1.got_ref = f32[576,256]{1,0:T(8,128)S(1)} collective-permute-done((f32[576,256]{1,0:T(8,128)S(1)}, f32[576,256]{1,0:T(8,128)S(1)}, u32[]{:S(2)}, u32[]{:S(2)}) %collective-permute-start.1) | collective-permute-done | bytes 589856 | tf_op jit(solution)/shard_map/ppermute | solution.py:343
  9.3 2.7 %shard_map.77 = f32[3072,128]{1,0:T(8,128)} custom-call(f32[1152,256]{1,0:T(8,128)S(1)} %get-tuple-element.38.keep_ref, f32[1152,256]{1,0:T(8,128)S(1)} %collective-permute-done.got_ref, bf16[2,2,256,192]{3,2,1,0:T(8,128)(2,1)S(1)} %copy-done, f32[192,128]{1,0:T(8,128)S(1)} %get-tuple-element.43._.refs_0_), custom_call_target="tpu_custom_call" | custom-call | flops 905969664 | bytes 4423680 | tf_op jit(solution)/shard_map/pallas_call | solution.py:294
  12.0 15.0 %all-to-all-start = ((f32[128,24,128]{2,1,0:T(8,128)}), f32[128,24,128]{2,1,0:T(8,128)S(1)}, u32[]{:S(2)}, u32[]{:S(2)}) async-start(f32[128,24,128]{2,1,0:T(8,128)} %bitcast), calls=%async_computation | async-start | bytes 3145728 | tf_op jit(solution)/shard_map/all_to_all | solution.py:359
  28.0 3.8 %collective-permute-start.3 = (f32[192,128]{1,0:T(8,128)S(1)}, f32[192,128]{1,0:T(8,128)S(1)}, u32[]{:S(2)}, u32[]{:S(2)}) collective-permute-start(f32[192,128]{1,0:T(8,128)S(1)} %get-tuple-element.45), channel_id=1, source_target_pairs={{16,0},{18,2},{20,4},{22,6},{24,8},{26,10},{28,12},{30,14},{32,16}... | collective-permute-start | bytes 294920 | tf_op jit(solution)/shard_map/ppermute | solution.py:318
  31.7 2.0 %collective-permute-start.4 = (f32[192,128]{1,0:T(8,128)S(1)}, f32[192,128]{1,0:T(8,128)S(1)}, u32[]{:S(2)}, u32[]{:S(2)}) collective-permute-start(f32[192,128]{1,0:T(8,128)S(1)} %get-tuple-element.46), channel_id=1, source_target_pairs={{24,0},{26,2},{28,4},{30,6},{32,8},{34,10},{36,12},{38,14},{40,16}... | collective-permute-start | bytes 294920 | tf_op jit(solution)/shard_map/ppermute | solution.py:318
  33.8 3.1 %collective-permute-start.5 = (f32[192,128]{1,0:T(8,128)S(1)}, f32[192,128]{1,0:T(8,128)S(1)}, u32[]{:S(2)}, u32[]{:S(2)}) collective-permute-start(f32[192,128]{1,0:T(8,128)S(1)} %get-tuple-element.47), channel_id=1, source_target_pairs={{32,0},{34,2},{36,4},{38,6},{40,8},{42,10},{44,12},{46,14},{48,16}... | collective-permute-start | bytes 294920 | tf_op jit(solution)/shard_map/ppermute | solution.py:318
  38.7 28.5 %collective-permute-done.2.refs_1_ = f32[192,128]{1,0:T(8,128)S(1)} collective-permute-done((f32[192,128]{1,0:T(8,128)S(1)}, f32[192,128]{1,0:T(8,128)S(1)}, u32[]{:S(2)}, u32[]{:S(2)}) %collective-permute-start.2) | collective-permute-done | bytes 98336 | tf_op jit(solution)/shard_map/ppermute | solution.py:318
  67.2 1.8 %collective-permute-start.7 = (f32[192,128]{1,0:T(8,128)S(1)}, f32[192,128]{1,0:T(8,128)S(1)}, u32[]{:S(2)}, u32[]{:S(2)}) collective-permute-start(f32[192,128]{1,0:T(8,128)S(1)} %get-tuple-element.49), channel_id=1, source_target_pairs={{48,0},{50,2},{52,4},{54,6},{56,8},{58,10},{60,12},{62,14},{0,16},... | collective-permute-start | bytes 294920 | tf_op jit(solution)/shard_map/ppermute | solution.py:318
  69.4 5.1 %collective-permute-start.8 = (f32[192,128]{1,0:T(8,128)S(1)}, f32[192,128]{1,0:T(8,128)S(1)}, u32[]{:S(2)}, u32[]{:S(2)}) collective-permute-start(f32[192,128]{1,0:T(8,128)S(1)} %get-tuple-element.50), channel_id=1, source_target_pairs={{56,0},{58,2},{60,4},{62,6},{0,8},{2,10},{4,12},{6,14},{8,16},{10,... | collective-permute-start | bytes 294920 | tf_op jit(solution)/shard_map/ppermute | solution.py:318
  74.5 2.9 %collective-permute-done.4.refs_3_ = f32[192,128]{1,0:T(8,128)S(1)} collective-permute-done((f32[192,128]{1,0:T(8,128)S(1)}, f32[192,128]{1,0:T(8,128)S(1)}, u32[]{:S(2)}, u32[]{:S(2)}) %collective-permute-start.4) | collective-permute-done | bytes 98336 | tf_op jit(solution)/shard_map/ppermute | solution.py:318
  77.4 4.5 %collective-permute-done.5.refs_4_ = f32[192,128]{1,0:T(8,128)S(1)} collective-permute-done((f32[192,128]{1,0:T(8,128)S(1)}, f32[192,128]{1,0:T(8,128)S(1)}, u32[]{:S(2)}, u32[]{:S(2)}) %collective-permute-start.5) | collective-permute-done | bytes 98336 | tf_op jit(solution)/shard_map/ppermute | solution.py:318
  82.4 3.1 %collective-permute-start.9 = (f32[96,128]{1,0:T(8,128)S(1)}, f32[96,128]{1,0:T(8,128)S(1)}, u32[]{:S(2)}, u32[]{:S(2)}) collective-permute-start(f32[96,128]{1,0:T(8,128)S(1)} %get-tuple-element.52), channel_id=1, source_target_pairs={{2,0},{4,2},{6,4},{0,6},{10,8},{12,10},{14,12},{8,14},{18,16},{20,... | collective-permute-start | bytes 147464 | tf_op jit(solution)/shard_map/ppermute | solution.py:318
  87.2 2.8 %collective-permute-start.12 = (f32[96,128]{1,0:T(8,128)S(1)}, f32[96,128]{1,0:T(8,128)S(1)}, u32[]{:S(2)}, u32[]{:S(2)}) collective-permute-start(f32[96,128]{1,0:T(8,128)S(1)} %get-tuple-element.55), channel_id=1, source_target_pairs={{64,0},{66,2},{68,4},{70,6},{72,8},{74,10},{76,12},{78,14},{80,16}... | collective-permute-start | bytes 147464 | tf_op jit(solution)/shard_map/ppermute | solution.py:318
  90.0 2.6 %collective-permute-start.13 = (f32[96,128]{1,0:T(8,128)S(1)}, f32[96,128]{1,0:T(8,128)S(1)}, u32[]{:S(2)}, u32[]{:S(2)}) collective-permute-start(f32[96,128]{1,0:T(8,128)S(1)} %get-tuple-element.56), channel_id=1, source_target_pairs={{66,0},{68,2},{70,4},{64,6},{74,8},{76,10},{78,12},{72,14},{82,16}... | collective-permute-start | bytes 147464 | tf_op jit(solution)/shard_map/ppermute | solution.py:318
  94.1 2.8 %collective-permute-start.16 = (f32[96,128]{1,0:T(8,128)S(1)}, f32[96,128]{1,0:T(8,128)S(1)}, u32[]{:S(2)}, u32[]{:S(2)}) collective-permute-start(f32[96,128]{1,0:T(8,128)S(1)} %get-tuple-element.59), channel_id=1, source_target_pairs={{128,0},{130,2},{132,4},{134,6},{136,8},{138,10},{140,12},{142,14}... | collective-permute-start | bytes 147464 | tf_op jit(solution)/shard_map/ppermute | solution.py:318
  96.9 3.4 %collective-permute-start.17 = (f32[96,128]{1,0:T(8,128)S(1)}, f32[96,128]{1,0:T(8,128)S(1)}, u32[]{:S(2)}, u32[]{:S(2)}) collective-permute-start(f32[96,128]{1,0:T(8,128)S(1)} %get-tuple-element.60), channel_id=1, source_target_pairs={{130,0},{132,2},{134,4},{128,6},{138,8},{140,10},{142,12},{136,14}... | collective-permute-start | bytes 147464 | tf_op jit(solution)/shard_map/ppermute | solution.py:318
  100.2 3.3 %collective-permute-start.18 = (f32[96,128]{1,0:T(8,128)S(1)}, f32[96,128]{1,0:T(8,128)S(1)}, u32[]{:S(2)}, u32[]{:S(2)}) collective-permute-start(f32[96,128]{1,0:T(8,128)S(1)} %get-tuple-element.61), channel_id=1, source_target_pairs={{132,0},{134,2},{128,4},{130,6},{140,8},{142,10},{136,12},{138,14}... | collective-permute-start | bytes 147464 | tf_op jit(solution)/shard_map/ppermute | solution.py:318
  104.6 4.5 %collective-permute-start.21 = (f32[96,128]{1,0:T(8,128)S(1)}, f32[96,128]{1,0:T(8,128)S(1)}, u32[]{:S(2)}, u32[]{:S(2)}) collective-permute-start(f32[96,128]{1,0:T(8,128)S(1)} %get-tuple-element.64), channel_id=1, source_target_pairs={{194,0},{196,2},{198,4},{192,6},{202,8},{204,10},{206,12},{200,14}... | collective-permute-start | bytes 147464 | tf_op jit(solution)/shard_map/ppermute | solution.py:318
  109.2 2.1 %collective-permute-start.22 = (f32[96,128]{1,0:T(8,128)S(1)}, f32[96,128]{1,0:T(8,128)S(1)}, u32[]{:S(2)}, u32[]{:S(2)}) collective-permute-start(f32[96,128]{1,0:T(8,128)S(1)} %get-tuple-element.65), channel_id=1, source_target_pairs={{196,0},{198,2},{192,4},{194,6},{204,8},{206,10},{200,12},{202,14}... | collective-permute-start | bytes 147464 | tf_op jit(solution)/shard_map/ppermute | solution.py:318
  111.9 4.9 %collective-permute-done.22.refs_14_ = f32[96,128]{1,0:T(8,128)S(1)} collective-permute-done((f32[96,128]{1,0:T(8,128)S(1)}, f32[96,128]{1,0:T(8,128)S(1)}, u32[]{:S(2)}, u32[]{:S(2)}) %collective-permute-start.22) | collective-permute-done | bytes 49184 | tf_op jit(solution)/shard_map/ppermute | solution.py:318
  116.9 1.8 %collective-permute-done.23.refs_15_ = f32[96,128]{1,0:T(8,128)S(1)} collective-permute-done((f32[96,128]{1,0:T(8,128)S(1)}, f32[96,128]{1,0:T(8,128)S(1)}, u32[]{:S(2)}, u32[]{:S(2)}) %collective-permute-start.23) | collective-permute-done | bytes 49184 | tf_op jit(solution)/shard_map/ppermute | solution.py:318
  119.6 2.9 %shard_map.79.early_ref = f32[3072,128]{1,0:T(8,128)S(1)} custom-call(f32[96,128]{1,0:T(8,128)S(1)} %get-tuple-element.51.refs_0_, f32[96,128]{1,0:T(8,128)S(1)} %collective-permute-done.9.refs_1_, f32[96,128]{1,0:T(8,128)S(1)} %collective-permute-done.10.refs_2_, f32[96,128]{1,0:T(8,128)S(1)} %collective-permute-done.11.refs_3_, ...), custom_call_target="tpu_custom_call" | custom-call | flops 603979776 | bytes 4194304 | tf_op jit(solution)/shard_map/pallas_call | solution.py:294
  122.6 2.6 %shard_map.80 = f32[3072,128]{1,0:T(8,128)} custom-call(f32[3072,128]{1,0:T(8,128)S(1)} %bitcast.4, f32[3072,128]{1,0:T(8,128)S(1)} %shard_map.79.early_ref, bf16[2,2,256,128]{3,2,1,0:T(8,128)(2,1)S(1)} %copy-done.1), custom_call_target="tpu_custom_call" | custom-call | flops 603979776 | bytes 4980736 | tf_op jit(solution)/shard_map/pallas_call | solution.py:294
  (42 shorter events, 13.8 us)
Async XLA Ops:
  4.6 4.7 %collective-permute-start = (f32[1152,256]{1,0:T(8,128)S(1)}, f32[1152,256]{1,0:T(8,128)S(1)}, u32[]{:S(2)}, u32[]{:S(2)}) collective-permute-start(f32[1152,256]{1,0:T(8,128)S(1)} %get-tuple-element.39), channel_id=1, source_target_pairs={{0,1},{1,0},{2,3},{3,2},{4,5},{5,4},{6,7},{7,6},{8,9},{9,8},{10,11... | collective-permute-start | bytes 3538952 | tf_op jit(solution)/shard_map/ppermute | solution.py:343
  12.0 110.6 %all-to-all-start = ((f32[128,24,128]{2,1,0:T(8,128)}), f32[128,24,128]{2,1,0:T(8,128)S(1)}, u32[]{:S(2)}, u32[]{:S(2)}) async-start(f32[128,24,128]{2,1,0:T(8,128)} %bitcast), calls=%async_computation | async-start | bytes 3145728 | tf_op jit(solution)/shard_map/all_to_all | solution.py:359
  27.0 40.2 %collective-permute-start.2 = (f32[192,128]{1,0:T(8,128)S(1)}, f32[192,128]{1,0:T(8,128)S(1)}, u32[]{:S(2)}, u32[]{:S(2)}) collective-permute-start(f32[192,128]{1,0:T(8,128)S(1)} %get-tuple-element.44), channel_id=1, source_target_pairs={{8,0},{10,2},{12,4},{14,6},{16,8},{18,10},{20,12},{22,14},{24,16},... | collective-permute-start | bytes 294920 | tf_op jit(solution)/shard_map/ppermute | solution.py:318
  28.0 41.5 %collective-permute-start.3 = (f32[192,128]{1,0:T(8,128)S(1)}, f32[192,128]{1,0:T(8,128)S(1)}, u32[]{:S(2)}, u32[]{:S(2)}) collective-permute-start(f32[192,128]{1,0:T(8,128)S(1)} %get-tuple-element.45), channel_id=1, source_target_pairs={{16,0},{18,2},{20,4},{22,6},{24,8},{26,10},{28,12},{30,14},{32,16}... | collective-permute-start | bytes 294920 | tf_op jit(solution)/shard_map/ppermute | solution.py:318
  31.7 45.7 %collective-permute-start.4 = (f32[192,128]{1,0:T(8,128)S(1)}, f32[192,128]{1,0:T(8,128)S(1)}, u32[]{:S(2)}, u32[]{:S(2)}) collective-permute-start(f32[192,128]{1,0:T(8,128)S(1)} %get-tuple-element.46), channel_id=1, source_target_pairs={{24,0},{26,2},{28,4},{30,6},{32,8},{34,10},{36,12},{38,14},{40,16}... | collective-permute-start | bytes 294920 | tf_op jit(solution)/shard_map/ppermute | solution.py:318
  33.8 48.1 %collective-permute-start.5 = (f32[192,128]{1,0:T(8,128)S(1)}, f32[192,128]{1,0:T(8,128)S(1)}, u32[]{:S(2)}, u32[]{:S(2)}) collective-permute-start(f32[192,128]{1,0:T(8,128)S(1)} %get-tuple-element.47), channel_id=1, source_target_pairs={{32,0},{34,2},{36,4},{38,6},{40,8},{42,10},{44,12},{46,14},{48,16}... | collective-permute-start | bytes 294920 | tf_op jit(solution)/shard_map/ppermute | solution.py:318
  36.9 45.0 %collective-permute-start.6 = (f32[192,128]{1,0:T(8,128)S(1)}, f32[192,128]{1,0:T(8,128)S(1)}, u32[]{:S(2)}, u32[]{:S(2)}) collective-permute-start(f32[192,128]{1,0:T(8,128)S(1)} %get-tuple-element.48), channel_id=1, source_target_pairs={{40,0},{42,2},{44,4},{46,6},{48,8},{50,10},{52,12},{54,14},{56,16}... | collective-permute-start | bytes 294920 | tf_op jit(solution)/shard_map/ppermute | solution.py:318
  67.2 14.7 %collective-permute-start.7 = (f32[192,128]{1,0:T(8,128)S(1)}, f32[192,128]{1,0:T(8,128)S(1)}, u32[]{:S(2)}, u32[]{:S(2)}) collective-permute-start(f32[192,128]{1,0:T(8,128)S(1)} %get-tuple-element.49), channel_id=1, source_target_pairs={{48,0},{50,2},{52,4},{54,6},{56,8},{58,10},{60,12},{62,14},{0,16},... | collective-permute-start | bytes 294920 | tf_op jit(solution)/shard_map/ppermute | solution.py:318
  69.4 12.5 %collective-permute-start.8 = (f32[192,128]{1,0:T(8,128)S(1)}, f32[192,128]{1,0:T(8,128)S(1)}, u32[]{:S(2)}, u32[]{:S(2)}) collective-permute-start(f32[192,128]{1,0:T(8,128)S(1)} %get-tuple-element.50), channel_id=1, source_target_pairs={{56,0},{58,2},{60,4},{62,6},{0,8},{2,10},{4,12},{6,14},{8,16},{10,... | collective-permute-start | bytes 294920 | tf_op jit(solution)/shard_map/ppermute | solution.py:318
  82.4 10.2 %collective-permute-start.9 = (f32[96,128]{1,0:T(8,128)S(1)}, f32[96,128]{1,0:T(8,128)S(1)}, u32[]{:S(2)}, u32[]{:S(2)}) collective-permute-start(f32[96,128]{1,0:T(8,128)S(1)} %get-tuple-element.52), channel_id=1, source_target_pairs={{2,0},{4,2},{6,4},{0,6},{10,8},{12,10},{14,12},{8,14},{18,16},{20,... | collective-permute-start | bytes 147464 | tf_op jit(solution)/shard_map/ppermute | solution.py:318
  85.5 8.6 %collective-permute-start.10 = (f32[96,128]{1,0:T(8,128)S(1)}, f32[96,128]{1,0:T(8,128)S(1)}, u32[]{:S(2)}, u32[]{:S(2)}) collective-permute-start(f32[96,128]{1,0:T(8,128)S(1)} %get-tuple-element.53), channel_id=1, source_target_pairs={{4,0},{6,2},{0,4},{2,6},{12,8},{14,10},{8,12},{10,14},{20,16},{22,... | collective-permute-start | bytes 147464 | tf_op jit(solution)/shard_map/ppermute | solution.py:318
  86.3 7.8 %collective-permute-start.11 = (f32[96,128]{1,0:T(8,128)S(1)}, f32[96,128]{1,0:T(8,128)S(1)}, u32[]{:S(2)}, u32[]{:S(2)}) collective-permute-start(f32[96,128]{1,0:T(8,128)S(1)} %get-tuple-element.54), channel_id=1, source_target_pairs={{6,0},{0,2},{2,4},{4,6},{14,8},{8,10},{10,12},{12,14},{22,16},{16,... | collective-permute-start | bytes 147464 | tf_op jit(solution)/shard_map/ppermute | solution.py:318
  87.2 9.7 %collective-permute-start.12 = (f32[96,128]{1,0:T(8,128)S(1)}, f32[96,128]{1,0:T(8,128)S(1)}, u32[]{:S(2)}, u32[]{:S(2)}) collective-permute-start(f32[96,128]{1,0:T(8,128)S(1)} %get-tuple-element.55), channel_id=1, source_target_pairs={{64,0},{66,2},{68,4},{70,6},{72,8},{74,10},{76,12},{78,14},{80,16}... | collective-permute-start | bytes 147464 | tf_op jit(solution)/shard_map/ppermute | solution.py:318
  90.0 10.3 %collective-permute-start.13 = (f32[96,128]{1,0:T(8,128)S(1)}, f32[96,128]{1,0:T(8,128)S(1)}, u32[]{:S(2)}, u32[]{:S(2)}) collective-permute-start(f32[96,128]{1,0:T(8,128)S(1)} %get-tuple-element.56), channel_id=1, source_target_pairs={{66,0},{68,2},{70,4},{64,6},{74,8},{76,10},{78,12},{72,14},{82,16}... | collective-permute-start | bytes 147464 | tf_op jit(solution)/shard_map/ppermute | solution.py:318
  92.6 10.9 %collective-permute-start.14 = (f32[96,128]{1,0:T(8,128)S(1)}, f32[96,128]{1,0:T(8,128)S(1)}, u32[]{:S(2)}, u32[]{:S(2)}) collective-permute-start(f32[96,128]{1,0:T(8,128)S(1)} %get-tuple-element.57), channel_id=1, source_target_pairs={{68,0},{70,2},{64,4},{66,6},{76,8},{78,10},{72,12},{74,14},{84,16}... | collective-permute-start | bytes 147464 | tf_op jit(solution)/shard_map/ppermute | solution.py:318
  94.0 9.6 %collective-permute-start.15 = (f32[96,128]{1,0:T(8,128)S(1)}, f32[96,128]{1,0:T(8,128)S(1)}, u32[]{:S(2)}, u32[]{:S(2)}) collective-permute-start(f32[96,128]{1,0:T(8,128)S(1)} %get-tuple-element.58), channel_id=1, source_target_pairs={{70,0},{64,2},{66,4},{68,6},{78,8},{72,10},{74,12},{76,14},{86,16}... | collective-permute-start | bytes 147464 | tf_op jit(solution)/shard_map/ppermute | solution.py:318
  94.1 10.5 %collective-permute-start.16 = (f32[96,128]{1,0:T(8,128)S(1)}, f32[96,128]{1,0:T(8,128)S(1)}, u32[]{:S(2)}, u32[]{:S(2)}) collective-permute-start(f32[96,128]{1,0:T(8,128)S(1)} %get-tuple-element.59), channel_id=1, source_target_pairs={{128,0},{130,2},{132,4},{134,6},{136,8},{138,10},{140,12},{142,14}... | collective-permute-start | bytes 147464 | tf_op jit(solution)/shard_map/ppermute | solution.py:318
  96.9 12.3 %collective-permute-start.17 = (f32[96,128]{1,0:T(8,128)S(1)}, f32[96,128]{1,0:T(8,128)S(1)}, u32[]{:S(2)}, u32[]{:S(2)}) collective-permute-start(f32[96,128]{1,0:T(8,128)S(1)} %get-tuple-element.60), channel_id=1, source_target_pairs={{130,0},{132,2},{134,4},{128,6},{138,8},{140,10},{142,12},{136,14}... | collective-permute-start | bytes 147464 | tf_op jit(solution)/shard_map/ppermute | solution.py:318
  100.2 11.0 %collective-permute-start.18 = (f32[96,128]{1,0:T(8,128)S(1)}, f32[96,128]{1,0:T(8,128)S(1)}, u32[]{:S(2)}, u32[]{:S(2)}) collective-permute-start(f32[96,128]{1,0:T(8,128)S(1)} %get-tuple-element.61), channel_id=1, source_target_pairs={{132,0},{134,2},{128,4},{130,6},{140,8},{142,10},{136,12},{138,14}... | collective-permute-start | bytes 147464 | tf_op jit(solution)/shard_map/ppermute | solution.py:318
  103.5 8.4 %collective-permute-start.19 = (f32[96,128]{1,0:T(8,128)S(1)}, f32[96,128]{1,0:T(8,128)S(1)}, u32[]{:S(2)}, u32[]{:S(2)}) collective-permute-start(f32[96,128]{1,0:T(8,128)S(1)} %get-tuple-element.62), channel_id=1, source_target_pairs={{134,0},{128,2},{130,4},{132,6},{142,8},{136,10},{138,12},{140,14}... | collective-permute-start | bytes 147464 | tf_op jit(solution)/shard_map/ppermute | solution.py:318
  103.7 8.3 %collective-permute-start.20 = (f32[96,128]{1,0:T(8,128)S(1)}, f32[96,128]{1,0:T(8,128)S(1)}, u32[]{:S(2)}, u32[]{:S(2)}) collective-permute-start(f32[96,128]{1,0:T(8,128)S(1)} %get-tuple-element.63), channel_id=1, source_target_pairs={{192,0},{194,2},{196,4},{198,6},{200,8},{202,10},{204,12},{206,14}... | collective-permute-start | bytes 147464 | tf_op jit(solution)/shard_map/ppermute | solution.py:318
  104.6 7.3 %collective-permute-start.21 = (f32[96,128]{1,0:T(8,128)S(1)}, f32[96,128]{1,0:T(8,128)S(1)}, u32[]{:S(2)}, u32[]{:S(2)}) collective-permute-start(f32[96,128]{1,0:T(8,128)S(1)} %get-tuple-element.64), channel_id=1, source_target_pairs={{194,0},{196,2},{198,4},{192,6},{202,8},{204,10},{206,12},{200,14}... | collective-permute-start | bytes 147464 | tf_op jit(solution)/shard_map/ppermute | solution.py:318
  109.2 7.7 %collective-permute-start.22 = (f32[96,128]{1,0:T(8,128)S(1)}, f32[96,128]{1,0:T(8,128)S(1)}, u32[]{:S(2)}, u32[]{:S(2)}) collective-permute-start(f32[96,128]{1,0:T(8,128)S(1)} %get-tuple-element.65), channel_id=1, source_target_pairs={{196,0},{198,2},{192,4},{194,6},{204,8},{206,10},{200,12},{202,14}... | collective-permute-start | bytes 147464 | tf_op jit(solution)/shard_map/ppermute | solution.py:318
  111.3 7.4 %collective-permute-start.23 = (f32[96,128]{1,0:T(8,128)S(1)}, f32[96,128]{1,0:T(8,128)S(1)}, u32[]{:S(2)}, u32[]{:S(2)}) collective-permute-start(f32[96,128]{1,0:T(8,128)S(1)} %get-tuple-element.66), channel_id=1, source_target_pairs={{198,0},{192,2},{194,4},{196,6},{206,8},{200,10},{202,12},{204,14}... | collective-permute-start | bytes 147464 | tf_op jit(solution)/shard_map/ppermute | solution.py:318
  (5 other events, 13.4 us)

commit v6 on v5

--- a/solution.py
+++ b/solution.py
@@ -107,12 +107,15 @@
         ]
         for plane in range(len(outs))
     ]
-    for group in copies:
+    for group in copies[:2]:
         for copy in group:
             copy.start()
     for plane, out_ref in enumerate(outs):
         for copy in copies[plane]:
             copy.wait()
+        for group in copies[plane + 2 : plane + 3]:
+            for copy in group:
+                copy.start()
         for c in range(3):
             a, b = (c + 1) % 3, (c + 2) % 3
             high, low = split(v_ref[plane, a] * w_ref[plane, b] - v_ref[plane, b] * w_ref[plane, a])

time: 126 us -> 126 us (level)
  no operation moved by 1% of the time
where the time goes in v6:
time: 126 us
  starting transfers between devices  63.3 us (50%)
  waiting for transfers between devices  45.7 us (36%)
  Pallas kernels  15.5 us (12%)
    ppermute x22, starting transfers between devices, from_shift(): return lax.ppermute(value, GROUP, pairs)  47.7 us
    ppermute x22, waiting for transfers between devices, from_shift(): return lax.ppermute(value, GROUP, pairs)  43.5 us
    pallas_call x8, Pallas kernels, run(): pl.pallas_call(kernel, out_shape=shapes[0] if single else shapes, in_spec...  15.5 us
    all_to_all x1, starting transfers between devices, per_device(): lax.all_to_all(packed.reshape(dests, per, lanes), GROUP, 0, 0, axis_index...  15 us
  transfers between devices with their start and end apart: 25, of which 8 were waited for; matrix products, arithmetic and copies ran while one was open for 0% of the time, Pallas kernels for 4%

profile of v6, /device:TPU:32, one launch (start us, length us, event | category | flops | bytes accessed | tf_op | source)
XLA Modules:
  0.0 125.8 jit_solution(12845723834964869729)
XLA Ops:
  0.0 3.4 %shard_map.73 = (bf16[576,768]{1,0:T(8,128)(2,1)S(1)}, bf16[576,768]{1,0:T(8,128)(2,1)S(1)}, bf16[576,768]{1,0:T(8,128)(2,1)S(1)}) custom-call(f32[3,3,192,384]{3,2,1,0:T(8,128)} %v_hbm.1, f32[3,3,192,384]{3,2,1,0:T(8,128)} %w_hbm.1), custom_call_target="tpu_custom_call" | custom-call | flops 3981312 | bytes 10616832 | tf_op jit(solution)/shard_map/pallas_call | solution.py:297
  6.7 2.2 %collective-permute-done.1.got_ref = f32[576,256]{1,0:T(8,128)S(1)} collective-permute-done((f32[576,256]{1,0:T(8,128)S(1)}, f32[576,256]{1,0:T(8,128)S(1)}, u32[]{:S(2)}, u32[]{:S(2)}) %collective-permute-start.1) | collective-permute-done | bytes 589856 | tf_op jit(solution)/shard_map/ppermute | solution.py:346
  9.8 2.7 %shard_map.77 = f32[3072,128]{1,0:T(8,128)} custom-call(f32[1152,256]{1,0:T(8,128)S(1)} %get-tuple-element.38.keep_ref, f32[1152,256]{1,0:T(8,128)S(1)} %collective-permute-done.got_ref, bf16[2,2,256,192]{3,2,1,0:T(8,128)(2,1)S(1)} %copy-done, f32[192,128]{1,0:T(8,128)S(1)} %get-tuple-element.43._.refs_0_), custom_call_target="tpu_custom_call" | custom-call | flops 905969664 | bytes 4423680 | tf_op jit(solution)/shard_map/pallas_call | solution.py:297
  12.5 15.0 %all-to-all-start = ((f32[128,24,128]{2,1,0:T(8,128)}), f32[128,24,128]{2,1,0:T(8,128)S(1)}, u32[]{:S(2)}, u32[]{:S(2)}) async-start(f32[128,24,128]{2,1,0:T(8,128)} %bitcast), calls=%async_computation | async-start | bytes 3145728 | tf_op jit(solution)/shard_map/all_to_all | solution.py:362
  28.4 3.8 %collective-permute-start.3 = (f32[192,128]{1,0:T(8,128)S(1)}, f32[192,128]{1,0:T(8,128)S(1)}, u32[]{:S(2)}, u32[]{:S(2)}) collective-permute-start(f32[192,128]{1,0:T(8,128)S(1)} %get-tuple-element.45), channel_id=1, source_target_pairs={{16,0},{18,2},{20,4},{22,6},{24,8},{26,10},{28,12},{30,14},{32,16}... | collective-permute-start | bytes 294920 | tf_op jit(solution)/shard_map/ppermute | solution.py:321
  32.2 2.0 %collective-permute-start.4 = (f32[192,128]{1,0:T(8,128)S(1)}, f32[192,128]{1,0:T(8,128)S(1)}, u32[]{:S(2)}, u32[]{:S(2)}) collective-permute-start(f32[192,128]{1,0:T(8,128)S(1)} %get-tuple-element.46), channel_id=1, source_target_pairs={{24,0},{26,2},{28,4},{30,6},{32,8},{34,10},{36,12},{38,14},{40,16}... | collective-permute-start | bytes 294920 | tf_op jit(solution)/shard_map/ppermute | solution.py:321
  34.2 3.1 %collective-permute-start.5 = (f32[192,128]{1,0:T(8,128)S(1)}, f32[192,128]{1,0:T(8,128)S(1)}, u32[]{:S(2)}, u32[]{:S(2)}) collective-permute-start(f32[192,128]{1,0:T(8,128)S(1)} %get-tuple-element.47), channel_id=1, source_target_pairs={{32,0},{34,2},{36,4},{38,6},{40,8},{42,10},{44,12},{46,14},{48,16}... | collective-permute-start | bytes 294920 | tf_op jit(solution)/shard_map/ppermute | solution.py:321
  39.2 28.5 %collective-permute-done.2.refs_1_ = f32[192,128]{1,0:T(8,128)S(1)} collective-permute-done((f32[192,128]{1,0:T(8,128)S(1)}, f32[192,128]{1,0:T(8,128)S(1)}, u32[]{:S(2)}, u32[]{:S(2)}) %collective-permute-start.2) | collective-permute-done | bytes 98336 | tf_op jit(solution)/shard_map/ppermute | solution.py:321
  67.7 1.9 %collective-permute-start.7 = (f32[192,128]{1,0:T(8,128)S(1)}, f32[192,128]{1,0:T(8,128)S(1)}, u32[]{:S(2)}, u32[]{:S(2)}) collective-permute-start(f32[192,128]{1,0:T(8,128)S(1)} %get-tuple-element.49), channel_id=1, source_target_pairs={{48,0},{50,2},{52,4},{54,6},{56,8},{58,10},{60,12},{62,14},{0,16},... | collective-permute-start | bytes 294920 | tf_op jit(solution)/shard_map/ppermute | solution.py:321
  69.8 5.2 %collective-permute-start.8 = (f32[192,128]{1,0:T(8,128)S(1)}, f32[192,128]{1,0:T(8,128)S(1)}, u32[]{:S(2)}, u32[]{:S(2)}) collective-permute-start(f32[192,128]{1,0:T(8,128)S(1)} %get-tuple-element.50), channel_id=1, source_target_pairs={{56,0},{58,2},{60,4},{62,6},{0,8},{2,10},{4,12},{6,14},{8,16},{10,... | collective-permute-start | bytes 294920 | tf_op jit(solution)/shard_map/ppermute | solution.py:321
  75.0 2.8 %collective-permute-done.4.refs_3_ = f32[192,128]{1,0:T(8,128)S(1)} collective-permute-done((f32[192,128]{1,0:T(8,128)S(1)}, f32[192,128]{1,0:T(8,128)S(1)}, u32[]{:S(2)}, u32[]{:S(2)}) %collective-permute-start.4) | collective-permute-done | bytes 98336 | tf_op jit(solution)/shard_map/ppermute | solution.py:321
  77.9 4.4 %collective-permute-done.5.refs_4_ = f32[192,128]{1,0:T(8,128)S(1)} collective-permute-done((f32[192,128]{1,0:T(8,128)S(1)}, f32[192,128]{1,0:T(8,128)S(1)}, u32[]{:S(2)}, u32[]{:S(2)}) %collective-permute-start.5) | collective-permute-done | bytes 98336 | tf_op jit(solution)/shard_map/ppermute | solution.py:321
  82.8 3.2 %collective-permute-start.9 = (f32[96,128]{1,0:T(8,128)S(1)}, f32[96,128]{1,0:T(8,128)S(1)}, u32[]{:S(2)}, u32[]{:S(2)}) collective-permute-start(f32[96,128]{1,0:T(8,128)S(1)} %get-tuple-element.52), channel_id=1, source_target_pairs={{2,0},{4,2},{6,4},{0,6},{10,8},{12,10},{14,12},{8,14},{18,16},{20,... | collective-permute-start | bytes 147464 | tf_op jit(solution)/shard_map/ppermute | solution.py:321
  87.7 2.8 %collective-permute-start.12 = (f32[96,128]{1,0:T(8,128)S(1)}, f32[96,128]{1,0:T(8,128)S(1)}, u32[]{:S(2)}, u32[]{:S(2)}) collective-permute-start(f32[96,128]{1,0:T(8,128)S(1)} %get-tuple-element.55), channel_id=1, source_target_pairs={{64,0},{66,2},{68,4},{70,6},{72,8},{74,10},{76,12},{78,14},{80,16}... | collective-permute-start | bytes 147464 | tf_op jit(solution)/shard_map/ppermute | solution.py:321
  90.4 2.6 %collective-permute-start.13 = (f32[96,128]{1,0:T(8,128)S(1)}, f32[96,128]{1,0:T(8,128)S(1)}, u32[]{:S(2)}, u32[]{:S(2)}) collective-permute-start(f32[96,128]{1,0:T(8,128)S(1)} %get-tuple-element.56), channel_id=1, source_target_pairs={{66,0},{68,2},{70,4},{64,6},{74,8},{76,10},{78,12},{72,14},{82,16}... | collective-permute-start | bytes 147464 | tf_op jit(solution)/shard_map/ppermute | solution.py:321
  94.6 2.8 %collective-permute-start.16 = (f32[96,128]{1,0:T(8,128)S(1)}, f32[96,128]{1,0:T(8,128)S(1)}, u32[]{:S(2)}, u32[]{:S(2)}) collective-permute-start(f32[96,128]{1,0:T(8,128)S(1)} %get-tuple-element.59), channel_id=1, source_target_pairs={{128,0},{130,2},{132,4},{134,6},{136,8},{138,10},{140,12},{142,14}... | collective-permute-start | bytes 147464 | tf_op jit(solution)/shard_map/ppermute | solution.py:321
  97.4 3.4 %collective-permute-start.17 = (f32[96,128]{1,0:T(8,128)S(1)}, f32[96,128]{1,0:T(8,128)S(1)}, u32[]{:S(2)}, u32[]{:S(2)}) collective-permute-start(f32[96,128]{1,0:T(8,128)S(1)} %get-tuple-element.60), channel_id=1, source_target_pairs={{130,0},{132,2},{134,4},{128,6},{138,8},{140,10},{142,12},{136,14}... | collective-permute-start | bytes 147464 | tf_op jit(solution)/shard_map/ppermute | solution.py:321
  100.7 3.3 %collective-permute-start.18 = (f32[96,128]{1,0:T(8,128)S(1)}, f32[96,128]{1,0:T(8,128)S(1)}, u32[]{:S(2)}, u32[]{:S(2)}) collective-permute-start(f32[96,128]{1,0:T(8,128)S(1)} %get-tuple-element.61), channel_id=1, source_target_pairs={{132,0},{134,2},{128,4},{130,6},{140,8},{142,10},{136,12},{138,14}... | collective-permute-start | bytes 147464 | tf_op jit(solution)/shard_map/ppermute | solution.py:321
  105.1 4.5 %collective-permute-start.21 = (f32[96,128]{1,0:T(8,128)S(1)}, f32[96,128]{1,0:T(8,128)S(1)}, u32[]{:S(2)}, u32[]{:S(2)}) collective-permute-start(f32[96,128]{1,0:T(8,128)S(1)} %get-tuple-element.64), channel_id=1, source_target_pairs={{194,0},{196,2},{198,4},{192,6},{202,8},{204,10},{206,12},{200,14}... | collective-permute-start | bytes 147464 | tf_op jit(solution)/shard_map/ppermute | solution.py:321
  109.6 2.1 %collective-permute-start.22 = (f32[96,128]{1,0:T(8,128)S(1)}, f32[96,128]{1,0:T(8,128)S(1)}, u32[]{:S(2)}, u32[]{:S(2)}) collective-permute-start(f32[96,128]{1,0:T(8,128)S(1)} %get-tuple-element.65), channel_id=1, source_target_pairs={{196,0},{198,2},{192,4},{194,6},{204,8},{206,10},{200,12},{202,14}... | collective-permute-start | bytes 147464 | tf_op jit(solution)/shard_map/ppermute | solution.py:321
  112.4 4.9 %collective-permute-done.22.refs_14_ = f32[96,128]{1,0:T(8,128)S(1)} collective-permute-done((f32[96,128]{1,0:T(8,128)S(1)}, f32[96,128]{1,0:T(8,128)S(1)}, u32[]{:S(2)}, u32[]{:S(2)}) %collective-permute-start.22) | collective-permute-done | bytes 49184 | tf_op jit(solution)/shard_map/ppermute | solution.py:321
  117.3 1.8 %collective-permute-done.23.refs_15_ = f32[96,128]{1,0:T(8,128)S(1)} collective-permute-done((f32[96,128]{1,0:T(8,128)S(1)}, f32[96,128]{1,0:T(8,128)S(1)}, u32[]{:S(2)}, u32[]{:S(2)}) %collective-permute-start.23) | collective-permute-done | bytes 49184 | tf_op jit(solution)/shard_map/ppermute | solution.py:321
  120.1 2.9 %shard_map.79.early_ref = f32[3072,128]{1,0:T(8,128)S(1)} custom-call(f32[96,128]{1,0:T(8,128)S(1)} %get-tuple-element.51.refs_0_, f32[96,128]{1,0:T(8,128)S(1)} %collective-permute-done.9.refs_1_, f32[96,128]{1,0:T(8,128)S(1)} %collective-permute-done.10.refs_2_, f32[96,128]{1,0:T(8,128)S(1)} %collective-permute-done.11.refs_3_, ...), custom_call_target="tpu_custom_call" | custom-call | flops 603979776 | bytes 4194304 | tf_op jit(solution)/shard_map/pallas_call | solution.py:297
  123.1 2.6 %shard_map.80 = f32[3072,128]{1,0:T(8,128)} custom-call(f32[3072,128]{1,0:T(8,128)S(1)} %bitcast.4, f32[3072,128]{1,0:T(8,128)S(1)} %shard_map.79.early_ref, bf16[2,2,256,128]{3,2,1,0:T(8,128)(2,1)S(1)} %copy-done.1), custom_call_target="tpu_custom_call" | custom-call | flops 603979776 | bytes 4980736 | tf_op jit(solution)/shard_map/pallas_call | solution.py:297
  (42 shorter events, 13.7 us)
Async XLA Ops:
  5.1 4.7 %collective-permute-start = (f32[1152,256]{1,0:T(8,128)S(1)}, f32[1152,256]{1,0:T(8,128)S(1)}, u32[]{:S(2)}, u32[]{:S(2)}) collective-permute-start(f32[1152,256]{1,0:T(8,128)S(1)} %get-tuple-element.39), channel_id=1, source_target_pairs={{0,1},{1,0},{2,3},{3,2},{4,5},{5,4},{6,7},{7,6},{8,9},{9,8},{10,11... | collective-permute-start | bytes 3538952 | tf_op jit(solution)/shard_map/ppermute | solution.py:346
  12.5 110.6 %all-to-all-start = ((f32[128,24,128]{2,1,0:T(8,128)}), f32[128,24,128]{2,1,0:T(8,128)S(1)}, u32[]{:S(2)}, u32[]{:S(2)}) async-start(f32[128,24,128]{2,1,0:T(8,128)} %bitcast), calls=%async_computation | async-start | bytes 3145728 | tf_op jit(solution)/shard_map/all_to_all | solution.py:362
  27.5 40.2 %collective-permute-start.2 = (f32[192,128]{1,0:T(8,128)S(1)}, f32[192,128]{1,0:T(8,128)S(1)}, u32[]{:S(2)}, u32[]{:S(2)}) collective-permute-start(f32[192,128]{1,0:T(8,128)S(1)} %get-tuple-element.44), channel_id=1, source_target_pairs={{8,0},{10,2},{12,4},{14,6},{16,8},{18,10},{20,12},{22,14},{24,16},... | collective-permute-start | bytes 294920 | tf_op jit(solution)/shard_map/ppermute | solution.py:321
  28.4 41.4 %collective-permute-start.3 = (f32[192,128]{1,0:T(8,128)S(1)}, f32[192,128]{1,0:T(8,128)S(1)}, u32[]{:S(2)}, u32[]{:S(2)}) collective-permute-start(f32[192,128]{1,0:T(8,128)S(1)} %get-tuple-element.45), channel_id=1, source_target_pairs={{16,0},{18,2},{20,4},{22,6},{24,8},{26,10},{28,12},{30,14},{32,16}... | collective-permute-start | bytes 294920 | tf_op jit(solution)/shard_map/ppermute | solution.py:321
  32.2 45.7 %collective-permute-start.4 = (f32[192,128]{1,0:T(8,128)S(1)}, f32[192,128]{1,0:T(8,128)S(1)}, u32[]{:S(2)}, u32[]{:S(2)}) collective-permute-start(f32[192,128]{1,0:T(8,128)S(1)} %get-tuple-element.46), channel_id=1, source_target_pairs={{24,0},{26,2},{28,4},{30,6},{32,8},{34,10},{36,12},{38,14},{40,16}... | collective-permute-start | bytes 294920 | tf_op jit(solution)/shard_map/ppermute | solution.py:321
  34.2 48.1 %collective-permute-start.5 = (f32[192,128]{1,0:T(8,128)S(1)}, f32[192,128]{1,0:T(8,128)S(1)}, u32[]{:S(2)}, u32[]{:S(2)}) collective-permute-start(f32[192,128]{1,0:T(8,128)S(1)} %get-tuple-element.47), channel_id=1, source_target_pairs={{32,0},{34,2},{36,4},{38,6},{40,8},{42,10},{44,12},{46,14},{48,16}... | collective-permute-start | bytes 294920 | tf_op jit(solution)/shard_map/ppermute | solution.py:321
  37.3 45.0 %collective-permute-start.6 = (f32[192,128]{1,0:T(8,128)S(1)}, f32[192,128]{1,0:T(8,128)S(1)}, u32[]{:S(2)}, u32[]{:S(2)}) collective-permute-start(f32[192,128]{1,0:T(8,128)S(1)} %get-tuple-element.48), channel_id=1, source_target_pairs={{40,0},{42,2},{44,4},{46,6},{48,8},{50,10},{52,12},{54,14},{56,16}... | collective-permute-start | bytes 294920 | tf_op jit(solution)/shard_map/ppermute | solution.py:321
  67.7 14.6 %collective-permute-start.7 = (f32[192,128]{1,0:T(8,128)S(1)}, f32[192,128]{1,0:T(8,128)S(1)}, u32[]{:S(2)}, u32[]{:S(2)}) collective-permute-start(f32[192,128]{1,0:T(8,128)S(1)} %get-tuple-element.49), channel_id=1, source_target_pairs={{48,0},{50,2},{52,4},{54,6},{56,8},{58,10},{60,12},{62,14},{0,16},... | collective-permute-start | bytes 294920 | tf_op jit(solution)/shard_map/ppermute | solution.py:321
  69.8 12.5 %collective-permute-start.8 = (f32[192,128]{1,0:T(8,128)S(1)}, f32[192,128]{1,0:T(8,128)S(1)}, u32[]{:S(2)}, u32[]{:S(2)}) collective-permute-start(f32[192,128]{1,0:T(8,128)S(1)} %get-tuple-element.50), channel_id=1, source_target_pairs={{56,0},{58,2},{60,4},{62,6},{0,8},{2,10},{4,12},{6,14},{8,16},{10,... | collective-permute-start | bytes 294920 | tf_op jit(solution)/shard_map/ppermute | solution.py:321
  82.8 10.3 %collective-permute-start.9 = (f32[96,128]{1,0:T(8,128)S(1)}, f32[96,128]{1,0:T(8,128)S(1)}, u32[]{:S(2)}, u32[]{:S(2)}) collective-permute-start(f32[96,128]{1,0:T(8,128)S(1)} %get-tuple-element.52), channel_id=1, source_target_pairs={{2,0},{4,2},{6,4},{0,6},{10,8},{12,10},{14,12},{8,14},{18,16},{20,... | collective-permute-start | bytes 147464 | tf_op jit(solution)/shard_map/ppermute | solution.py:321
  86.0 8.6 %collective-permute-start.10 = (f32[96,128]{1,0:T(8,128)S(1)}, f32[96,128]{1,0:T(8,128)S(1)}, u32[]{:S(2)}, u32[]{:S(2)}) collective-permute-start(f32[96,128]{1,0:T(8,128)S(1)} %get-tuple-element.53), channel_id=1, source_target_pairs={{4,0},{6,2},{0,4},{2,6},{12,8},{14,10},{8,12},{10,14},{20,16},{22,... | collective-permute-start | bytes 147464 | tf_op jit(solution)/shard_map/ppermute | solution.py:321
  86.8 7.8 %collective-permute-start.11 = (f32[96,128]{1,0:T(8,128)S(1)}, f32[96,128]{1,0:T(8,128)S(1)}, u32[]{:S(2)}, u32[]{:S(2)}) collective-permute-start(f32[96,128]{1,0:T(8,128)S(1)} %get-tuple-element.54), channel_id=1, source_target_pairs={{6,0},{0,2},{2,4},{4,6},{14,8},{8,10},{10,12},{12,14},{22,16},{16,... | collective-permute-start | bytes 147464 | tf_op jit(solution)/shard_map/ppermute | solution.py:321
  87.7 9.7 %collective-permute-start.12 = (f32[96,128]{1,0:T(8,128)S(1)}, f32[96,128]{1,0:T(8,128)S(1)}, u32[]{:S(2)}, u32[]{:S(2)}) collective-permute-start(f32[96,128]{1,0:T(8,128)S(1)} %get-tuple-element.55), channel_id=1, source_target_pairs={{64,0},{66,2},{68,4},{70,6},{72,8},{74,10},{76,12},{78,14},{80,16}... | collective-permute-start | bytes 147464 | tf_op jit(solution)/shard_map/ppermute | solution.py:321
  90.4 10.3 %collective-permute-start.13 = (f32[96,128]{1,0:T(8,128)S(1)}, f32[96,128]{1,0:T(8,128)S(1)}, u32[]{:S(2)}, u32[]{:S(2)}) collective-permute-start(f32[96,128]{1,0:T(8,128)S(1)} %get-tuple-element.56), channel_id=1, source_target_pairs={{66,0},{68,2},{70,4},{64,6},{74,8},{76,10},{78,12},{72,14},{82,16}... | collective-permute-start | bytes 147464 | tf_op jit(solution)/shard_map/ppermute | solution.py:321
  93.1 10.9 %collective-permute-start.14 = (f32[96,128]{1,0:T(8,128)S(1)}, f32[96,128]{1,0:T(8,128)S(1)}, u32[]{:S(2)}, u32[]{:S(2)}) collective-permute-start(f32[96,128]{1,0:T(8,128)S(1)} %get-tuple-element.57), channel_id=1, source_target_pairs={{68,0},{70,2},{64,4},{66,6},{76,8},{78,10},{72,12},{74,14},{84,16}... | collective-permute-start | bytes 147464 | tf_op jit(solution)/shard_map/ppermute | solution.py:321
  94.5 9.6 %collective-permute-start.15 = (f32[96,128]{1,0:T(8,128)S(1)}, f32[96,128]{1,0:T(8,128)S(1)}, u32[]{:S(2)}, u32[]{:S(2)}) collective-permute-start(f32[96,128]{1,0:T(8,128)S(1)} %get-tuple-element.58), channel_id=1, source_target_pairs={{70,0},{64,2},{66,4},{68,6},{78,8},{72,10},{74,12},{76,14},{86,16}... | collective-permute-start | bytes 147464 | tf_op jit(solution)/shard_map/ppermute | solution.py:321
  94.6 10.5 %collective-permute-start.16 = (f32[96,128]{1,0:T(8,128)S(1)}, f32[96,128]{1,0:T(8,128)S(1)}, u32[]{:S(2)}, u32[]{:S(2)}) collective-permute-start(f32[96,128]{1,0:T(8,128)S(1)} %get-tuple-element.59), channel_id=1, source_target_pairs={{128,0},{130,2},{132,4},{134,6},{136,8},{138,10},{140,12},{142,14}... | collective-permute-start | bytes 147464 | tf_op jit(solution)/shard_map/ppermute | solution.py:321
  97.4 12.3 %collective-permute-start.17 = (f32[96,128]{1,0:T(8,128)S(1)}, f32[96,128]{1,0:T(8,128)S(1)}, u32[]{:S(2)}, u32[]{:S(2)}) collective-permute-start(f32[96,128]{1,0:T(8,128)S(1)} %get-tuple-element.60), channel_id=1, source_target_pairs={{130,0},{132,2},{134,4},{128,6},{138,8},{140,10},{142,12},{136,14}... | collective-permute-start | bytes 147464 | tf_op jit(solution)/shard_map/ppermute | solution.py:321
  100.7 11.0 %collective-permute-start.18 = (f32[96,128]{1,0:T(8,128)S(1)}, f32[96,128]{1,0:T(8,128)S(1)}, u32[]{:S(2)}, u32[]{:S(2)}) collective-permute-start(f32[96,128]{1,0:T(8,128)S(1)} %get-tuple-element.61), channel_id=1, source_target_pairs={{132,0},{134,2},{128,4},{130,6},{140,8},{142,10},{136,12},{138,14}... | collective-permute-start | bytes 147464 | tf_op jit(solution)/shard_map/ppermute | solution.py:321
  104.0 8.4 %collective-permute-start.19 = (f32[96,128]{1,0:T(8,128)S(1)}, f32[96,128]{1,0:T(8,128)S(1)}, u32[]{:S(2)}, u32[]{:S(2)}) collective-permute-start(f32[96,128]{1,0:T(8,128)S(1)} %get-tuple-element.62), channel_id=1, source_target_pairs={{134,0},{128,2},{130,4},{132,6},{142,8},{136,10},{138,12},{140,14}... | collective-permute-start | bytes 147464 | tf_op jit(solution)/shard_map/ppermute | solution.py:321
  104.1 8.3 %collective-permute-start.20 = (f32[96,128]{1,0:T(8,128)S(1)}, f32[96,128]{1,0:T(8,128)S(1)}, u32[]{:S(2)}, u32[]{:S(2)}) collective-permute-start(f32[96,128]{1,0:T(8,128)S(1)} %get-tuple-element.63), channel_id=1, source_target_pairs={{192,0},{194,2},{196,4},{198,6},{200,8},{202,10},{204,12},{206,14}... | collective-permute-start | bytes 147464 | tf_op jit(solution)/shard_map/ppermute | solution.py:321
  105.1 7.3 %collective-permute-start.21 = (f32[96,128]{1,0:T(8,128)S(1)}, f32[96,128]{1,0:T(8,128)S(1)}, u32[]{:S(2)}, u32[]{:S(2)}) collective-permute-start(f32[96,128]{1,0:T(8,128)S(1)} %get-tuple-element.64), channel_id=1, source_target_pairs={{194,0},{196,2},{198,4},{192,6},{202,8},{204,10},{206,12},{200,14}... | collective-permute-start | bytes 147464 | tf_op jit(solution)/shard_map/ppermute | solution.py:321
  109.6 7.7 %collective-permute-start.22 = (f32[96,128]{1,0:T(8,128)S(1)}, f32[96,128]{1,0:T(8,128)S(1)}, u32[]{:S(2)}, u32[]{:S(2)}) collective-permute-start(f32[96,128]{1,0:T(8,128)S(1)} %get-tuple-element.65), channel_id=1, source_target_pairs={{196,0},{198,2},{192,4},{194,6},{204,8},{206,10},{200,12},{202,14}... | collective-permute-start | bytes 147464 | tf_op jit(solution)/shard_map/ppermute | solution.py:321
  111.7 7.4 %collective-permute-start.23 = (f32[96,128]{1,0:T(8,128)S(1)}, f32[96,128]{1,0:T(8,128)S(1)}, u32[]{:S(2)}, u32[]{:S(2)}) collective-permute-start(f32[96,128]{1,0:T(8,128)S(1)} %get-tuple-element.66), channel_id=1, source_target_pairs={{198,0},{192,2},{194,4},{196,6},{206,8},{200,10},{202,12},{204,14}... | collective-permute-start | bytes 147464 | tf_op jit(solution)/shard_map/ppermute | solution.py:321
  (5 other events, 13.8 us)

commit v7 on v5

--- a/solution.py
+++ b/solution.py
@@ -96,14 +96,17 @@
 def cross_kernel(v_hbm, w_hbm, *refs):
     outs, (v_ref, w_ref, sems) = refs[:-3], refs[-3:]
     rows, cells = v_ref.shape[2:]
+    part = rows // 2
     copies = [
         [
-            copy
+            pltpu.make_async_copy(
+                hbm.at[c, plane, pl.ds(i * part, part)],
+                ref.at[plane, c, pl.ds(i * part, part)],
+                sems.at[((plane * 3 + c) * 2 + i) * 2 + k],
+            )
             for c in range(3)
-            for copy in (
-                pltpu.make_async_copy(v_hbm.at[c, plane], v_ref.at[plane, c], sems.at[plane * 6 + c]),
-                pltpu.make_async_copy(w_hbm.at[c, plane], w_ref.at[plane, c], sems.at[plane * 6 + 3 + c]),
-            )
+            for i in range(2)
+            for k, (hbm, ref) in enumerate(((v_hbm, v_ref), (w_hbm, w_ref)))
         ]
         for plane in range(len(outs))
     ]
@@ -329,7 +332,7 @@
         cross_kernel,
         [(3 * rows_y, 2 * cells)] * planes,
         6 * planes * 3 * rows_y * cells,
-        [VMEM((planes, 3, rows_y, cells), jnp.float32)] * 2 + [pltpu.SemaphoreType.DMA((6 * planes,))],
+        [VMEM((planes, 3, rows_y, cells), jnp.float32)] * 2 + [pltpu.SemaphoreType.DMA((12 * planes,))],
         pltpu.HBM,
         limit=50 << 20,
         kind=jnp.bfloat16,
@@ -368,7 +371,7 @@
         [
             VMEM((kinds * dests, lanes), jnp.float32),
             VMEM((3 * keep * 4, lanes), jnp.float32),
-            pltpu.SemaphoreType.DMA((6,)),
+            pltpu.SemaphoreType.DMA((12,)),
         ],
         [VMEM] * NXY + [pltpu.HBM, VMEM],
         limit=50 << 20,

time: 126 us -> 126 us (level)
  no operation moved by 1% of the time
where the time goes in v7:
time: 126 us
  starting transfers between devices  63.1 us (50%)
  waiting for transfers between devices  45.9 us (36%)
  Pallas kernels  15.4 us (12%)
    ppermute x22, starting transfers between devices, from_shift(): return lax.ppermute(value, GROUP, pairs)  47.4 us
    ppermute x22, waiting for transfers between devices, from_shift(): return lax.ppermute(value, GROUP, pairs)  43.7 us
    pallas_call x8, Pallas kernels, run(): pl.pallas_call(kernel, out_shape=shapes[0] if single else shapes, in_spec...  15.4 us
    all_to_all x1, starting transfers between devices, per_device(): lax.all_to_all(packed.reshape(dests, per, lanes), GROUP, 0, 0, axis_index...  15 us
  transfers between devices with their start and end apart: 25, of which 8 were waited for; matrix products, arithmetic and copies ran while one was open for 0% of the time, Pallas kernels for 4%

profile of v7, /device:TPU:32, one launch (start us, length us, event | category | flops | bytes accessed | tf_op | source)
XLA Modules:
  0.0 125.7 jit_solution(9676541846551596305)
XLA Ops:
  0.0 3.2 %shard_map.73 = (bf16[576,768]{1,0:T(8,128)(2,1)S(1)}, bf16[576,768]{1,0:T(8,128)(2,1)S(1)}, bf16[576,768]{1,0:T(8,128)(2,1)S(1)}) custom-call(f32[3,3,192,384]{3,2,1,0:T(8,128)} %v_hbm.1, f32[3,3,192,384]{3,2,1,0:T(8,128)} %w_hbm.1), custom_call_target="tpu_custom_call" | custom-call | flops 3981312 | bytes 10616832 | tf_op jit(solution)/shard_map/pallas_call | solution.py:297
  6.5 2.2 %collective-permute-done.1.got_ref = f32[576,256]{1,0:T(8,128)S(1)} collective-permute-done((f32[576,256]{1,0:T(8,128)S(1)}, f32[576,256]{1,0:T(8,128)S(1)}, u32[]{:S(2)}, u32[]{:S(2)}) %collective-permute-start.1) | collective-permute-done | bytes 589856 | tf_op jit(solution)/shard_map/ppermute | solution.py:346
  9.6 2.7 %shard_map.77 = f32[3072,128]{1,0:T(8,128)} custom-call(f32[1152,256]{1,0:T(8,128)S(1)} %get-tuple-element.38.keep_ref, f32[1152,256]{1,0:T(8,128)S(1)} %collective-permute-done.got_ref, bf16[2,2,256,192]{3,2,1,0:T(8,128)(2,1)S(1)} %copy-done, f32[192,128]{1,0:T(8,128)S(1)} %get-tuple-element.43._.refs_0_), custom_call_target="tpu_custom_call" | custom-call | flops 905969664 | bytes 4423680 | tf_op jit(solution)/shard_map/pallas_call | solution.py:297
  12.2 15.0 %all-to-all-start = ((f32[128,24,128]{2,1,0:T(8,128)}), f32[128,24,128]{2,1,0:T(8,128)S(1)}, u32[]{:S(2)}, u32[]{:S(2)}) async-start(f32[128,24,128]{2,1,0:T(8,128)} %bitcast), calls=%async_computation | async-start | bytes 3145728 | tf_op jit(solution)/shard_map/all_to_all | solution.py:362
  28.2 3.8 %collective-permute-start.3 = (f32[192,128]{1,0:T(8,128)S(1)}, f32[192,128]{1,0:T(8,128)S(1)}, u32[]{:S(2)}, u32[]{:S(2)}) collective-permute-start(f32[192,128]{1,0:T(8,128)S(1)} %get-tuple-element.45), channel_id=1, source_target_pairs={{16,0},{18,2},{20,4},{22,6},{24,8},{26,10},{28,12},{30,14},{32,16}... | collective-permute-start | bytes 294920 | tf_op jit(solution)/shard_map/ppermute | solution.py:321
  32.0 2.0 %collective-permute-start.4 = (f32[192,128]{1,0:T(8,128)S(1)}, f32[192,128]{1,0:T(8,128)S(1)}, u32[]{:S(2)}, u32[]{:S(2)}) collective-permute-start(f32[192,128]{1,0:T(8,128)S(1)} %get-tuple-element.46), channel_id=1, source_target_pairs={{24,0},{26,2},{28,4},{30,6},{32,8},{34,10},{36,12},{38,14},{40,16}... | collective-permute-start | bytes 294920 | tf_op jit(solution)/shard_map/ppermute | solution.py:321
  34.0 3.1 %collective-permute-start.5 = (f32[192,128]{1,0:T(8,128)S(1)}, f32[192,128]{1,0:T(8,128)S(1)}, u32[]{:S(2)}, u32[]{:S(2)}) collective-permute-start(f32[192,128]{1,0:T(8,128)S(1)} %get-tuple-element.47), channel_id=1, source_target_pairs={{32,0},{34,2},{36,4},{38,6},{40,8},{42,10},{44,12},{46,14},{48,16}... | collective-permute-start | bytes 294920 | tf_op jit(solution)/shard_map/ppermute | solution.py:321
  39.0 28.5 %collective-permute-done.2.refs_1_ = f32[192,128]{1,0:T(8,128)S(1)} collective-permute-done((f32[192,128]{1,0:T(8,128)S(1)}, f32[192,128]{1,0:T(8,128)S(1)}, u32[]{:S(2)}, u32[]{:S(2)}) %collective-permute-start.2) | collective-permute-done | bytes 98336 | tf_op jit(solution)/shard_map/ppermute | solution.py:321
  67.5 1.8 %collective-permute-start.7 = (f32[192,128]{1,0:T(8,128)S(1)}, f32[192,128]{1,0:T(8,128)S(1)}, u32[]{:S(2)}, u32[]{:S(2)}) collective-permute-start(f32[192,128]{1,0:T(8,128)S(1)} %get-tuple-element.49), channel_id=1, source_target_pairs={{48,0},{50,2},{52,4},{54,6},{56,8},{58,10},{60,12},{62,14},{0,16},... | collective-permute-start | bytes 294920 | tf_op jit(solution)/shard_map/ppermute | solution.py:321
  69.7 5.1 %collective-permute-start.8 = (f32[192,128]{1,0:T(8,128)S(1)}, f32[192,128]{1,0:T(8,128)S(1)}, u32[]{:S(2)}, u32[]{:S(2)}) collective-permute-start(f32[192,128]{1,0:T(8,128)S(1)} %get-tuple-element.50), channel_id=1, source_target_pairs={{56,0},{58,2},{60,4},{62,6},{0,8},{2,10},{4,12},{6,14},{8,16},{10,... | collective-permute-start | bytes 294920 | tf_op jit(solution)/shard_map/ppermute | solution.py:321
  74.8 2.9 %collective-permute-done.4.refs_3_ = f32[192,128]{1,0:T(8,128)S(1)} collective-permute-done((f32[192,128]{1,0:T(8,128)S(1)}, f32[192,128]{1,0:T(8,128)S(1)}, u32[]{:S(2)}, u32[]{:S(2)}) %collective-permute-start.4) | collective-permute-done | bytes 98336 | tf_op jit(solution)/shard_map/ppermute | solution.py:321
  77.7 4.5 %collective-permute-done.5.refs_4_ = f32[192,128]{1,0:T(8,128)S(1)} collective-permute-done((f32[192,128]{1,0:T(8,128)S(1)}, f32[192,128]{1,0:T(8,128)S(1)}, u32[]{:S(2)}, u32[]{:S(2)}) %collective-permute-start.5) | collective-permute-done | bytes 98336 | tf_op jit(solution)/shard_map/ppermute | solution.py:321
  82.7 3.1 %collective-permute-start.9 = (f32[96,128]{1,0:T(8,128)S(1)}, f32[96,128]{1,0:T(8,128)S(1)}, u32[]{:S(2)}, u32[]{:S(2)}) collective-permute-start(f32[96,128]{1,0:T(8,128)S(1)} %get-tuple-element.52), channel_id=1, source_target_pairs={{2,0},{4,2},{6,4},{0,6},{10,8},{12,10},{14,12},{8,14},{18,16},{20,... | collective-permute-start | bytes 147464 | tf_op jit(solution)/shard_map/ppermute | solution.py:321
  87.5 2.8 %collective-permute-start.12 = (f32[96,128]{1,0:T(8,128)S(1)}, f32[96,128]{1,0:T(8,128)S(1)}, u32[]{:S(2)}, u32[]{:S(2)}) collective-permute-start(f32[96,128]{1,0:T(8,128)S(1)} %get-tuple-element.55), channel_id=1, source_target_pairs={{64,0},{66,2},{68,4},{70,6},{72,8},{74,10},{76,12},{78,14},{80,16}... | collective-permute-start | bytes 147464 | tf_op jit(solution)/shard_map/ppermute | solution.py:321
  90.2 2.6 %collective-permute-start.13 = (f32[96,128]{1,0:T(8,128)S(1)}, f32[96,128]{1,0:T(8,128)S(1)}, u32[]{:S(2)}, u32[]{:S(2)}) collective-permute-start(f32[96,128]{1,0:T(8,128)S(1)} %get-tuple-element.56), channel_id=1, source_target_pairs={{66,0},{68,2},{70,4},{64,6},{74,8},{76,10},{78,12},{72,14},{82,16}... | collective-permute-start | bytes 147464 | tf_op jit(solution)/shard_map/ppermute | solution.py:321
  94.4 2.8 %collective-permute-start.16 = (f32[96,128]{1,0:T(8,128)S(1)}, f32[96,128]{1,0:T(8,128)S(1)}, u32[]{:S(2)}, u32[]{:S(2)}) collective-permute-start(f32[96,128]{1,0:T(8,128)S(1)} %get-tuple-element.59), channel_id=1, source_target_pairs={{128,0},{130,2},{132,4},{134,6},{136,8},{138,10},{140,12},{142,14}... | collective-permute-start | bytes 147464 | tf_op jit(solution)/shard_map/ppermute | solution.py:321
  97.1 3.4 %collective-permute-start.17 = (f32[96,128]{1,0:T(8,128)S(1)}, f32[96,128]{1,0:T(8,128)S(1)}, u32[]{:S(2)}, u32[]{:S(2)}) collective-permute-start(f32[96,128]{1,0:T(8,128)S(1)} %get-tuple-element.60), channel_id=1, source_target_pairs={{130,0},{132,2},{134,4},{128,6},{138,8},{140,10},{142,12},{136,14}... | collective-permute-start | bytes 147464 | tf_op jit(solution)/shard_map/ppermute | solution.py:321
  100.5 3.3 %collective-permute-start.18 = (f32[96,128]{1,0:T(8,128)S(1)}, f32[96,128]{1,0:T(8,128)S(1)}, u32[]{:S(2)}, u32[]{:S(2)}) collective-permute-start(f32[96,128]{1,0:T(8,128)S(1)} %get-tuple-element.61), channel_id=1, source_target_pairs={{132,0},{134,2},{128,4},{130,6},{140,8},{142,10},{136,12},{138,14}... | collective-permute-start | bytes 147464 | tf_op jit(solution)/shard_map/ppermute | solution.py:321
  104.9 4.5 %collective-permute-start.21 = (f32[96,128]{1,0:T(8,128)S(1)}, f32[96,128]{1,0:T(8,128)S(1)}, u32[]{:S(2)}, u32[]{:S(2)}) collective-permute-start(f32[96,128]{1,0:T(8,128)S(1)} %get-tuple-element.64), channel_id=1, source_target_pairs={{194,0},{196,2},{198,4},{192,6},{202,8},{204,10},{206,12},{200,14}... | collective-permute-start | bytes 147464 | tf_op jit(solution)/shard_map/ppermute | solution.py:321
  109.4 2.1 %collective-permute-start.22 = (f32[96,128]{1,0:T(8,128)S(1)}, f32[96,128]{1,0:T(8,128)S(1)}, u32[]{:S(2)}, u32[]{:S(2)}) collective-permute-start(f32[96,128]{1,0:T(8,128)S(1)} %get-tuple-element.65), channel_id=1, source_target_pairs={{196,0},{198,2},{192,4},{194,6},{204,8},{206,10},{200,12},{202,14}... | collective-permute-start | bytes 147464 | tf_op jit(solution)/shard_map/ppermute | solution.py:321
  112.2 4.9 %collective-permute-done.22.refs_14_ = f32[96,128]{1,0:T(8,128)S(1)} collective-permute-done((f32[96,128]{1,0:T(8,128)S(1)}, f32[96,128]{1,0:T(8,128)S(1)}, u32[]{:S(2)}, u32[]{:S(2)}) %collective-permute-start.22) | collective-permute-done | bytes 49184 | tf_op jit(solution)/shard_map/ppermute | solution.py:321
  117.1 1.8 %collective-permute-done.23.refs_15_ = f32[96,128]{1,0:T(8,128)S(1)} collective-permute-done((f32[96,128]{1,0:T(8,128)S(1)}, f32[96,128]{1,0:T(8,128)S(1)}, u32[]{:S(2)}, u32[]{:S(2)}) %collective-permute-start.23) | collective-permute-done | bytes 49184 | tf_op jit(solution)/shard_map/ppermute | solution.py:321
  119.9 3.1 %shard_map.79.early_ref = f32[3072,128]{1,0:T(8,128)S(1)} custom-call(f32[96,128]{1,0:T(8,128)S(1)} %get-tuple-element.51.refs_0_, f32[96,128]{1,0:T(8,128)S(1)} %collective-permute-done.9.refs_1_, f32[96,128]{1,0:T(8,128)S(1)} %collective-permute-done.10.refs_2_, f32[96,128]{1,0:T(8,128)S(1)} %collective-permute-done.11.refs_3_, ...), custom_call_target="tpu_custom_call" | custom-call | flops 603979776 | bytes 4194304 | tf_op jit(solution)/shard_map/pallas_call | solution.py:297
  123.0 2.6 %shard_map.80 = f32[3072,128]{1,0:T(8,128)} custom-call(f32[3072,128]{1,0:T(8,128)S(1)} %bitcast.4, f32[3072,128]{1,0:T(8,128)S(1)} %shard_map.79.early_ref, bf16[2,2,256,128]{3,2,1,0:T(8,128)(2,1)S(1)} %copy-done.1), custom_call_target="tpu_custom_call" | custom-call | flops 603979776 | bytes 4980736 | tf_op jit(solution)/shard_map/pallas_call | solution.py:297
  (42 shorter events, 13.8 us)
Async XLA Ops:
  4.9 4.7 %collective-permute-start = (f32[1152,256]{1,0:T(8,128)S(1)}, f32[1152,256]{1,0:T(8,128)S(1)}, u32[]{:S(2)}, u32[]{:S(2)}) collective-permute-start(f32[1152,256]{1,0:T(8,128)S(1)} %get-tuple-element.39), channel_id=1, source_target_pairs={{0,1},{1,0},{2,3},{3,2},{4,5},{5,4},{6,7},{7,6},{8,9},{9,8},{10,11... | collective-permute-start | bytes 3538952 | tf_op jit(solution)/shard_map/ppermute | solution.py:346
  12.2 110.7 %all-to-all-start = ((f32[128,24,128]{2,1,0:T(8,128)}), f32[128,24,128]{2,1,0:T(8,128)S(1)}, u32[]{:S(2)}, u32[]{:S(2)}) async-start(f32[128,24,128]{2,1,0:T(8,128)} %bitcast), calls=%async_computation | async-start | bytes 3145728 | tf_op jit(solution)/shard_map/all_to_all | solution.py:362
  27.3 40.2 %collective-permute-start.2 = (f32[192,128]{1,0:T(8,128)S(1)}, f32[192,128]{1,0:T(8,128)S(1)}, u32[]{:S(2)}, u32[]{:S(2)}) collective-permute-start(f32[192,128]{1,0:T(8,128)S(1)} %get-tuple-element.44), channel_id=1, source_target_pairs={{8,0},{10,2},{12,4},{14,6},{16,8},{18,10},{20,12},{22,14},{24,16},... | collective-permute-start | bytes 294920 | tf_op jit(solution)/shard_map/ppermute | solution.py:321
  28.2 41.5 %collective-permute-start.3 = (f32[192,128]{1,0:T(8,128)S(1)}, f32[192,128]{1,0:T(8,128)S(1)}, u32[]{:S(2)}, u32[]{:S(2)}) collective-permute-start(f32[192,128]{1,0:T(8,128)S(1)} %get-tuple-element.45), channel_id=1, source_target_pairs={{16,0},{18,2},{20,4},{22,6},{24,8},{26,10},{28,12},{30,14},{32,16}... | collective-permute-start | bytes 294920 | tf_op jit(solution)/shard_map/ppermute | solution.py:321
  32.0 45.7 %collective-permute-start.4 = (f32[192,128]{1,0:T(8,128)S(1)}, f32[192,128]{1,0:T(8,128)S(1)}, u32[]{:S(2)}, u32[]{:S(2)}) collective-permute-start(f32[192,128]{1,0:T(8,128)S(1)} %get-tuple-element.46), channel_id=1, source_target_pairs={{24,0},{26,2},{28,4},{30,6},{32,8},{34,10},{36,12},{38,14},{40,16}... | collective-permute-start | bytes 294920 | tf_op jit(solution)/shard_map/ppermute | solution.py:321
  34.0 48.1 %collective-permute-start.5 = (f32[192,128]{1,0:T(8,128)S(1)}, f32[192,128]{1,0:T(8,128)S(1)}, u32[]{:S(2)}, u32[]{:S(2)}) collective-permute-start(f32[192,128]{1,0:T(8,128)S(1)} %get-tuple-element.47), channel_id=1, source_target_pairs={{32,0},{34,2},{36,4},{38,6},{40,8},{42,10},{44,12},{46,14},{48,16}... | collective-permute-start | bytes 294920 | tf_op jit(solution)/shard_map/ppermute | solution.py:321
  37.1 45.0 %collective-permute-start.6 = (f32[192,128]{1,0:T(8,128)S(1)}, f32[192,128]{1,0:T(8,128)S(1)}, u32[]{:S(2)}, u32[]{:S(2)}) collective-permute-start(f32[192,128]{1,0:T(8,128)S(1)} %get-tuple-element.48), channel_id=1, source_target_pairs={{40,0},{42,2},{44,4},{46,6},{48,8},{50,10},{52,12},{54,14},{56,16}... | collective-permute-start | bytes 294920 | tf_op jit(solution)/shard_map/ppermute | solution.py:321
  67.5 14.7 %collective-permute-start.7 = (f32[192,128]{1,0:T(8,128)S(1)}, f32[192,128]{1,0:T(8,128)S(1)}, u32[]{:S(2)}, u32[]{:S(2)}) collective-permute-start(f32[192,128]{1,0:T(8,128)S(1)} %get-tuple-element.49), channel_id=1, source_target_pairs={{48,0},{50,2},{52,4},{54,6},{56,8},{58,10},{60,12},{62,14},{0,16},... | collective-permute-start | bytes 294920 | tf_op jit(solution)/shard_map/ppermute | solution.py:321
  69.7 12.5 %collective-permute-start.8 = (f32[192,128]{1,0:T(8,128)S(1)}, f32[192,128]{1,0:T(8,128)S(1)}, u32[]{:S(2)}, u32[]{:S(2)}) collective-permute-start(f32[192,128]{1,0:T(8,128)S(1)} %get-tuple-element.50), channel_id=1, source_target_pairs={{56,0},{58,2},{60,4},{62,6},{0,8},{2,10},{4,12},{6,14},{8,16},{10,... | collective-permute-start | bytes 294920 | tf_op jit(solution)/shard_map/ppermute | solution.py:321
  82.7 10.2 %collective-permute-start.9 = (f32[96,128]{1,0:T(8,128)S(1)}, f32[96,128]{1,0:T(8,128)S(1)}, u32[]{:S(2)}, u32[]{:S(2)}) collective-permute-start(f32[96,128]{1,0:T(8,128)S(1)} %get-tuple-element.52), channel_id=1, source_target_pairs={{2,0},{4,2},{6,4},{0,6},{10,8},{12,10},{14,12},{8,14},{18,16},{20,... | collective-permute-start | bytes 147464 | tf_op jit(solution)/shard_map/ppermute | solution.py:321
  85.7 8.6 %collective-permute-start.10 = (f32[96,128]{1,0:T(8,128)S(1)}, f32[96,128]{1,0:T(8,128)S(1)}, u32[]{:S(2)}, u32[]{:S(2)}) collective-permute-start(f32[96,128]{1,0:T(8,128)S(1)} %get-tuple-element.53), channel_id=1, source_target_pairs={{4,0},{6,2},{0,4},{2,6},{12,8},{14,10},{8,12},{10,14},{20,16},{22,... | collective-permute-start | bytes 147464 | tf_op jit(solution)/shard_map/ppermute | solution.py:321
  86.6 7.8 %collective-permute-start.11 = (f32[96,128]{1,0:T(8,128)S(1)}, f32[96,128]{1,0:T(8,128)S(1)}, u32[]{:S(2)}, u32[]{:S(2)}) collective-permute-start(f32[96,128]{1,0:T(8,128)S(1)} %get-tuple-element.54), channel_id=1, source_target_pairs={{6,0},{0,2},{2,4},{4,6},{14,8},{8,10},{10,12},{12,14},{22,16},{16,... | collective-permute-start | bytes 147464 | tf_op jit(solution)/shard_map/ppermute | solution.py:321
  87.5 9.7 %collective-permute-start.12 = (f32[96,128]{1,0:T(8,128)S(1)}, f32[96,128]{1,0:T(8,128)S(1)}, u32[]{:S(2)}, u32[]{:S(2)}) collective-permute-start(f32[96,128]{1,0:T(8,128)S(1)} %get-tuple-element.55), channel_id=1, source_target_pairs={{64,0},{66,2},{68,4},{70,6},{72,8},{74,10},{76,12},{78,14},{80,16}... | collective-permute-start | bytes 147464 | tf_op jit(solution)/shard_map/ppermute | solution.py:321
  90.2 10.3 %collective-permute-start.13 = (f32[96,128]{1,0:T(8,128)S(1)}, f32[96,128]{1,0:T(8,128)S(1)}, u32[]{:S(2)}, u32[]{:S(2)}) collective-permute-start(f32[96,128]{1,0:T(8,128)S(1)} %get-tuple-element.56), channel_id=1, source_target_pairs={{66,0},{68,2},{70,4},{64,6},{74,8},{76,10},{78,12},{72,14},{82,16}... | collective-permute-start | bytes 147464 | tf_op jit(solution)/shard_map/ppermute | solution.py:321
  92.8 10.9 %collective-permute-start.14 = (f32[96,128]{1,0:T(8,128)S(1)}, f32[96,128]{1,0:T(8,128)S(1)}, u32[]{:S(2)}, u32[]{:S(2)}) collective-permute-start(f32[96,128]{1,0:T(8,128)S(1)} %get-tuple-element.57), channel_id=1, source_target_pairs={{68,0},{70,2},{64,4},{66,6},{76,8},{78,10},{72,12},{74,14},{84,16}... | collective-permute-start | bytes 147464 | tf_op jit(solution)/shard_map/ppermute | solution.py:321
  94.3 9.6 %collective-permute-start.15 = (f32[96,128]{1,0:T(8,128)S(1)}, f32[96,128]{1,0:T(8,128)S(1)}, u32[]{:S(2)}, u32[]{:S(2)}) collective-permute-start(f32[96,128]{1,0:T(8,128)S(1)} %get-tuple-element.58), channel_id=1, source_target_pairs={{70,0},{64,2},{66,4},{68,6},{78,8},{72,10},{74,12},{76,14},{86,16}... | collective-permute-start | bytes 147464 | tf_op jit(solution)/shard_map/ppermute | solution.py:321
  94.4 10.5 %collective-permute-start.16 = (f32[96,128]{1,0:T(8,128)S(1)}, f32[96,128]{1,0:T(8,128)S(1)}, u32[]{:S(2)}, u32[]{:S(2)}) collective-permute-start(f32[96,128]{1,0:T(8,128)S(1)} %get-tuple-element.59), channel_id=1, source_target_pairs={{128,0},{130,2},{132,4},{134,6},{136,8},{138,10},{140,12},{142,14}... | collective-permute-start | bytes 147464 | tf_op jit(solution)/shard_map/ppermute | solution.py:321
  97.1 12.3 %collective-permute-start.17 = (f32[96,128]{1,0:T(8,128)S(1)}, f32[96,128]{1,0:T(8,128)S(1)}, u32[]{:S(2)}, u32[]{:S(2)}) collective-permute-start(f32[96,128]{1,0:T(8,128)S(1)} %get-tuple-element.60), channel_id=1, source_target_pairs={{130,0},{132,2},{134,4},{128,6},{138,8},{140,10},{142,12},{136,14}... | collective-permute-start | bytes 147464 | tf_op jit(solution)/shard_map/ppermute | solution.py:321
  100.5 11.0 %collective-permute-start.18 = (f32[96,128]{1,0:T(8,128)S(1)}, f32[96,128]{1,0:T(8,128)S(1)}, u32[]{:S(2)}, u32[]{:S(2)}) collective-permute-start(f32[96,128]{1,0:T(8,128)S(1)} %get-tuple-element.61), channel_id=1, source_target_pairs={{132,0},{134,2},{128,4},{130,6},{140,8},{142,10},{136,12},{138,14}... | collective-permute-start | bytes 147464 | tf_op jit(solution)/shard_map/ppermute | solution.py:321
  103.8 8.4 %collective-permute-start.19 = (f32[96,128]{1,0:T(8,128)S(1)}, f32[96,128]{1,0:T(8,128)S(1)}, u32[]{:S(2)}, u32[]{:S(2)}) collective-permute-start(f32[96,128]{1,0:T(8,128)S(1)} %get-tuple-element.62), channel_id=1, source_target_pairs={{134,0},{128,2},{130,4},{132,6},{142,8},{136,10},{138,12},{140,14}... | collective-permute-start | bytes 147464 | tf_op jit(solution)/shard_map/ppermute | solution.py:321
  103.9 8.3 %collective-permute-start.20 = (f32[96,128]{1,0:T(8,128)S(1)}, f32[96,128]{1,0:T(8,128)S(1)}, u32[]{:S(2)}, u32[]{:S(2)}) collective-permute-start(f32[96,128]{1,0:T(8,128)S(1)} %get-tuple-element.63), channel_id=1, source_target_pairs={{192,0},{194,2},{196,4},{198,6},{200,8},{202,10},{204,12},{206,14}... | collective-permute-start | bytes 147464 | tf_op jit(solution)/shard_map/ppermute | solution.py:321
  104.9 7.3 %collective-permute-start.21 = (f32[96,128]{1,0:T(8,128)S(1)}, f32[96,128]{1,0:T(8,128)S(1)}, u32[]{:S(2)}, u32[]{:S(2)}) collective-permute-start(f32[96,128]{1,0:T(8,128)S(1)} %get-tuple-element.64), channel_id=1, source_target_pairs={{194,0},{196,2},{198,4},{192,6},{202,8},{204,10},{206,12},{200,14}... | collective-permute-start | bytes 147464 | tf_op jit(solution)/shard_map/ppermute | solution.py:321
  109.4 7.7 %collective-permute-start.22 = (f32[96,128]{1,0:T(8,128)S(1)}, f32[96,128]{1,0:T(8,128)S(1)}, u32[]{:S(2)}, u32[]{:S(2)}) collective-permute-start(f32[96,128]{1,0:T(8,128)S(1)} %get-tuple-element.65), channel_id=1, source_target_pairs={{196,0},{198,2},{192,4},{194,6},{204,8},{206,10},{200,12},{202,14}... | collective-permute-start | bytes 147464 | tf_op jit(solution)/shard_map/ppermute | solution.py:321
  111.5 7.4 %collective-permute-start.23 = (f32[96,128]{1,0:T(8,128)S(1)}, f32[96,128]{1,0:T(8,128)S(1)}, u32[]{:S(2)}, u32[]{:S(2)}) collective-permute-start(f32[96,128]{1,0:T(8,128)S(1)} %get-tuple-element.66), channel_id=1, source_target_pairs={{198,0},{192,2},{194,4},{196,6},{206,8},{200,10},{202,12},{204,14}... | collective-permute-start | bytes 147464 | tf_op jit(solution)/shard_map/ppermute | solution.py:321
  (5 other events, 13.8 us)
